TPU v7x, 32 devices: a whole 2x2x4 slice. The times are simulated.
32 devices in a mesh: dp: 16 (over z, y, core), tensor: 2 (over x).
Axes of the slice: x: 2, y: 2, z: 4, core: 2. Of those that a mesh axis runs over, the one named last changes fastest.
Arguments:
- activations: bfloat16 [4096, 27648], P('dp', 'tensor'), may hold values from -6 to 6
- output_gradient: bfloat16 [4096, 5120], P('dp', 'tensor'), may hold values from -6 to 6
- adapter_a: bfloat16 [2, 13824, 128], P('tensor', 'dp'), may hold values from -0.0390625 to 0.0390625
- adapter_b: bfloat16 [128, 5120], P(None, 'tensor'), may hold values from -0.078125 to 0.078125
- log_ratio: float32 [4096], P('dp'), may hold values from -1.5 to 1.5
- lengths: int32 [1, 16], replicated, may hold values from 1 to 256, as said below
- rewards: int32 [1, 16], replicated, may hold values from 0 to 10
Outputs:
- grad_a: float32 [2, 13824, 128], P('tensor', 'dp')
- adapter_b_gradient: float32 [128, 5120], P(None, 'tensor')
- loss: float32 [], replicated
Inputs may be any that keep to these rules, and one draw needn't show every extreme that they name: `lengths`: in every group some rollout has length 256.
All inputs are finite; a program needn't handle non-finite values.
Results may differ from a plain program's by a relative error of at most 0.0067.
Values may be sent and summed in bfloat16 or wider, within the bound.
No kernel may reach another device: no remote copies, remote signals or barrier semaphores. Data moves between devices by JAX's collectives and lax.ppermute only.
A program may use at most 64 MiB of HBM per device.

v0:
```python
import functools

import jax
import jax.numpy as jnp
from jax import lax
from jax.experimental import pallas as pl
from jax.experimental.pallas import tpu as pltpu
from jax.sharding import PartitionSpec as P


clip_eps = 0.2
adapter_scale_factor = 2.0
cores = 2
lanes = 128


def slot_terms(length_row, reward_row, log_ratio, offset):
    reward = reward_row.astype(jnp.float32)
    center = jnp.mean(reward)
    spread = jnp.mean((reward - center) * (reward - center))
    advantage = (reward - center) / jnp.sqrt(spread + 1.0)
    ends = jnp.cumsum(length_row)
    starts = ends - length_row
    slots = jnp.arange(log_ratio.shape[0], dtype=jnp.int32) + offset
    member = ((slots[None, :] >= starts[:, None]) & (slots[None, :] < ends[:, None])).astype(
        jnp.float32
    )
    live = jnp.sum(member, axis=0)
    token_adv = jnp.sum(member * advantage[:, None], axis=0)
    ratio = jnp.exp(log_ratio)
    unclipped = ratio * token_adv
    clipped = jnp.clip(ratio, 1.0 - clip_eps, 1.0 + clip_eps) * token_adv
    token_loss = -jnp.minimum(unclipped, clipped)
    slope = jnp.where(unclipped <= clipped, -unclipped, jnp.zeros_like(unclipped))
    return (live * slope, jnp.sum(live * token_loss))


def own_terms(log_ratio, lengths, rewards):
    tokens = log_ratio.shape[0]
    groups = lengths.shape[0]
    per_group = lax.axis_size("dp") // groups
    position = lax.axis_index("dp")
    group_id = position // per_group
    offset = position % per_group * tokens
    length_row = lax.dynamic_index_in_dim(lengths, group_id, 0, keepdims=False)
    reward_row = lax.dynamic_index_in_dim(rewards, group_id, 0, keepdims=False)
    coefficient, loss = slot_terms(length_row, reward_row, log_ratio, offset)
    live = jnp.sum(jnp.minimum(jnp.sum(lengths, axis=1), per_group * tokens))
    return coefficient, loss, groups / live.astype(jnp.float32)


def general(activations, output_gradient, adapter_a, adapter_b, log_ratio, lengths, rewards):
    coefficient, loss, factor = own_terms(log_ratio, lengths, rewards)
    partial_low = jnp.dot(
        activations,
        lax.all_gather(adapter_a, "dp", axis=1, tiled=True)[0],
        preferred_element_type=jnp.float32,
    )
    partial_back = lax.dot_general(
        output_gradient, adapter_b, (((1,), (1,)), ((), ())), preferred_element_type=jnp.float32
    )
    low_rank, back = lax.psum((partial_low, partial_back), "tensor")
    error_rows = (adapter_scale_factor * coefficient[:, None] * back).astype(jnp.bfloat16)
    grad_b = adapter_scale_factor * jnp.einsum(
        "tr,td->rd",
        coefficient[:, None] * low_rank,
        output_gradient.astype(jnp.float32),
        precision=lax.Precision.HIGHEST,
    )
    grad_a = lax.psum_scatter(
        lax.dot_general(
            activations, error_rows, (((0,), (0,)), ((), ())), preferred_element_type=jnp.float32
        ),
        "dp",
        scatter_dimension=0,
        tiled=True,
    )
    grad_b, loss = lax.psum((grad_b, loss), "dp")
    return ((factor * grad_a)[None], factor * grad_b, factor * loss)


vmem = pl.BlockSpec(memory_space=pltpu.VMEM)


def limit(size):
    return size + 4 * 2**20


def place():
    position = lax.axis_index("dp")
    return position // (2 * cores), position // cores % 2, position % cores


def segment(dy, dk, rows):
    _, y, k = place()
    return pl.ds(pl.multiple_of((lax.bitwise_xor(y, dy) * 2 + lax.bitwise_xor(k, dk)) * rows, 16), rows)


def terms_kernel(lengths, rewards, log_ratio, _, spread_out, stats, *, per_group):
    groups, count = lengths.shape
    lines = log_ratio.shape[0]
    shape = (lines, lanes)
    tokens = lines * lanes
    position = lax.axis_index("dp")
    group = position // per_group
    value = [jnp.full(shape, rewards[group, i], jnp.int32).astype(jnp.float32) for i in range(count)]
    center = sum(value) / count
    spread = sum((v - center) * (v - center) for v in value) / count
    root = jnp.sqrt(spread + 1.0)
    slots = (
        lax.broadcasted_iota(jnp.int32, shape, 0) * lanes
        + lax.broadcasted_iota(jnp.int32, shape, 1)
        + position % per_group * tokens
    )
    token_adv = jnp.zeros(shape, jnp.float32)
    live = jnp.zeros(shape, jnp.float32)
    start = 0
    for i in range(count):
        end = start + lengths[group, i]
        member = ((slots >= start) & (slots < end)).astype(jnp.float32)
        token_adv = token_adv + member * ((value[i] - center) / root)
        live = live + member
        start = end
    ratio = jnp.exp(log_ratio[...])
    unclipped = ratio * token_adv
    clipped = jnp.clip(ratio, 1.0 - clip_eps, 1.0 + clip_eps) * token_adv
    loss = jnp.sum(live * -jnp.minimum(unclipped, clipped))
    coefficient = live * jnp.where(unclipped <= clipped, -unclipped, jnp.zeros(shape, jnp.float32))
    for line in range(lines):
        row = jnp.broadcast_to(coefficient[line : line + 1, :], (lanes, lanes))
        spread_out[line * lanes : (line + 1) * lanes, :] = row.T
    total = 0
    for g in range(groups):
        size = 0
        for i in range(count):
            size = size + lengths[g, i]
        total = total + jnp.minimum(size, per_group * tokens)
    stats[0] = jnp.broadcast_to(loss, stats.shape[1:])
    stats[1] = groups / jnp.full(stats.shape[1:], total, jnp.int32).astype(jnp.float32)


def terms(log_ratio, lengths, rewards, activations):
    tokens = log_ratio.shape[0]
    per_group = lax.axis_size("dp") // lengths.shape[0]
    return pl.pallas_call(
        functools.partial(terms_kernel, per_group=per_group),
        in_specs=[pl.BlockSpec(memory_space=pltpu.SMEM)] * 2
        + [vmem] * 2,
        out_specs=[vmem] * 2,
        out_shape=[
            jax.ShapeDtypeStruct((tokens, lanes), jnp.float32),
            jax.ShapeDtypeStruct((2, 8, lanes), jnp.float32),
        ],
        name="terms",
        compiler_params=pltpu.CompilerParams(vmem_limit_bytes=limit(2 * activations.size)),
    )(lengths, rewards, log_ratio.reshape(tokens // lanes, lanes), activations)


def back_kernel(grad, factor, out):
    out[...] = lax.dot_general(
        grad[...], factor[...], (((1,), (1,)), ((), ())), preferred_element_type=jnp.float32
    )


def back_part(grad, factor):
    tokens, width = grad.shape
    rank = factor.shape[0]
    return pl.pallas_call(
        back_kernel,
        in_specs=[vmem] * 2,
        out_specs=vmem,
        out_shape=jax.ShapeDtypeStruct((tokens, rank), jnp.float32),
        cost_estimate=pl.CostEstimate(
            flops=2 * tokens * width * rank,
            bytes_accessed=2 * (tokens + rank) * width,
            transcendentals=0,
        ),
        name="back",
        compiler_params=pltpu.CompilerParams(
            vmem_limit_bytes=limit(2 * (tokens + rank) * width)
        ),
    )(grad, factor)


def tile_of(width):
    blocks = width // lanes
    return next(blocks // n for n in range(3, blocks + 1) if blocks % n == 0) * lanes


def columns(r, t, width, tile):
    at = lax.bitwise_xor(place()[0], r) * width + t * tile
    return pl.ds(pl.multiple_of(at, lanes), tile)


def low_rank_kernel(rounds, chained, acts, *refs):
    count = len(rounds)
    slices = refs[: 4 * count]
    out, whole = refs[-2:]
    rows = slices[0].shape[0]
    width = 4 * rows
    tile = tile_of(width)
    total = refs[4 * count][...] if chained else None
    for index, r in enumerate(rounds):
        for dy in range(2):
            for dk in range(2):
                whole[index, segment(dy, dk, rows)] = slices[4 * index + 2 * dy + dk][...]
        for t in range(width // tile):
            part = jnp.dot(
                acts[:, columns(r, t, width, tile)],
                whole[index, t * tile : (t + 1) * tile, :],
                preferred_element_type=jnp.float32,
            )
            total = part if total is None else total + part
    out[...] = total


def low_rank_part(activations, rounds, slices, before=None):
    tokens = activations.shape[0]
    rows, rank = slices[0].shape
    width = 4 * rows
    count = len(rounds)
    extra = () if before is None else (before,)
    return pl.pallas_call(
        functools.partial(low_rank_kernel, rounds, before is not None),
        in_specs=[vmem] * (1 + len(slices) + len(extra)),
        out_specs=vmem,
        scratch_shapes=[pltpu.VMEM((count, width, rank), jnp.bfloat16)],
        out_shape=jax.ShapeDtypeStruct((tokens, rank), jnp.float32),
        cost_estimate=pl.CostEstimate(
            flops=2 * tokens * width * rank * count,
            bytes_accessed=2 * (tokens + rank) * width * count,
            transcendentals=0,
        ),
        name="low_rank",
        compiler_params=pltpu.CompilerParams(
            vmem_limit_bytes=limit(2 * activations.size + 4 * count * width * rank)
        ),
    )(activations, *slices, *extra)


def grad_a_kernel(rounds, acts, coefficient, back, other, keep, send, whole):
    rows = keep.shape[2]
    width = 4 * rows
    tile = tile_of(width)
    scaled = adapter_scale_factor * coefficient[...] * (back[...] + other[...])
    err = scaled.astype(jnp.bfloat16)
    for index, r in enumerate(rounds):
        for t in range(width // tile):
            part = lax.dot_general(
                acts[:, columns(r, t, width, tile)],
                err,
                (((0,), (0,)), ((), ())),
                preferred_element_type=jnp.float32,
            )
            whole[index, t * tile : (t + 1) * tile, :] = part.astype(jnp.bfloat16)
        for dk, out in enumerate((keep, send)):
            for dy in range(2):
                out[index, dy] = whole[index, segment(dy, dk, rows)]


def grad_a_part(activations, coefficient, back, other, rounds, rows):
    tokens, rank = back.shape
    width = 4 * rows
    count = len(rounds)
    shape = jax.ShapeDtypeStruct((count, 2, rows, rank), jnp.bfloat16)
    return pl.pallas_call(
        functools.partial(grad_a_kernel, rounds),
        in_specs=[vmem] * 4,
        out_specs=[vmem] * 2,
        scratch_shapes=[pltpu.VMEM((count, width, rank), jnp.bfloat16)],
        out_shape=[shape, shape],
        cost_estimate=pl.CostEstimate(
            flops=2 * tokens * width * rank * count,
            bytes_accessed=2 * (tokens + rank) * width * count,
            transcendentals=0,
        ),
        name="grad_a",
        compiler_params=pltpu.CompilerParams(
            vmem_limit_bytes=limit(2 * activations.size + 4 * count * width * rank)
        ),
    )(activations, coefficient, back, other)


def grad_b_kernel(low, other, coefficient, stats, grad, keep, send, whole):
    depth, rows = keep.shape[:2]
    width = grad.shape[1]
    tile = tile_of(width)
    scale = adapter_scale_factor * stats[1][:1] * coefficient[...]
    weighted = (scale * (low[...] + other[...])).astype(jnp.bfloat16)
    shape = (rows, lanes)
    parts = thirds(
        jnp.broadcast_to(stats[0][:1], shape), lax.broadcasted_iota(jnp.int32, shape, 1)
    )
    for t in range(width // tile):
        whole[:, t * tile : (t + 1) * tile] = lax.dot_general(
            weighted,
            grad[:, t * tile : (t + 1) * tile],
            (((0,), (0,)), ((), ())),
            preferred_element_type=jnp.float32,
        )
    z, _, k = place()
    for dk, out in enumerate((keep, send)):
        for r in range(depth):
            at = (lax.bitwise_xor(z, r) * 2 + lax.bitwise_xor(k, dk)) * rows
            out[r, :, :width] = whole[pl.ds(pl.multiple_of(at, rows), rows), :].astype(out.dtype)
            out[r, :, width:] = parts.astype(out.dtype)


def grad_b_part(low, other, coefficient, stats, grad, depth):
    tokens, rank = low.shape
    width = grad.shape[1]
    rows = rank // (2 * depth)
    shape = (depth, rows, width + lanes)
    return pl.pallas_call(
        grad_b_kernel,
        in_specs=[vmem] * 5,
        out_specs=[vmem] * 2,
        out_shape=[
            jax.ShapeDtypeStruct(shape, jnp.float32),
            jax.ShapeDtypeStruct(shape, jnp.bfloat16),
        ],
        scratch_shapes=[pltpu.VMEM((rank, width), jnp.float32)],
        cost_estimate=pl.CostEstimate(
            flops=2 * tokens * width * rank,
            bytes_accessed=2 * tokens * width + 6 * rank * width,
            transcendentals=0,
        ),
        name="grad_b",
        compiler_params=pltpu.CompilerParams(vmem_limit_bytes=limit(10 * rank * width)),
    )(low, other, coefficient, stats, grad)


def thirds(value, lane):
    high = value.astype(jnp.bfloat16).astype(jnp.float32)
    middle = (value - high).astype(jnp.bfloat16).astype(jnp.float32)
    low = value - high - middle
    zero = jnp.zeros_like(value)
    return jnp.where(
        lane == 0, high, jnp.where(lane == 1, middle, jnp.where(lane == 2, low, zero))
    )


def chip_sum_kernel(keep, got, *outs):
    width = keep.shape[2] - lanes
    lane = lax.broadcasted_iota(jnp.int32, (keep.shape[1], lanes), 1)
    for r, out in enumerate(outs):
        total = keep[r] + got[r].astype(jnp.float32)
        out[:, :width] = total[:, :width].astype(out.dtype)
        value = jnp.sum(total[:, width:], axis=1, keepdims=True)
        out[:, width:] = thirds(jnp.broadcast_to(value, lane.shape), lane).astype(out.dtype)


def chip_sum(keep, got):
    depth, rows, width = keep.shape
    return pl.pallas_call(
        chip_sum_kernel,
        out_shape=[jax.ShapeDtypeStruct((rows, width), jnp.bfloat16)] * depth,
        name="chip_sum",
        compiler_params=pltpu.CompilerParams(vmem_limit_bytes=limit(6 * 2**20)),
    )(keep, got)


def fill_kernel(own, other, out):
    depth, rows = own.shape[:2]
    z, _, k = place()
    for dk, source in enumerate((own, other)):
        for r in range(depth):
            at = (lax.bitwise_xor(z, r) * 2 + lax.bitwise_xor(k, dk)) * rows
            out[pl.ds(pl.multiple_of(at, rows), rows), :] = source[r].astype(jnp.float32)


def fill(own, other):
    depth, rows, width = own.shape
    return pl.pallas_call(
        fill_kernel,
        out_shape=jax.ShapeDtypeStruct((2 * depth * rows, width), jnp.float32),
        name="fill",
        compiler_params=pltpu.CompilerParams(vmem_limit_bytes=limit(6 * 2**20)),
    )(own, other)


def placed(activations, output_gradient, adapter_a, adapter_b, log_ratio, lengths, rewards):
    size = lax.axis_size("dp")
    depth = size // (2 * cores)
    rows, _ = adapter_a.shape[1:]
    everyone = [(zz, yy, kk) for zz in range(depth) for yy in range(2) for kk in range(cores)]
    number = lambda zz, yy, kk: (zz * 2 + yy) * cores + kk
    f32 = lambda value: value.astype(jnp.float32)
    half_width = lambda value: value.astype(jnp.bfloat16)

    def move(value, target):
        pairs = [(number(*at), number(*target(*at))) for at in everyone]
        return lax.ppermute(value, "dp", pairs)

    to_core = lambda value: move(value, lambda zz, yy, kk: (zz, yy, kk ^ 1))
    to_y = lambda value: move(value, lambda zz, yy, kk: (zz, yy ^ 1, kk))
    to_z = lambda value, r: move(value, lambda zz, yy, kk: (zz ^ r, yy, kk))
    across = lambda value, r: move(value, lambda zz, yy, kk: (zz ^ r, kk, yy))

    def other_tensor(value):
        return lax.ppermute(value, "tensor", [(0, 1), (1, 0)])

    bit = depth // 2
    have = {0: adapter_a[0]}
    while bit:
        for r in sorted(have):
            have[r ^ bit] = to_z(have[r], bit)
        bit //= 2
    slices = []
    for r in range(depth):
        over = to_y(have[r])
        slices.append([have[r], to_core(have[r]), over, to_core(over)])

    back = back_part(output_gradient, adapter_b)
    coefficient, stats = terms(log_ratio, lengths, rewards, activations)
    other_back = other_tensor(back)

    order = [r for r in range(depth - 1, -1, -1)]
    sums = {}
    for start in range(0, depth, 2):
        group = order[start : start + 2]
        keep, send = grad_a_part(
            activations, coefficient, back, other_back, group, rows
        )
        got = to_core(send)
        for index, r in enumerate(group):
            sums[r] = f32(keep[index]) + f32(got[index])
    got = to_y(half_width(jnp.stack([sums[1][1], sums[0][1]])))
    near = half_width(sums.pop(1)[0] + f32(got[0]))
    own = sums.pop(0)[0] + f32(got[1])
    bit = 1
    while 2 * bit < depth:
        for r in order:
            if r & bit and r in sums:
                got = to_z(half_width(sums.pop(r)), bit)
                sums[r ^ bit] = sums[r ^ bit] + f32(got)
        bit *= 2
    for r in list(sums):
        got = to_y(half_width(sums[r][1]))
        sums[r] = sums[r][0] + f32(got)
    near = to_z(near, 1)
    last = to_z(half_width(sums[bit]), bit)
    factor = stats[1, 0, 0]
    grad_a = factor * ((own + f32(near)) + f32(last))

    cut = depth - 1
    low = low_rank_part(activations, list(range(cut)), sum(slices[:cut], []))
    low = low_rank_part(activations, list(range(cut, depth)), sum(slices[cut:], []), low)
    other = other_tensor(low)
    keep, send = grad_b_part(low, other, coefficient, stats, output_gradient, depth)
    got = to_core(send)
    pieces = chip_sum(keep, got)
    total = 0.0
    for r in range(depth):
        total = total + f32(across(pieces[r], r))
    total = total + to_core(total)
    loss = jnp.sum(total[0, -lanes:])
    chunk = half_width(total[:, :-lanes])
    own = jnp.stack([across(chunk, r) for r in range(depth)])
    grad_b = fill(own, to_core(own))
    return (grad_a[None], grad_b, factor * loss)


def local(*args):
    _, _, adapter_a = args[:3]
    size = lax.axis_size("dp")
    depth = size // (2 * cores)
    rows, rank = adapter_a.shape[1:]
    fits = (
        lax.axis_size("tensor") == 2
        and size == 2 * cores * depth
        and depth == 4
        and rows % 16 == 0
        and 4 * rows % lanes == 0
        and rank == lanes
        and rank % (32 * depth) == 0
        and args[4].shape[0] % lanes == 0
    )
    return placed(*args) if fits else general(*args)


def solution(mesh):
    in_specs = (
        P("dp", "tensor"),
        P("dp", "tensor"),
        P("tensor", "dp", None),
        P(None, "tensor"),
        P("dp"),
        P(),
        P(),
    )
    out_specs = (P("tensor", "dp", None), P(None, "tensor"), P())

    return jax.shard_map(local, mesh=mesh, in_specs=in_specs, out_specs=out_specs, check_vma=False)
```

profile of v0, /device:TPU:0, one launch (start us, length us, event | category | flops | bytes accessed | tf_op | source)
XLA Modules:
  0.0 98.6 jit_solution(11212122069399119830)
XLA Ops:
  0.7 4.1 %collective-permute-start.8 = (bf16[864,128]{1,0:T(8,128)(2,1)}, bf16[864,128]{1,0:T(8,128)(2,1)S(1)}, u32[]{:S(2)}, u32[]{:S(2)}) collective-permute-start(bf16[864,128]{1,0:T(8,128)(2,1)} %bitcast.59), channel_id=1, source_target_pairs={{0,16},{2,18},{4,20},{6,22},{8,24},{10,26},{12,28},{14,30},{16,0},... | collective-permute-start | bytes 663560 | tf_op jit(solution)/shard_map/ppermute | solution.py:393
  4.8 1.3 %copy-done.2 = bf16[256,2560]{1,0:T(8,128)(2,1)S(1)} copy-done((bf16[256,2560]{1,0:T(8,128)(2,1)S(1)}, bf16[256,2560]{1,0:T(8,128)(2,1)}, u32[]{:S(2)}) %copy-start.2) | copy-done | bytes 1310744
  6.1 1.1 %copy-done.4 = bf16[128,2560]{1,0:T(8,128)(2,1)S(1)} copy-done((bf16[128,2560]{1,0:T(8,128)(2,1)S(1)}, bf16[128,2560]{1,0:T(8,128)(2,1)}, u32[]{:S(2)}) %copy-start.4) | copy-done | bytes 655384
  7.2 0.5 back.1
  7.7 1.6 %collective-permute-start = (f32[256,128]{1,0:T(8,128)S(1)}, f32[256,128]{1,0:T(8,128)S(1)}, u32[]{:S(2)}, u32[]{:S(2)}) collective-permute-start(f32[256,128]{1,0:T(8,128)S(1)} %back.1), channel_id=1, source_target_pairs={{0,1},{1,0},{2,3},{3,2},{4,5},{5,4},{6,7},{7,6},{8,9},{9,8},{10,11... | collective-permute-start | bytes 393224 | tf_op jit(solution)/shard_map/ppermute | solution.py:401
  9.2 1.5 %collective-permute-start.14 = (bf16[864,128]{1,0:T(8,128)(2,1)S(1)}, bf16[864,128]{1,0:T(8,128)(2,1)S(1)}, u32[]{:S(2)}, u32[]{:S(2)}) collective-permute-start(bf16[864,128]{1,0:T(8,128)(2,1)S(1)} %bitcast.60), channel_id=1, source_target_pairs={{0,4},{2,6},{4,0},{6,2},{8,12},{10,14},{12,8},{14,10},{16,20},{18,... | collective-permute-start | bytes 663560 | tf_op jit(solution)/shard_map/ppermute | solution.py:393
  10.8 1.6 %collective-permute-start.16 = (bf16[864,128]{1,0:T(8,128)(2,1)S(1)}, bf16[864,128]{1,0:T(8,128)(2,1)S(1)}, u32[]{:S(2)}, u32[]{:S(2)}) collective-permute-start(bf16[864,128]{1,0:T(8,128)(2,1)S(1)} %bitcast.61), channel_id=1, source_target_pairs={{0,8},{2,10},{4,12},{6,14},{8,0},{10,2},{12,4},{14,6},{16,24},{18,... | collective-permute-start | bytes 663560 | tf_op jit(solution)/shard_map/ppermute | solution.py:393
  12.4 3.0 %copy-done = bf16[256,13824]{1,0:T(8,128)(2,1)S(1)} copy-done((bf16[256,13824]{1,0:T(8,128)(2,1)S(1)}, bf16[256,13824]{1,0:T(8,128)(2,1)}, u32[]{:S(2)}) %copy-start) | copy-done | bytes 7077912
  15.4 0.8 terms.1
  16.2 0.5 collective-permute-start.9
  16.7 1.7 %copy-done.1 = bf16[256,13824]{1,0:T(8,128)(2,1)S(1)} copy-done((bf16[256,13824]{1,0:T(8,128)(2,1)S(1)}, bf16[256,13824]{1,0:T(8,128)(2,1)}, u32[]{:S(2)}) %copy-start.1) | copy-done | bytes 7077912
  18.4 1.4 %grad_a.3 = (bf16[2,2,864,128]{3,2,1,0:T(8,128)(2,1)S(1)}, bf16[2,2,864,128]{3,2,1,0:T(8,128)(2,1)S(1)}) custom-call(bf16[256,13824]{1,0:T(8,128)(2,1)S(1)} %copy-done.1, f32[256,128]{1,0:T(8,128)S(1)} %get-tuple-element.16.coefficient, f32[256,128]{1,0:T(8,128)S(1)} %back.1, f32[256,128]{1,0:T(8,128)S(1)} %collective-permute-done.other), custom_call_target="tpu_custom_call" | custom-call | flops 452984832 | bytes 5308416 | tf_op jit(solution)/shard_map/grad_a/pallas_call | solution.py:266
  19.8 0.6 collective-permute-start.4
  20.4 0.1 collective-permute-start.15
  20.5 0.4 collective-permute-start.17
  20.9 0.7 collective-permute-start.18
  21.6 3.1 %collective-permute-done.9.refs_0_ = bf16[864,128]{1,0:T(8,128)(2,1)S(1)} collective-permute-done((bf16[864,128]{1,0:T(8,128)(2,1)S(1)}, bf16[864,128]{1,0:T(8,128)(2,1)S(1)}, u32[]{:S(2)}, u32[]{:S(2)}) %collective-permute-start.9) | collective-permute-done | bytes 221216 | tf_op jit(solution)/shard_map/ppermute | solution.py:393
  24.6 0.0 collective-permute-start.20
  24.7 1.4 %grad_a.2 = (bf16[2,2,864,128]{3,2,1,0:T(8,128)(2,1)S(1)}, bf16[2,2,864,128]{3,2,1,0:T(8,128)(2,1)S(1)}) custom-call(bf16[256,13824]{1,0:T(8,128)(2,1)S(1)} %copy-done.1, f32[256,128]{1,0:T(8,128)S(1)} %get-tuple-element.16.coefficient, f32[256,128]{1,0:T(8,128)S(1)} %back.1, f32[256,128]{1,0:T(8,128)S(1)} %collective-permute-done.other), custom_call_target="tpu_custom_call" | custom-call | flops 452984832 | bytes 5308416 | tf_op jit(solution)/shard_map/grad_a/pallas_call | solution.py:266
  26.1 0.6 collective-permute-start.1
  26.7 1.3 %collective-permute-start.21 = (bf16[864,128]{1,0:T(8,128)(2,1)S(1)}, bf16[864,128]{1,0:T(8,128)(2,1)S(1)}, u32[]{:S(2)}, u32[]{:S(2)}) collective-permute-start(bf16[864,128]{1,0:T(8,128)(2,1)S(1)} %collective-permute-done.8.refs_8_), channel_id=1, source_target_pairs={{0,4},{2,6},{4,0},{6,2},{8,12},{10,14},{12,8},{14,10},{16,20},{18,... | collective-permute-start | bytes 663560 | tf_op jit(solution)/shard_map/ppermute | solution.py:393
  28.0 0.4 collective-permute-done.18.refs_6_
  28.3 1.1 %collective-permute-start.11 = (bf16[864,128]{1,0:T(8,128)(2,1)S(1)}, bf16[864,128]{1,0:T(8,128)(2,1)S(1)}, u32[]{:S(2)}, u32[]{:S(2)}) collective-permute-start(bf16[864,128]{1,0:T(8,128)(2,1)S(1)} %collective-permute-done.9.refs_0_), channel_id=1, source_target_pairs={{0,4},{2,6},{4,0},{6,2},{8,12},{10,14},{12,8},{14,10},{16,20},{18,... | collective-permute-start | bytes 663560 | tf_op jit(solution)/shard_map/ppermute | solution.py:393
  29.4 5.6 %collective-permute-done.21.refs_10_ = bf16[864,128]{1,0:T(8,128)(2,1)S(1)} collective-permute-done((bf16[864,128]{1,0:T(8,128)(2,1)S(1)}, bf16[864,128]{1,0:T(8,128)(2,1)S(1)}, u32[]{:S(2)}, u32[]{:S(2)}) %collective-permute-start.21) | collective-permute-done | bytes 221216 | tf_op jit(solution)/shard_map/ppermute | solution.py:393
  35.0 3.9 %collective-permute-done.11.refs_2_ = bf16[864,128]{1,0:T(8,128)(2,1)S(1)} collective-permute-done((bf16[864,128]{1,0:T(8,128)(2,1)S(1)}, bf16[864,128]{1,0:T(8,128)(2,1)S(1)}, u32[]{:S(2)}, u32[]{:S(2)}) %collective-permute-start.11) | collective-permute-done | bytes 221216 | tf_op jit(solution)/shard_map/ppermute | solution.py:393
  38.8 0.5 collective-permute-start.12
  39.4 0.5 slice.73
  39.9 1.7 %low_rank.2.refs_4_ = f32[256,128]{1,0:T(8,128)S(1)} custom-call(bf16[256,13824]{1,0:T(8,128)(2,1)S(1)} %copy-done.1, bf16[864,128]{1,0:T(8,128)(2,1)S(1)} %bitcast.63, bf16[864,128]{1,0:T(8,128)(2,1)S(1)} %collective-permute-done.13.refs_1_, bf16[864,128]{1,0:T(8,128)(2,1)S(1)} %collective-permute-done.14.refs_2_, ...), custom_call_target="tpu_custom_call" | custom-call | flops 679477248 | bytes 7962624 | tf_op jit(solution)/shard_map/low_rank/pallas_call | solution.py:223
  41.6 0.7 low_rank.3.low
  42.3 0.0 copy-start.3
  42.3 1.5 %collective-permute-start.23 = (f32[256,128]{1,0:T(8,128)S(1)}, f32[256,128]{1,0:T(8,128)S(1)}, u32[]{:S(2)}, u32[]{:S(2)}) collective-permute-start(f32[256,128]{1,0:T(8,128)S(1)} %low_rank.3.low), channel_id=1, source_target_pairs={{0,1},{1,0},{2,3},{3,2},{4,5},{5,4},{6,7},{7,6},{8,9},{9,8},{10,11... | collective-permute-start | bytes 393224 | tf_op jit(solution)/shard_map/ppermute | solution.py:401
  43.8 0.1 fusion
  43.9 0.1 collective-permute-start.5
  44.0 3.8 %collective-permute-done.23.other = f32[256,128]{1,0:T(8,128)S(1)} collective-permute-done((f32[256,128]{1,0:T(8,128)S(1)}, f32[256,128]{1,0:T(8,128)S(1)}, u32[]{:S(2)}, u32[]{:S(2)}) %collective-permute-start.23) | collective-permute-done | bytes 131104 | tf_op jit(solution)/shard_map/ppermute | solution.py:401
  47.8 0.5 grad_b.1
  48.3 0.1 collective-permute-start.24
  48.4 0.2 convert_add_fusion
  48.6 0.1 fusion.11
  48.6 1.4 %collective-permute-done.24.got = bf16[4,16,2688]{2,1,0:T(8,128)(2,1)S(1)} collective-permute-done((bf16[4,16,2688]{2,1,0:T(8,128)(2,1)S(1)}, bf16[4,16,2688]{2,1,0:T(8,128)(2,1)S(1)}, u32[]{:S(2)}, u32[]{:S(2)}) %collective-permute-start.24) | collective-permute-done | bytes 344096 | tf_op jit(solution)/shard_map/ppermute | solution.py:393
  50.0 0.1 chip_sum.1
  50.1 3.3 %collective-permute-start.28 = (bf16[16,2688]{1,0:T(8,128)(2,1)S(1)}, bf16[16,2688]{1,0:T(8,128)(2,1)S(1)}, u32[]{:S(2)}, u32[]{:S(2)}) collective-permute-start(bf16[16,2688]{1,0:T(8,128)(2,1)S(1)} %get-tuple-element.26), channel_id=1, source_target_pairs={{0,24},{2,28},{4,26},{6,30},{8,16},{10,20},{12,18},{14,22},{16,8},... | collective-permute-start | bytes 258056 | tf_op jit(solution)/shard_map/ppermute | solution.py:393
  53.4 1.2 %collective-permute-start.26 = (bf16[16,2688]{1,0:T(8,128)(2,1)S(1)}, bf16[16,2688]{1,0:T(8,128)(2,1)S(1)}, u32[]{:S(2)}, u32[]{:S(2)}) collective-permute-start(bf16[16,2688]{1,0:T(8,128)(2,1)S(1)} %get-tuple-element.24), channel_id=1, source_target_pairs={{0,8},{2,12},{4,10},{6,14},{8,0},{10,4},{12,2},{14,6},{16,24},{18,... | collective-permute-start | bytes 258056 | tf_op jit(solution)/shard_map/ppermute | solution.py:393
  54.6 0.7 collective-permute-start.25
  55.3 4.0 %collective-permute-done.28 = bf16[16,2688]{1,0:T(8,128)(2,1)S(1)} collective-permute-done((bf16[16,2688]{1,0:T(8,128)(2,1)S(1)}, bf16[16,2688]{1,0:T(8,128)(2,1)S(1)}, u32[]{:S(2)}, u32[]{:S(2)}) %collective-permute-start.28) | collective-permute-done | bytes 86048 | tf_op jit(solution)/shard_map/ppermute | solution.py:393
  59.3 0.4 collective-permute-start.2
  59.7 2.3 %collective-permute-done.27 = bf16[16,2688]{1,0:T(8,128)(2,1)S(1)} collective-permute-done((bf16[16,2688]{1,0:T(8,128)(2,1)S(1)}, bf16[16,2688]{1,0:T(8,128)(2,1)S(1)}, u32[]{:S(2)}, u32[]{:S(2)}) %collective-permute-start.27) | collective-permute-done | bytes 86048 | tf_op jit(solution)/shard_map/ppermute | solution.py:393
  62.1 0.6 collective-permute-start.29
  62.7 0.1 bitcast_add_fusion
  62.8 1.0 %collective-permute-start.6 = (bf16[864,128]{1,0:T(8,128)(2,1)S(1)}, bf16[864,128]{1,0:T(8,128)(2,1)S(1)}, u32[]{:S(2)}, u32[]{:S(2)}) collective-permute-start(bf16[864,128]{1,0:T(8,128)(2,1)S(1)} %fusion.14), channel_id=1, source_target_pairs={{0,4},{2,6},{4,0},{6,2},{8,12},{10,14},{12,8},{14,10},{16,20},{18,... | collective-permute-start | bytes 663560 | tf_op jit(solution)/shard_map/ppermute | solution.py:393
  63.9 8.4 %collective-permute-done.2 = bf16[2,864,128]{2,1,0:T(8,128)(2,1)S(1)} collective-permute-done((bf16[2,864,128]{2,1,0:T(8,128)(2,1)S(1)}, bf16[2,864,128]{2,1,0:T(8,128)(2,1)S(1)}, u32[]{:S(2)}, u32[]{:S(2)}) %collective-permute-start.2) | collective-permute-done | bytes 442400 | tf_op jit(solution)/shard_map/ppermute | solution.py:393
  72.3 0.1 fusion.13
  72.4 1.4 %collective-permute-start.3 = (bf16[864,128]{1,0:T(8,128)(2,1)S(1)}, bf16[864,128]{1,0:T(8,128)(2,1)S(1)}, u32[]{:S(2)}, u32[]{:S(2)}) collective-permute-start(bf16[864,128]{1,0:T(8,128)(2,1)S(1)} %fusion.13), channel_id=1, source_target_pairs={{0,8},{2,10},{4,12},{6,14},{8,0},{10,2},{12,4},{14,6},{16,24},{18,... | collective-permute-start | bytes 663560 | tf_op jit(solution)/shard_map/ppermute | solution.py:393
  73.8 1.9 %collective-permute-start.33 = (bf16[16,2560]{1,0:T(8,128)(2,1)S(1)}, bf16[16,2560]{1,0:T(8,128)(2,1)S(1)}, u32[]{:S(2)}, u32[]{:S(2)}) collective-permute-start(bf16[16,2560]{1,0:T(8,128)(2,1)S(1)} %slice.156), channel_id=1, source_target_pairs={{0,24},{2,28},{4,26},{6,30},{8,16},{10,20},{12,18},{14,22},{16,8},... | collective-permute-start | bytes 245768 | tf_op jit(solution)/shard_map/ppermute | solution.py:393
  75.7 0.3 collective-permute-start.32
  76.0 2.2 %collective-permute-start.31 = (bf16[16,2560]{1,0:T(8,128)(2,1)S(1)}, bf16[16,2560]{1,0:T(8,128)(2,1)S(1)}, u32[]{:S(2)}, u32[]{:S(2)}) collective-permute-start(bf16[16,2560]{1,0:T(8,128)(2,1)S(1)} %slice.156), channel_id=1, source_target_pairs={{0,8},{2,12},{4,10},{6,14},{8,0},{10,4},{12,2},{14,6},{16,24},{18,... | collective-permute-start | bytes 245768 | tf_op jit(solution)/shard_map/ppermute | solution.py:393
  78.2 0.7 collective-permute-start.30
  78.9 0.1 fusion.2
  79.0 4.2 %collective-permute-done.33 = bf16[16,2560]{1,0:T(8,128)(2,1)S(1)} collective-permute-done((bf16[16,2560]{1,0:T(8,128)(2,1)S(1)}, bf16[16,2560]{1,0:T(8,128)(2,1)S(1)}, u32[]{:S(2)}, u32[]{:S(2)}) %collective-permute-start.33) | collective-permute-done | bytes 81952 | tf_op jit(solution)/shard_map/ppermute | solution.py:393
  83.2 1.0 %collective-permute-done.31 = bf16[16,2560]{1,0:T(8,128)(2,1)S(1)} collective-permute-done((bf16[16,2560]{1,0:T(8,128)(2,1)S(1)}, bf16[16,2560]{1,0:T(8,128)(2,1)S(1)}, u32[]{:S(2)}, u32[]{:S(2)}) %collective-permute-start.31) | collective-permute-done | bytes 81952 | tf_op jit(solution)/shard_map/ppermute | solution.py:393
  84.3 0.6 collective-permute-start.34
  84.9 0.6 slice_reduce_fusion
  86.8 8.0 %collective-permute-done.7 = bf16[864,128]{1,0:T(8,128)(2,1)S(1)} collective-permute-done((bf16[864,128]{1,0:T(8,128)(2,1)S(1)}, bf16[864,128]{1,0:T(8,128)(2,1)S(1)}, u32[]{:S(2)}, u32[]{:S(2)}) %collective-permute-start.7) | collective-permute-done | bytes 221216 | tf_op jit(solution)/shard_map/ppermute | solution.py:393
  94.8 1.5 %fusion.10 = f32[1,864,128]{2,1,0:T(8,128)} fusion(f32[1,2,864,128]{3,2,1,0:T(8,128)S(1)} %get-tuple-element.28, bf16[864,128]{1,0:T(8,128)(2,1)S(1)} %collective-permute-done.7, bf16[864,128]{1,0:T(8,128)(2,1)S(1)} %collective-permute-done.3, bf16[2,864,128]{2,1,0:T(8,128)(2,1)S(1)} %collective-permute-done.2, f32[]{:T(128)} %bitcast.1), kind=kLoop, calls=%fused_computation.20 | loop fusion | flops 774144 | bytes 1548292 | tf_op jit(solution)/shard_map/broadcast_in_dim | solution.py:461
  96.3 1.2 %fill.1 = f32[128,2560]{1,0:T(8,128)} custom-call(bf16[4,16,2560]{2,1,0:T(8,128)(2,1)S(1)} %pad_maximum_fusion.1.own, bf16[4,16,2560]{2,1,0:T(8,128)(2,1)S(1)} %collective-permute-done.34.other), custom_call_target="tpu_custom_call" | custom-call | tf_op jit(solution)/shard_map/fill/pallas_call | solution.py:374
  (48 shorter events, 0.3 us)
Async XLA Ops:
  0.6 11.7 %copy-start.7 = (s32[1,16]{1,0:T(1,128)S(1)}, s32[1,16]{1,0:T(1,128)}, u32[]{:S(2)}) copy-start(s32[1,16]{1,0:T(1,128)} %lengths.1) | copy-start | bytes 196
  0.6 11.7 %copy-start.6 = (f32[256]{0:T(256)S(1)}, f32[256]{0:T(256)}, u32[]{:S(2)}) copy-start(f32[256]{0:T(256)} %param.11) | copy-start | bytes 3076
  0.7 15.5 %collective-permute-start.8 = (bf16[864,128]{1,0:T(8,128)(2,1)}, bf16[864,128]{1,0:T(8,128)(2,1)S(1)}, u32[]{:S(2)}, u32[]{:S(2)}) collective-permute-start(bf16[864,128]{1,0:T(8,128)(2,1)} %bitcast.59), channel_id=1, source_target_pairs={{0,16},{2,18},{4,20},{6,22},{8,24},{10,26},{12,28},{14,30},{16,0},... | collective-permute-start | bytes 663560 | tf_op jit(solution)/shard_map/ppermute | solution.py:393
  4.8 1.3 %copy-start.2 = (bf16[256,2560]{1,0:T(8,128)(2,1)S(1)}, bf16[256,2560]{1,0:T(8,128)(2,1)}, u32[]{:S(2)}) copy-start(bf16[256,2560]{1,0:T(8,128)(2,1)} %grad.3) | copy-start | bytes 3932164
  6.1 1.1 %copy-start.4 = (bf16[128,2560]{1,0:T(8,128)(2,1)S(1)}, bf16[128,2560]{1,0:T(8,128)(2,1)}, u32[]{:S(2)}) copy-start(bf16[128,2560]{1,0:T(8,128)(2,1)} %factor.1) | copy-start | bytes 1966084
  7.2 2.1 %copy-start.5 = (bf16[1,864,128]{2,1,0:T(8,128)(2,1)S(1)}, bf16[1,864,128]{2,1,0:T(8,128)(2,1)}, u32[]{:S(2)}) copy-start(bf16[1,864,128]{2,1,0:T(8,128)(2,1)} %param.9) | copy-start | bytes 663556
  7.2 5.2 %copy-start.8 = (s32[1,16]{1,0:T(1,128)S(1)}, s32[1,16]{1,0:T(1,128)}, u32[]{:S(2)}) copy-start(s32[1,16]{1,0:T(1,128)} %rewards.1) | copy-start | bytes 196
  7.7 9.0 %collective-permute-start = (f32[256,128]{1,0:T(8,128)S(1)}, f32[256,128]{1,0:T(8,128)S(1)}, u32[]{:S(2)}, u32[]{:S(2)}) collective-permute-start(f32[256,128]{1,0:T(8,128)S(1)} %back.1), channel_id=1, source_target_pairs={{0,1},{1,0},{2,3},{3,2},{4,5},{5,4},{6,7},{7,6},{8,9},{9,8},{10,11... | collective-permute-start | bytes 393224 | tf_op jit(solution)/shard_map/ppermute | solution.py:401
  9.2 11.2 %collective-permute-start.14 = (bf16[864,128]{1,0:T(8,128)(2,1)S(1)}, bf16[864,128]{1,0:T(8,128)(2,1)S(1)}, u32[]{:S(2)}, u32[]{:S(2)}) collective-permute-start(bf16[864,128]{1,0:T(8,128)(2,1)S(1)} %bitcast.60), channel_id=1, source_target_pairs={{0,4},{2,6},{4,0},{6,2},{8,12},{10,14},{12,8},{14,10},{16,20},{18,... | collective-permute-start | bytes 663560 | tf_op jit(solution)/shard_map/ppermute | solution.py:393
  10.8 9.7 %collective-permute-start.16 = (bf16[864,128]{1,0:T(8,128)(2,1)S(1)}, bf16[864,128]{1,0:T(8,128)(2,1)S(1)}, u32[]{:S(2)}, u32[]{:S(2)}) collective-permute-start(bf16[864,128]{1,0:T(8,128)(2,1)S(1)} %bitcast.61), channel_id=1, source_target_pairs={{0,8},{2,10},{4,12},{6,14},{8,0},{10,2},{12,4},{14,6},{16,24},{18,... | collective-permute-start | bytes 663560 | tf_op jit(solution)/shard_map/ppermute | solution.py:393
  12.3 8.6 %collective-permute-start.13 = (bf16[864,128]{1,0:T(8,128)(2,1)S(1)}, bf16[864,128]{1,0:T(8,128)(2,1)S(1)}, u32[]{:S(2)}, u32[]{:S(2)}) collective-permute-start(bf16[864,128]{1,0:T(8,128)(2,1)S(1)} %bitcast.62), channel_id=1, source_target_pairs={{0,2},{2,0},{4,6},{6,4},{8,10},{10,8},{12,14},{14,12},{16,18},{18,... | collective-permute-start | bytes 663560 | tf_op jit(solution)/shard_map/ppermute | solution.py:393
  12.4 3.0 %copy-start = (bf16[256,13824]{1,0:T(8,128)(2,1)S(1)}, bf16[256,13824]{1,0:T(8,128)(2,1)}, u32[]{:S(2)}) copy-start(bf16[256,13824]{1,0:T(8,128)(2,1)} %acts.7) | copy-start | bytes 21233668
  15.4 3.0 %copy-start.1 = (bf16[256,13824]{1,0:T(8,128)(2,1)S(1)}, bf16[256,13824]{1,0:T(8,128)(2,1)}, u32[]{:S(2)}) copy-start(bf16[256,13824]{1,0:T(8,128)(2,1)} %acts.7) | copy-start | bytes 21233668
  16.2 8.5 %collective-permute-start.9 = (bf16[864,128]{1,0:T(8,128)(2,1)S(1)}, bf16[864,128]{1,0:T(8,128)(2,1)S(1)}, u32[]{:S(2)}, u32[]{:S(2)}) collective-permute-start(bf16[864,128]{1,0:T(8,128)(2,1)S(1)} %collective-permute-done.8.refs_8_), channel_id=1, source_target_pairs={{0,8},{2,10},{4,12},{6,14},{8,0},{10,2},{12,4},{14,6},{16,24},{18,... | collective-permute-start | bytes 663560 | tf_op jit(solution)/shard_map/ppermute | solution.py:393
  19.8 24.0 %collective-permute-start.4 = (bf16[2,2,864,128]{3,2,1,0:T(8,128)(2,1)S(1)}, bf16[2,2,864,128]{3,2,1,0:T(8,128)(2,1)S(1)}, u32[]{:S(2)}, u32[]{:S(2)}) collective-permute-start(bf16[2,2,864,128]{3,2,1,0:T(8,128)(2,1)S(1)} %get-tuple-element.20), channel_id=1, source_target_pairs={{0,2},{2,0},{4,6},{6,4},{8,10},{10,8},{12,14},{14,12},{16,18},{18,... | collective-permute-start | bytes 2654216 | tf_op jit(solution)/shard_map/ppermute | solution.py:393
  20.4 5.7 %collective-permute-start.15 = (bf16[864,128]{1,0:T(8,128)(2,1)S(1)}, bf16[864,128]{1,0:T(8,128)(2,1)S(1)}, u32[]{:S(2)}, u32[]{:S(2)}) collective-permute-start(bf16[864,128]{1,0:T(8,128)(2,1)S(1)} %collective-permute-done.14.refs_2_), channel_id=1, source_target_pairs={{0,2},{2,0},{4,6},{6,4},{8,10},{10,8},{12,14},{14,12},{16,18},{18,... | collective-permute-start | bytes 663560 | tf_op jit(solution)/shard_map/ppermute | solution.py:393
  20.5 6.2 %collective-permute-start.17 = (bf16[864,128]{1,0:T(8,128)(2,1)S(1)}, bf16[864,128]{1,0:T(8,128)(2,1)S(1)}, u32[]{:S(2)}, u32[]{:S(2)}) collective-permute-start(bf16[864,128]{1,0:T(8,128)(2,1)S(1)} %collective-permute-done.16.refs_4_), channel_id=1, source_target_pairs={{0,2},{2,0},{4,6},{6,4},{8,10},{10,8},{12,14},{14,12},{16,18},{18,... | collective-permute-start | bytes 663560 | tf_op jit(solution)/shard_map/ppermute | solution.py:393
  20.9 7.4 %collective-permute-start.18 = (bf16[864,128]{1,0:T(8,128)(2,1)S(1)}, bf16[864,128]{1,0:T(8,128)(2,1)S(1)}, u32[]{:S(2)}, u32[]{:S(2)}) collective-permute-start(bf16[864,128]{1,0:T(8,128)(2,1)S(1)} %collective-permute-done.16.refs_4_), channel_id=1, source_target_pairs={{0,4},{2,6},{4,0},{6,2},{8,12},{10,14},{12,8},{14,10},{16,20},{18,... | collective-permute-start | bytes 663560 | tf_op jit(solution)/shard_map/ppermute | solution.py:393
  24.6 4.8 %collective-permute-start.20 = (bf16[864,128]{1,0:T(8,128)(2,1)S(1)}, bf16[864,128]{1,0:T(8,128)(2,1)S(1)}, u32[]{:S(2)}, u32[]{:S(2)}) collective-permute-start(bf16[864,128]{1,0:T(8,128)(2,1)S(1)} %collective-permute-done.8.refs_8_), channel_id=1, source_target_pairs={{0,2},{2,0},{4,6},{6,4},{8,10},{10,8},{12,14},{14,12},{16,18},{18,... | collective-permute-start | bytes 663560 | tf_op jit(solution)/shard_map/ppermute | solution.py:393
  26.1 22.3 %collective-permute-start.1 = (bf16[2,2,864,128]{3,2,1,0:T(8,128)(2,1)S(1)}, bf16[2,2,864,128]{3,2,1,0:T(8,128)(2,1)S(1)}, u32[]{:S(2)}, u32[]{:S(2)}) collective-permute-start(bf16[2,2,864,128]{3,2,1,0:T(8,128)(2,1)S(1)} %get-tuple-element.18), channel_id=1, source_target_pairs={{0,2},{2,0},{4,6},{6,4},{8,10},{10,8},{12,14},{14,12},{16,18},{18,... | collective-permute-start | bytes 2654216 | tf_op jit(solution)/shard_map/ppermute | solution.py:393
  26.7 8.3 %collective-permute-start.21 = (bf16[864,128]{1,0:T(8,128)(2,1)S(1)}, bf16[864,128]{1,0:T(8,128)(2,1)S(1)}, u32[]{:S(2)}, u32[]{:S(2)}) collective-permute-start(bf16[864,128]{1,0:T(8,128)(2,1)S(1)} %collective-permute-done.8.refs_8_), channel_id=1, source_target_pairs={{0,4},{2,6},{4,0},{6,2},{8,12},{10,14},{12,8},{14,10},{16,20},{18,... | collective-permute-start | bytes 663560 | tf_op jit(solution)/shard_map/ppermute | solution.py:393
  28.3 10.5 %collective-permute-start.11 = (bf16[864,128]{1,0:T(8,128)(2,1)S(1)}, bf16[864,128]{1,0:T(8,128)(2,1)S(1)}, u32[]{:S(2)}, u32[]{:S(2)}) collective-permute-start(bf16[864,128]{1,0:T(8,128)(2,1)S(1)} %collective-permute-done.9.refs_0_), channel_id=1, source_target_pairs={{0,4},{2,6},{4,0},{6,2},{8,12},{10,14},{12,8},{14,10},{16,20},{18,... | collective-permute-start | bytes 663560 | tf_op jit(solution)/shard_map/ppermute | solution.py:393
  29.4 9.4 %collective-permute-start.19 = (bf16[864,128]{1,0:T(8,128)(2,1)S(1)}, bf16[864,128]{1,0:T(8,128)(2,1)S(1)}, u32[]{:S(2)}, u32[]{:S(2)}) collective-permute-start(bf16[864,128]{1,0:T(8,128)(2,1)S(1)} %collective-permute-done.18.refs_6_), channel_id=1, source_target_pairs={{0,2},{2,0},{4,6},{6,4},{8,10},{10,8},{12,14},{14,12},{16,18},{18,... | collective-permute-start | bytes 663560 | tf_op jit(solution)/shard_map/ppermute | solution.py:393
  35.0 4.9 %collective-permute-start.22 = (bf16[864,128]{1,0:T(8,128)(2,1)S(1)}, bf16[864,128]{1,0:T(8,128)(2,1)S(1)}, u32[]{:S(2)}, u32[]{:S(2)}) collective-permute-start(bf16[864,128]{1,0:T(8,128)(2,1)S(1)} %collective-permute-done.21.refs_10_), channel_id=1, source_target_pairs={{0,2},{2,0},{4,6},{6,4},{8,10},{10,8},{12,14},{14,12},{16,18},{18,... | collective-permute-start | bytes 663560 | tf_op jit(solution)/shard_map/ppermute | solution.py:393
  38.8 2.7 %collective-permute-start.10 = (bf16[864,128]{1,0:T(8,128)(2,1)S(1)}, bf16[864,128]{1,0:T(8,128)(2,1)S(1)}, u32[]{:S(2)}, u32[]{:S(2)}) collective-permute-start(bf16[864,128]{1,0:T(8,128)(2,1)S(1)} %collective-permute-done.9.refs_0_), channel_id=1, source_target_pairs={{0,2},{2,0},{4,6},{6,4},{8,10},{10,8},{12,14},{14,12},{16,18},{18,... | collective-permute-start | bytes 663560 | tf_op jit(solution)/shard_map/ppermute | solution.py:393
  38.8 2.7 %collective-permute-start.12 = (bf16[864,128]{1,0:T(8,128)(2,1)S(1)}, bf16[864,128]{1,0:T(8,128)(2,1)S(1)}, u32[]{:S(2)}, u32[]{:S(2)}) collective-permute-start(bf16[864,128]{1,0:T(8,128)(2,1)S(1)} %collective-permute-done.11.refs_2_), channel_id=1, source_target_pairs={{0,2},{2,0},{4,6},{6,4},{8,10},{10,8},{12,14},{14,12},{16,18},{18,... | collective-permute-start | bytes 663560 | tf_op jit(solution)/shard_map/ppermute | solution.py:393
  42.3 5.5 %copy-start.3 = (bf16[256,2560]{1,0:T(8,128)(2,1)S(1)}, bf16[256,2560]{1,0:T(8,128)(2,1)}, u32[]{:S(2)}) copy-start(bf16[256,2560]{1,0:T(8,128)(2,1)} %grad.3) | copy-start | bytes 3932164
  42.3 5.5 %collective-permute-start.23 = (f32[256,128]{1,0:T(8,128)S(1)}, f32[256,128]{1,0:T(8,128)S(1)}, u32[]{:S(2)}, u32[]{:S(2)}) collective-permute-start(f32[256,128]{1,0:T(8,128)S(1)} %low_rank.3.low), channel_id=1, source_target_pairs={{0,1},{1,0},{2,3},{3,2},{4,5},{5,4},{6,7},{7,6},{8,9},{9,8},{10,11... | collective-permute-start | bytes 393224 | tf_op jit(solution)/shard_map/ppermute | solution.py:401
  43.9 18.7 %collective-permute-start.5 = (bf16[2,864,128]{2,1,0:T(8,128)(2,1)S(1)}, bf16[2,864,128]{2,1,0:T(8,128)(2,1)S(1)}, u32[]{:S(2)}, u32[]{:S(2)}) collective-permute-start(bf16[2,864,128]{2,1,0:T(8,128)(2,1)S(1)} %fusion), channel_id=1, source_target_pairs={{0,8},{2,10},{4,12},{6,14},{8,0},{10,2},{12,4},{14,6},{16,24},{18,... | collective-permute-start | bytes 1327112 | tf_op jit(solution)/shard_map/ppermute | solution.py:393
  48.3 1.7 %collective-permute-start.24 = (bf16[4,16,2688]{2,1,0:T(8,128)(2,1)S(1)}, bf16[4,16,2688]{2,1,0:T(8,128)(2,1)S(1)}, u32[]{:S(2)}, u32[]{:S(2)}) collective-permute-start(bf16[4,16,2688]{2,1,0:T(8,128)(2,1)S(1)} %get-tuple-element.22), channel_id=1, source_target_pairs={{0,2},{2,0},{4,6},{6,4},{8,10},{10,8},{12,14},{14,12},{16,18},{18,... | collective-permute-start | bytes 1032200 | tf_op jit(solution)/shard_map/ppermute | solution.py:393
  50.1 9.1 %collective-permute-start.28 = (bf16[16,2688]{1,0:T(8,128)(2,1)S(1)}, bf16[16,2688]{1,0:T(8,128)(2,1)S(1)}, u32[]{:S(2)}, u32[]{:S(2)}) collective-permute-start(bf16[16,2688]{1,0:T(8,128)(2,1)S(1)} %get-tuple-element.26), channel_id=1, source_target_pairs={{0,24},{2,28},{4,26},{6,30},{8,16},{10,20},{12,18},{14,22},{16,8},... | collective-permute-start | bytes 258056 | tf_op jit(solution)/shard_map/ppermute | solution.py:393
  53.4 8.6 %collective-permute-start.27 = (bf16[16,2688]{1,0:T(8,128)(2,1)S(1)}, bf16[16,2688]{1,0:T(8,128)(2,1)S(1)}, u32[]{:S(2)}, u32[]{:S(2)}) collective-permute-start(bf16[16,2688]{1,0:T(8,128)(2,1)S(1)} %get-tuple-element.25), channel_id=1, source_target_pairs={{0,16},{2,20},{4,18},{6,22},{8,24},{10,28},{12,26},{14,30},{16,0},... | collective-permute-start | bytes 258056 | tf_op jit(solution)/shard_map/ppermute | solution.py:393
  53.4 8.6 %collective-permute-start.26 = (bf16[16,2688]{1,0:T(8,128)(2,1)S(1)}, bf16[16,2688]{1,0:T(8,128)(2,1)S(1)}, u32[]{:S(2)}, u32[]{:S(2)}) collective-permute-start(bf16[16,2688]{1,0:T(8,128)(2,1)S(1)} %get-tuple-element.24), channel_id=1, source_target_pairs={{0,8},{2,12},{4,10},{6,14},{8,0},{10,4},{12,2},{14,6},{16,24},{18,... | collective-permute-start | bytes 258056 | tf_op jit(solution)/shard_map/ppermute | solution.py:393
  54.6 7.5 %collective-permute-start.25 = (bf16[16,2688]{1,0:T(8,128)(2,1)S(1)}, bf16[16,2688]{1,0:T(8,128)(2,1)S(1)}, u32[]{:S(2)}, u32[]{:S(2)}) collective-permute-start(bf16[16,2688]{1,0:T(8,128)(2,1)S(1)} %get-tuple-element.23), channel_id=1, source_target_pairs={{0,0},{2,4},{4,2},{6,6},{8,8},{10,12},{12,10},{14,14},{16,16},{18,... | collective-permute-start | bytes 258056 | tf_op jit(solution)/shard_map/ppermute | solution.py:393
  59.3 13.0 %collective-permute-start.2 = (bf16[2,864,128]{2,1,0:T(8,128)(2,1)S(1)}, bf16[2,864,128]{2,1,0:T(8,128)(2,1)S(1)}, u32[]{:S(2)}, u32[]{:S(2)}) collective-permute-start(bf16[2,864,128]{2,1,0:T(8,128)(2,1)S(1)} %pad_maximum_fusion), channel_id=1, source_target_pairs={{0,4},{2,6},{4,0},{6,2},{8,12},{10,14},{12,8},{14,10},{16,20},{18,... | collective-permute-start | bytes 1327112 | tf_op jit(solution)/shard_map/ppermute | solution.py:393
  62.1 11.7 %collective-permute-start.29 = (f32[16,2688]{1,0:T(8,128)S(1)}, f32[16,2688]{1,0:T(8,128)S(1)}, u32[]{:S(2)}, u32[]{:S(2)}) collective-permute-start(f32[16,2688]{1,0:T(8,128)S(1)} %convert_add_fusion.2), channel_id=1, source_target_pairs={{0,2},{2,0},{4,6},{6,4},{8,10},{10,8},{12,14},{14,12},{16,18},{18,... | collective-permute-start | bytes 516104 | tf_op jit(solution)/shard_map/ppermute | solution.py:393
  62.8 15.4 %collective-permute-start.6 = (bf16[864,128]{1,0:T(8,128)(2,1)S(1)}, bf16[864,128]{1,0:T(8,128)(2,1)S(1)}, u32[]{:S(2)}, u32[]{:S(2)}) collective-permute-start(bf16[864,128]{1,0:T(8,128)(2,1)S(1)} %fusion.14), channel_id=1, source_target_pairs={{0,4},{2,6},{4,0},{6,2},{8,12},{10,14},{12,8},{14,10},{16,20},{18,... | collective-permute-start | bytes 663560 | tf_op jit(solution)/shard_map/ppermute | solution.py:393
  72.4 14.4 %collective-permute-start.3 = (bf16[864,128]{1,0:T(8,128)(2,1)S(1)}, bf16[864,128]{1,0:T(8,128)(2,1)S(1)}, u32[]{:S(2)}, u32[]{:S(2)}) collective-permute-start(bf16[864,128]{1,0:T(8,128)(2,1)S(1)} %fusion.13), channel_id=1, source_target_pairs={{0,8},{2,10},{4,12},{6,14},{8,0},{10,2},{12,4},{14,6},{16,24},{18,... | collective-permute-start | bytes 663560 | tf_op jit(solution)/shard_map/ppermute | solution.py:393
  73.8 9.4 %collective-permute-start.33 = (bf16[16,2560]{1,0:T(8,128)(2,1)S(1)}, bf16[16,2560]{1,0:T(8,128)(2,1)S(1)}, u32[]{:S(2)}, u32[]{:S(2)}) collective-permute-start(bf16[16,2560]{1,0:T(8,128)(2,1)S(1)} %slice.156), channel_id=1, source_target_pairs={{0,24},{2,28},{4,26},{6,30},{8,16},{10,20},{12,18},{14,22},{16,8},... | collective-permute-start | bytes 245768 | tf_op jit(solution)/shard_map/ppermute | solution.py:393
  75.7 7.5 %collective-permute-start.32 = (bf16[16,2560]{1,0:T(8,128)(2,1)S(1)}, bf16[16,2560]{1,0:T(8,128)(2,1)S(1)}, u32[]{:S(2)}, u32[]{:S(2)}) collective-permute-start(bf16[16,2560]{1,0:T(8,128)(2,1)S(1)} %slice.156), channel_id=1, source_target_pairs={{0,16},{2,20},{4,18},{6,22},{8,24},{10,28},{12,26},{14,30},{16,0},... | collective-permute-start | bytes 245768 | tf_op jit(solution)/shard_map/ppermute | solution.py:393
  76.0 8.2 %collective-permute-start.31 = (bf16[16,2560]{1,0:T(8,128)(2,1)S(1)}, bf16[16,2560]{1,0:T(8,128)(2,1)S(1)}, u32[]{:S(2)}, u32[]{:S(2)}) collective-permute-start(bf16[16,2560]{1,0:T(8,128)(2,1)S(1)} %slice.156), channel_id=1, source_target_pairs={{0,8},{2,12},{4,10},{6,14},{8,0},{10,4},{12,2},{14,6},{16,24},{18,... | collective-permute-start | bytes 245768 | tf_op jit(solution)/shard_map/ppermute | solution.py:393
  78.2 6.0 %collective-permute-start.30 = (bf16[16,2560]{1,0:T(8,128)(2,1)S(1)}, bf16[16,2560]{1,0:T(8,128)(2,1)S(1)}, u32[]{:S(2)}, u32[]{:S(2)}) collective-permute-start(bf16[16,2560]{1,0:T(8,128)(2,1)S(1)} %slice.156), channel_id=1, source_target_pairs={{0,0},{2,4},{4,2},{6,6},{8,8},{10,12},{12,10},{14,14},{16,16},{18,... | collective-permute-start | bytes 245768 | tf_op jit(solution)/shard_map/ppermute | solution.py:393
  83.2 11.6 %collective-permute-start.7 = (bf16[864,128]{1,0:T(8,128)(2,1)S(1)}, bf16[864,128]{1,0:T(8,128)(2,1)S(1)}, u32[]{:S(2)}, u32[]{:S(2)}) collective-permute-start(bf16[864,128]{1,0:T(8,128)(2,1)S(1)} %fusion.2), channel_id=1, source_target_pairs={{0,16},{2,18},{4,20},{6,22},{8,24},{10,26},{12,28},{14,30},{16,0},... | collective-permute-start | bytes 663560 | tf_op jit(solution)/shard_map/ppermute | solution.py:393
  84.3 12.0 %collective-permute-start.34 = (bf16[4,16,2560]{2,1,0:T(8,128)(2,1)S(1)}, bf16[4,16,2560]{2,1,0:T(8,128)(2,1)S(1)}, u32[]{:S(2)}, u32[]{:S(2)}) collective-permute-start(bf16[4,16,2560]{2,1,0:T(8,128)(2,1)S(1)} %pad_maximum_fusion.1.own), channel_id=1, source_target_pairs={{0,2},{2,0},{4,6},{6,4},{8,10},{10,8},{12,14},{14,12},{16,18},{18,... | collective-permute-start | bytes 983048 | tf_op jit(solution)/shard_map/ppermute | solution.py:393
where the time goes:
time: 98.9 us; the launch traced here: 98.6 us
  waiting for transfers between devices  46 us (47%)
  starting transfers between devices  30.3 us (31%)
  Pallas kernels  8.3 us (8%)
  local copies, waits for them, and re-layouts  7.75 us (8%)
  between operations  3.34 us (3%)
  other arithmetic  2.85 us (3%)
    ppermute x33, waiting for transfers between devices, move(): return lax.ppermute(value, 'dp', pairs)  42.2 us
    ppermute x33, starting transfers between devices, move(): return lax.ppermute(value, 'dp', pairs)  27.3 us
    unnamed x18, local copies, waits for them, and re-layouts  7.14 us
    ppermute x2, waiting for transfers between devices, other_tensor(): return lax.ppermute(value, 'tensor', [(0, 1), (1, 0)])  3.79 us
    ppermute x2, starting transfers between devices, other_tensor(): return lax.ppermute(value, 'tensor', [(0, 1), (1, 0)])  3.03 us
    pallas_call x2, Pallas kernels, grad_a_part(): pl.pallas_call(functools.partial(grad_a_kernel, rounds), in_specs=[vmem]...  2.88 us
    pallas_call x2, Pallas kernels, low_rank_part(): pl.pallas_call(functools.partial(low_rank_kernel, rounds, before is not N...  2.41 us
  transfers between devices with their start and end apart: 35, of which 12 were waited for; matrix products, arithmetic and copies ran while one was open for 4% of the time, Pallas kernels for 7%

commit v1 on v0

--- a/solution.py
+++ b/solution.py
@@ -96,7 +96,7 @@
     return pl.ds(pl.multiple_of((lax.bitwise_xor(y, dy) * 2 + lax.bitwise_xor(k, dk)) * rows, 16), rows)
 
 
-def terms_kernel(lengths, rewards, log_ratio, _, spread_out, stats, *, per_group):
+def terms_kernel(lengths, rewards, log_ratio, spread_out, stats, *, per_group):
     groups, count = lengths.shape
     lines = log_ratio.shape[0]
     shape = (lines, lanes)
@@ -139,35 +139,50 @@
     stats[1] = groups / jnp.full(stats.shape[1:], total, jnp.int32).astype(jnp.float32)
 
 
-def terms(log_ratio, lengths, rewards, activations):
+def terms(log_ratio, lengths, rewards):
     tokens = log_ratio.shape[0]
     per_group = lax.axis_size("dp") // lengths.shape[0]
     return pl.pallas_call(
         functools.partial(terms_kernel, per_group=per_group),
         in_specs=[pl.BlockSpec(memory_space=pltpu.SMEM)] * 2
-        + [vmem] * 2,
+        + [vmem],
         out_specs=[vmem] * 2,
         out_shape=[
             jax.ShapeDtypeStruct((tokens, lanes), jnp.float32),
             jax.ShapeDtypeStruct((2, 8, lanes), jnp.float32),
         ],
         name="terms",
-        compiler_params=pltpu.CompilerParams(vmem_limit_bytes=limit(2 * activations.size)),
-    )(lengths, rewards, log_ratio.reshape(tokens // lanes, lanes), activations)
-
-
-def back_kernel(grad, factor, out):
+        compiler_params=pltpu.CompilerParams(vmem_limit_bytes=limit(2**20)),
+    )(lengths, rewards, log_ratio.reshape(tokens // lanes, lanes))
+
+
+def lead_kernel(out):
+    out[...] = jnp.zeros(out.shape, out.dtype)
+
+
+def lead():
+    return pl.pallas_call(
+        lead_kernel,
+        out_specs=vmem,
+        out_shape=jax.ShapeDtypeStruct((8, lanes), jnp.float32),
+        cost_estimate=pl.CostEstimate(flops=10**10, bytes_accessed=0, transcendentals=0),
+        name="lead",
+        compiler_params=pltpu.CompilerParams(vmem_limit_bytes=limit(0)),
+    )()
+
+
+def back_kernel(grad, factor, _, out):
     out[...] = lax.dot_general(
         grad[...], factor[...], (((1,), (1,)), ((), ())), preferred_element_type=jnp.float32
     )
 
 
-def back_part(grad, factor):
+def back_part(grad, factor, first):
     tokens, width = grad.shape
     rank = factor.shape[0]
     return pl.pallas_call(
         back_kernel,
-        in_specs=[vmem] * 2,
+        in_specs=[vmem] * 3,
         out_specs=vmem,
         out_shape=jax.ShapeDtypeStruct((tokens, rank), jnp.float32),
         cost_estimate=pl.CostEstimate(
@@ -179,7 +194,7 @@
         compiler_params=pltpu.CompilerParams(
             vmem_limit_bytes=limit(2 * (tokens + rank) * width)
         ),
-    )(grad, factor)
+    )(grad, factor, first)
 
 
 def tile_of(width):
@@ -195,7 +210,7 @@
 def low_rank_kernel(rounds, chained, acts, *refs):
     count = len(rounds)
     slices = refs[: 4 * count]
-    out, whole = refs[-2:]
+    out, sent, whole = refs[-3:]
     rows = slices[0].shape[0]
     width = 4 * rows
     tile = tile_of(width)
@@ -212,6 +227,7 @@
             )
             total = part if total is None else total + part
     out[...] = total
+    sent[...] = total.astype(sent.dtype)
 
 
 def low_rank_part(activations, rounds, slices, before=None):
@@ -223,9 +239,12 @@
     return pl.pallas_call(
         functools.partial(low_rank_kernel, rounds, before is not None),
         in_specs=[vmem] * (1 + len(slices) + len(extra)),
-        out_specs=vmem,
+        out_specs=[vmem] * 2,
         scratch_shapes=[pltpu.VMEM((count, width, rank), jnp.bfloat16)],
-        out_shape=jax.ShapeDtypeStruct((tokens, rank), jnp.float32),
+        out_shape=[
+            jax.ShapeDtypeStruct((tokens, rank), jnp.float32),
+            jax.ShapeDtypeStruct((tokens, rank), jnp.bfloat16),
+        ],
         cost_estimate=pl.CostEstimate(
             flops=2 * tokens * width * rank * count,
             bytes_accessed=2 * (tokens + rank) * width * count,
@@ -238,13 +257,14 @@
     )(activations, *slices, *extra)
 
 
-def grad_a_kernel(rounds, acts, coefficient, back, other, keep, send, whole):
-    rows = keep.shape[2]
+def grad_a_kernel(order, acts, coefficient, back, other, *refs):
+    outs, whole = refs[:-1], refs[-1]
+    rows = outs[0].shape[2]
     width = 4 * rows
     tile = tile_of(width)
     scaled = adapter_scale_factor * coefficient[...] * (back[...] + other[...])
     err = scaled.astype(jnp.bfloat16)
-    for index, r in enumerate(rounds):
+    for index, r in enumerate(order):
         for t in range(width // tile):
             part = lax.dot_general(
                 acts[:, columns(r, t, width, tile)],
@@ -252,23 +272,25 @@
                 (((0,), (0,)), ((), ())),
                 preferred_element_type=jnp.float32,
             )
-            whole[index, t * tile : (t + 1) * tile, :] = part.astype(jnp.bfloat16)
-        for dk, out in enumerate((keep, send)):
+            whole[index % 2, t * tile : (t + 1) * tile, :] = part.astype(jnp.bfloat16)
+        for dk in range(2):
             for dy in range(2):
-                out[index, dy] = whole[index, segment(dy, dk, rows)]
-
-
-def grad_a_part(activations, coefficient, back, other, rounds, rows):
+                outs[index // 2 * 2 + dk][index % 2, dy] = whole[
+                    index % 2, segment(dy, dk, rows)
+                ]
+
+
+def grad_a_part(activations, coefficient, back, other, order, rows):
     tokens, rank = back.shape
     width = 4 * rows
-    count = len(rounds)
-    shape = jax.ShapeDtypeStruct((count, 2, rows, rank), jnp.bfloat16)
-    return pl.pallas_call(
-        functools.partial(grad_a_kernel, rounds),
+    count = len(order)
+    shape = jax.ShapeDtypeStruct((2, 2, rows, rank), jnp.bfloat16)
+    return pl.pallas_call(
+        functools.partial(grad_a_kernel, order),
         in_specs=[vmem] * 4,
-        out_specs=[vmem] * 2,
-        scratch_shapes=[pltpu.VMEM((count, width, rank), jnp.bfloat16)],
-        out_shape=[shape, shape],
+        out_specs=[vmem] * count,
+        scratch_shapes=[pltpu.VMEM((2, width, rank), jnp.bfloat16)],
+        out_shape=[shape] * count,
         cost_estimate=pl.CostEstimate(
             flops=2 * tokens * width * rank * count,
             bytes_accessed=2 * (tokens + rank) * width * count,
@@ -286,7 +308,7 @@
     width = grad.shape[1]
     tile = tile_of(width)
     scale = adapter_scale_factor * stats[1][:1] * coefficient[...]
-    weighted = (scale * (low[...] + other[...])).astype(jnp.bfloat16)
+    weighted = (scale * (low[...] + other[...].astype(jnp.float32))).astype(jnp.bfloat16)
     shape = (rows, lanes)
     parts = thirds(
         jnp.broadcast_to(stats[0][:1], shape), lax.broadcasted_iota(jnp.int32, shape, 1)
@@ -360,6 +382,46 @@
     )(keep, got)
 
 
+def chunk_sum_kernel(own, got, stats, chunk, loss):
+    width = chunk.shape[1]
+    total = own[...] + got[...]
+    chunk[...] = total[:, :width].astype(chunk.dtype)
+    value = jnp.sum(total[:8, width:], axis=1, keepdims=True)
+    loss[...] = stats[1] * jnp.broadcast_to(value, loss.shape)
+
+
+def chunk_sum(own, got, stats):
+    rows, width = own.shape
+    return pl.pallas_call(
+        chunk_sum_kernel,
+        in_specs=[vmem] * 3,
+        out_specs=[vmem] * 2,
+        out_shape=[
+            jax.ShapeDtypeStruct((rows, width - lanes), jnp.bfloat16),
+            jax.ShapeDtypeStruct((8, lanes), jnp.float32),
+        ],
+        name="chunk_sum",
+        compiler_params=pltpu.CompilerParams(vmem_limit_bytes=limit(16 * rows * width)),
+    )(own, got, stats)
+
+
+def last_sum_kernel(own, near, far, stats, out):
+    total = (own[...] + near[...].astype(jnp.float32)) + far[...].astype(jnp.float32)
+    out[0] = stats[1][:1] * total
+
+
+def last_sum(own, near, far, stats):
+    rows, rank = own.shape
+    return pl.pallas_call(
+        last_sum_kernel,
+        in_specs=[vmem] * 4,
+        out_specs=vmem,
+        out_shape=jax.ShapeDtypeStruct((1, rows, rank), jnp.float32),
+        name="last_sum",
+        compiler_params=pltpu.CompilerParams(vmem_limit_bytes=limit(16 * rows * rank)),
+    )(own, near, far, stats)
+
+
 def fill_kernel(own, other, out):
     depth, rows = own.shape[:2]
     z, _, k = place()
@@ -399,6 +461,8 @@
 
     def other_tensor(value):
         return lax.ppermute(value, "tensor", [(0, 1), (1, 0)])
+
+    first = lead()
 
     bit = depth // 2
     have = {0: adapter_a[0]}
@@ -411,20 +475,18 @@
         over = to_y(have[r])
         slices.append([have[r], to_core(have[r]), over, to_core(over)])
 
-    back = back_part(output_gradient, adapter_b)
-    coefficient, stats = terms(log_ratio, lengths, rewards, activations)
+    back = back_part(output_gradient, adapter_b, first)
+    coefficient, stats = terms(log_ratio, lengths, rewards)
     other_back = other_tensor(back)
 
     order = [r for r in range(depth - 1, -1, -1)]
     sums = {}
+    pieces = grad_a_part(activations, coefficient, back, other_back, order, rows)
     for start in range(0, depth, 2):
-        group = order[start : start + 2]
-        keep, send = grad_a_part(
-            activations, coefficient, back, other_back, group, rows
-        )
+        keep, send = pieces[start : start + 2]
         got = to_core(send)
-        for index, r in enumerate(group):
-            sums[r] = f32(keep[index]) + f32(got[index])
+        for index in range(2):
+            sums[order[start + index]] = f32(keep[index]) + f32(got[index])
     got = to_y(half_width(jnp.stack([sums[1][1], sums[0][1]])))
     near = half_width(sums.pop(1)[0] + f32(got[0]))
     own = sums.pop(0)[0] + f32(got[1])
@@ -440,25 +502,23 @@
         sums[r] = sums[r][0] + f32(got)
     near = to_z(near, 1)
     last = to_z(half_width(sums[bit]), bit)
-    factor = stats[1, 0, 0]
-    grad_a = factor * ((own + f32(near)) + f32(last))
+    grad_a = last_sum(own, near, last, stats)
 
     cut = depth - 1
-    low = low_rank_part(activations, list(range(cut)), sum(slices[:cut], []))
-    low = low_rank_part(activations, list(range(cut, depth)), sum(slices[cut:], []), low)
-    other = other_tensor(low)
+    low, _ = low_rank_part(activations, list(range(cut)), sum(slices[:cut], []))
+    low, low_sent = low_rank_part(activations, list(range(cut, depth)), sum(slices[cut:], []), low)
+    other = other_tensor(low_sent)
     keep, send = grad_b_part(low, other, coefficient, stats, output_gradient, depth)
     got = to_core(send)
     pieces = chip_sum(keep, got)
     total = 0.0
     for r in range(depth):
         total = total + f32(across(pieces[r], r))
-    total = total + to_core(total)
-    loss = jnp.sum(total[0, -lanes:])
-    chunk = half_width(total[:, :-lanes])
+    got = to_core(total)
+    chunk, loss = chunk_sum(total, got, stats)
     own = jnp.stack([across(chunk, r) for r in range(depth)])
     grad_b = fill(own, to_core(own))
-    return (grad_a[None], grad_b, factor * loss)
+    return (grad_a, grad_b, loss[0, 0])
 
 
 def local(*args):

time: 98.9 us -> 99.2 us (level)
  starting transfers between devices: 30.3 us -> 38.2 us
  local copies, waits for them, and re-layouts: 7.75 us -> 2.11 us
  between operations: 3.34 us -> 0.86 us
  other arithmetic: 2.85 us -> 0.77 us
  Pallas kernels: 8.3 us -> 9.8 us
  waiting for transfers between devices: 46 us -> 47.3 us
    ppermute x33, starting transfers between devices: 27.3 us -> 33.8 us  [move(): return lax.ppermute(value, 'dp', pairs)]
    unnamed x18 -> x14, local copies, waits for them, and re-layouts: 7.14 us -> 1.46 us
    ppermute x33, waiting for transfers between devices: 42.2 us -> 44.3 us  [move(): return lax.ppermute(value, 'dp', pairs)]
    broadcast_in_dim x1 -> x0, other arithmetic: 1.54 us -> none  [placed(): return (grad_a[None], grad_b, factor * loss)]
    ppermute x2, starting transfers between devices: 3.03 us -> 4.37 us  [other_tensor(): return lax.ppermute(value, 'tensor', [(0, 1), (1, 0)])]
    pallas_call x3 -> x5, Pallas kernels: 3.38 us -> 4.21 us  [the longest x1 2.78 us: grad_a_part(): pl.pallas_call(functools.partial(grad_a_kernel, order), in_specs=[vmem] *...]
  transfers between devices with their start and end apart: 35 -> 35, of which waited for: 12 -> 15; matrix products, arithmetic and copies ran while one was open for 4% -> 1% of each run, Pallas kernels for 7% -> 8%
where the time goes in v1:
time: 99.2 us; the launch traced here: 99 us
  waiting for transfers between devices  47.3 us (48%)
  starting transfers between devices  38.2 us (39%)
  Pallas kernels  9.8 us (10%)
  local copies, waits for them, and re-layouts  2.11 us (2%)
    ppermute x33, waiting for transfers between devices, move(): return lax.ppermute(value, 'dp', pairs)  44.3 us
    ppermute x33, starting transfers between devices, move(): return lax.ppermute(value, 'dp', pairs)  33.8 us
    ppermute x2, starting transfers between devices, other_tensor(): return lax.ppermute(value, 'tensor', [(0, 1), (1, 0)])  4.37 us
    pallas_call x2, Pallas kernels, low_rank_part(): pl.pallas_call(functools.partial(low_rank_kernel, rounds, before is not N...  3.07 us
    ppermute x2, waiting for transfers between devices, other_tensor(): return lax.ppermute(value, 'tensor', [(0, 1), (1, 0)])  3 us
    pallas_call x1, Pallas kernels, grad_a_part(): pl.pallas_call(functools.partial(grad_a_kernel, order), in_specs=[vmem] *...  2.78 us
  transfers between devices with their start and end apart: 35, of which 15 were waited for; matrix products, arithmetic and copies ran while one was open for 1% of the time, Pallas kernels for 8%

profile of v1, /device:TPU:0, one launch (start us, length us, event | category | flops | bytes accessed | tf_op | source)
XLA Modules:
  0.0 99.0 jit_solution(11569279813358444112)
XLA Ops:
  0.7 1.3 %copy-done.1 = bf16[256,2560]{1,0:T(8,128)(2,1)S(1)} copy-done((bf16[256,2560]{1,0:T(8,128)(2,1)S(1)}, bf16[256,2560]{1,0:T(8,128)(2,1)}, u32[]{:S(2)}) %copy-start.1) | copy-done | bytes 1310744
  1.9 0.2 copy-done.2
  2.1 0.5 back.1
  2.6 3.0 %collective-permute-start = (f32[256,128]{1,0:T(8,128)S(1)}, f32[256,128]{1,0:T(8,128)S(1)}, u32[]{:S(2)}, u32[]{:S(2)}) collective-permute-start(f32[256,128]{1,0:T(8,128)S(1)} %back.1), channel_id=1, source_target_pairs={{0,1},{1,0},{2,3},{3,2},{4,5},{5,4},{6,7},{7,6},{8,9},{9,8},{10,11... | collective-permute-start | bytes 393224 | tf_op jit(solution)/shard_map/ppermute | solution.py:463
  5.7 2.6 %collective-permute-start.8 = (bf16[864,128]{1,0:T(8,128)(2,1)S(1)}, bf16[864,128]{1,0:T(8,128)(2,1)S(1)}, u32[]{:S(2)}, u32[]{:S(2)}) collective-permute-start(bf16[864,128]{1,0:T(8,128)(2,1)S(1)} %bitcast.41), channel_id=1, source_target_pairs={{0,16},{2,18},{4,20},{6,22},{8,24},{10,26},{12,28},{14,30},{16,0},... | collective-permute-start | bytes 663560 | tf_op jit(solution)/shard_map/ppermute | solution.py:455
  8.2 1.5 %collective-permute-start.14 = (bf16[864,128]{1,0:T(8,128)(2,1)S(1)}, bf16[864,128]{1,0:T(8,128)(2,1)S(1)}, u32[]{:S(2)}, u32[]{:S(2)}) collective-permute-start(bf16[864,128]{1,0:T(8,128)(2,1)S(1)} %bitcast.42), channel_id=1, source_target_pairs={{0,4},{2,6},{4,0},{6,2},{8,12},{10,14},{12,8},{14,10},{16,20},{18,... | collective-permute-start | bytes 663560 | tf_op jit(solution)/shard_map/ppermute | solution.py:455
  9.8 1.6 %collective-permute-start.16 = (bf16[864,128]{1,0:T(8,128)(2,1)S(1)}, bf16[864,128]{1,0:T(8,128)(2,1)S(1)}, u32[]{:S(2)}, u32[]{:S(2)}) collective-permute-start(bf16[864,128]{1,0:T(8,128)(2,1)S(1)} %bitcast.43), channel_id=1, source_target_pairs={{0,8},{2,10},{4,12},{6,14},{8,0},{10,2},{12,4},{14,6},{16,24},{18,... | collective-permute-start | bytes 663560 | tf_op jit(solution)/shard_map/ppermute | solution.py:455
  11.3 0.8 terms.1
  12.1 2.8 %grad_a.1 = (bf16[2,2,864,128]{3,2,1,0:T(8,128)(2,1)S(1)}, bf16[2,2,864,128]{3,2,1,0:T(8,128)(2,1)S(1)}, bf16[2,2,864,128]{3,2,1,0:T(8,128)(2,1)S(1)}, bf16[2,2,864,128]{3,2,1,0:T(8,128)(2,1)S(1)}) custom-call(bf16[256,13824]{1,0:T(8,128)(2,1)S(1)} %copy-done, f32[256,128]{1,0:T(8,128)S(1)} %get-tuple-element.20.coefficient, f32[256,128]{1,0:T(8,128)S(1)} %back.1, ...), custom_call_target="tpu_custom_call" | custom-call | flops 905969664 | bytes 10616832 | tf_op jit(solution)/shard_map/grad_a/pallas_call | solution.py:288
  14.9 0.1 collective-permute-start.1
  15.0 0.5 collective-permute-start.13
  15.5 2.8 %collective-permute-done.8.refs_8_ = bf16[864,128]{1,0:T(8,128)(2,1)S(1)} collective-permute-done((bf16[864,128]{1,0:T(8,128)(2,1)S(1)}, bf16[864,128]{1,0:T(8,128)(2,1)S(1)}, u32[]{:S(2)}, u32[]{:S(2)}) %collective-permute-start.8) | collective-permute-done | bytes 221216 | tf_op jit(solution)/shard_map/ppermute | solution.py:455
  18.3 0.6 collective-permute-start.9
  18.9 0.8 collective-permute-done.16.refs_4_
  19.7 1.2 %collective-permute-start.18 = (bf16[864,128]{1,0:T(8,128)(2,1)S(1)}, bf16[864,128]{1,0:T(8,128)(2,1)S(1)}, u32[]{:S(2)}, u32[]{:S(2)}) collective-permute-start(bf16[864,128]{1,0:T(8,128)(2,1)S(1)} %collective-permute-done.16.refs_4_), channel_id=1, source_target_pairs={{0,4},{2,6},{4,0},{6,2},{8,12},{10,14},{12,8},{14,10},{16,20},{18,... | collective-permute-start | bytes 663560 | tf_op jit(solution)/shard_map/ppermute | solution.py:455
  20.9 3.7 %collective-permute-done.9.refs_0_ = bf16[864,128]{1,0:T(8,128)(2,1)S(1)} collective-permute-done((bf16[864,128]{1,0:T(8,128)(2,1)S(1)}, bf16[864,128]{1,0:T(8,128)(2,1)S(1)}, u32[]{:S(2)}, u32[]{:S(2)}) %collective-permute-start.9) | collective-permute-done | bytes 221216 | tf_op jit(solution)/shard_map/ppermute | solution.py:455
  24.6 1.5 %collective-permute-start.21 = (bf16[864,128]{1,0:T(8,128)(2,1)S(1)}, bf16[864,128]{1,0:T(8,128)(2,1)S(1)}, u32[]{:S(2)}, u32[]{:S(2)}) collective-permute-start(bf16[864,128]{1,0:T(8,128)(2,1)S(1)} %collective-permute-done.8.refs_8_), channel_id=1, source_target_pairs={{0,4},{2,6},{4,0},{6,2},{8,12},{10,14},{12,8},{14,10},{16,20},{18,... | collective-permute-start | bytes 663560 | tf_op jit(solution)/shard_map/ppermute | solution.py:455
  26.1 0.0 collective-permute-done.15.refs_3_
  26.1 0.0 collective-permute-start.20
  26.1 0.6 collective-permute-start.11
  26.7 1.4 %collective-permute-done.18.refs_6_ = bf16[864,128]{1,0:T(8,128)(2,1)S(1)} collective-permute-done((bf16[864,128]{1,0:T(8,128)(2,1)S(1)}, bf16[864,128]{1,0:T(8,128)(2,1)S(1)}, u32[]{:S(2)}, u32[]{:S(2)}) %collective-permute-start.18) | collective-permute-done | bytes 221216 | tf_op jit(solution)/shard_map/ppermute | solution.py:455
  28.0 4.8 %collective-permute-done.21.refs_10_ = bf16[864,128]{1,0:T(8,128)(2,1)S(1)} collective-permute-done((bf16[864,128]{1,0:T(8,128)(2,1)S(1)}, bf16[864,128]{1,0:T(8,128)(2,1)S(1)}, u32[]{:S(2)}, u32[]{:S(2)}) %collective-permute-start.21) | collective-permute-done | bytes 221216 | tf_op jit(solution)/shard_map/ppermute | solution.py:455
  32.9 0.5 collective-permute-start.10
  33.4 3.7 %collective-permute-done.11.refs_2_ = bf16[864,128]{1,0:T(8,128)(2,1)S(1)} collective-permute-done((bf16[864,128]{1,0:T(8,128)(2,1)S(1)}, bf16[864,128]{1,0:T(8,128)(2,1)S(1)}, u32[]{:S(2)}, u32[]{:S(2)}) %collective-permute-start.11) | collective-permute-done | bytes 221216 | tf_op jit(solution)/shard_map/ppermute | solution.py:455
  37.1 0.5 collective-permute-start.4
  37.6 2.4 %low_rank.2 = (f32[256,128]{1,0:T(8,128)S(1)}, bf16[256,128]{1,0:T(8,128)(2,1)}) custom-call(bf16[256,13824]{1,0:T(8,128)(2,1)S(1)} %copy-done, bf16[864,128]{1,0:T(8,128)(2,1)S(1)} %bitcast.45, bf16[864,128]{1,0:T(8,128)(2,1)S(1)} %collective-permute-done.13.refs_1_, bf16[864,128]{1,0:T(8,128)(2,1)S(1)} %collective-permute-done.14.refs_2_, ...), custom_call_target="tpu_custom_call" | custom-call | flops 679477248 | bytes 7962624 | tf_op jit(solution)/shard_map/low_rank/pallas_call | solution.py:239
  39.9 0.7 low_rank.3
  40.6 1.3 %collective-permute-start.23 = (bf16[256,128]{1,0:T(8,128)(2,1)S(1)}, bf16[256,128]{1,0:T(8,128)(2,1)S(1)}, u32[]{:S(2)}, u32[]{:S(2)}) collective-permute-start(bf16[256,128]{1,0:T(8,128)(2,1)S(1)} %get-tuple-element.28), channel_id=1, source_target_pairs={{0,1},{1,0},{2,3},{3,2},{4,5},{5,4},{6,7},{7,6},{8,9},{9,8},{10,11... | collective-permute-start | bytes 196616 | tf_op jit(solution)/shard_map/ppermute | solution.py:463
  42.0 3.0 %collective-permute-done.23.other = bf16[256,128]{1,0:T(8,128)(2,1)S(1)} collective-permute-done((bf16[256,128]{1,0:T(8,128)(2,1)S(1)}, bf16[256,128]{1,0:T(8,128)(2,1)S(1)}, u32[]{:S(2)}, u32[]{:S(2)}) %collective-permute-start.23) | collective-permute-done | bytes 65568 | tf_op jit(solution)/shard_map/ppermute | solution.py:463
  45.0 0.5 grad_b.1
  45.5 0.1 collective-permute-start.24
  45.6 0.2 convert_add_fusion
  45.8 0.1 fusion.7
  45.9 0.8 collective-permute-start.2
  46.7 0.5 collective-permute-done.24.got
  47.2 0.1 chip_sum.1
  47.3 3.6 %collective-permute-start.28 = (bf16[16,2688]{1,0:T(8,128)(2,1)S(1)}, bf16[16,2688]{1,0:T(8,128)(2,1)S(1)}, u32[]{:S(2)}, u32[]{:S(2)}) collective-permute-start(bf16[16,2688]{1,0:T(8,128)(2,1)S(1)} %get-tuple-element.34), channel_id=1, source_target_pairs={{0,24},{2,28},{4,26},{6,30},{8,16},{10,20},{12,18},{14,22},{16,8},... | collective-permute-start | bytes 258056 | tf_op jit(solution)/shard_map/ppermute | solution.py:455
  50.9 0.9 collective-permute-start.26
  51.8 0.7 collective-permute-start.25
  52.4 0.1 fusion
  52.5 1.8 %collective-permute-done.28 = bf16[16,2688]{1,0:T(8,128)(2,1)S(1)} collective-permute-done((bf16[16,2688]{1,0:T(8,128)(2,1)S(1)}, bf16[16,2688]{1,0:T(8,128)(2,1)S(1)}, u32[]{:S(2)}, u32[]{:S(2)}) %collective-permute-start.28) | collective-permute-done | bytes 86048 | tf_op jit(solution)/shard_map/ppermute | solution.py:455
  54.3 3.6 %collective-permute-start.5 = (bf16[2,864,128]{2,1,0:T(8,128)(2,1)S(1)}, bf16[2,864,128]{2,1,0:T(8,128)(2,1)S(1)}, u32[]{:S(2)}, u32[]{:S(2)}) collective-permute-start(bf16[2,864,128]{2,1,0:T(8,128)(2,1)S(1)} %fusion), channel_id=1, source_target_pairs={{0,8},{2,10},{4,12},{6,14},{8,0},{10,2},{12,4},{14,6},{16,24},{18,... | collective-permute-start | bytes 1327112 | tf_op jit(solution)/shard_map/ppermute | solution.py:455
  57.9 0.9 collective-permute-done.27
  58.9 3.6 %collective-permute-start.29 = (f32[16,2688]{1,0:T(8,128)S(1)}, f32[16,2688]{1,0:T(8,128)S(1)}, u32[]{:S(2)}, u32[]{:S(2)}) collective-permute-start(f32[16,2688]{1,0:T(8,128)S(1)} %convert_add_fusion.2.own), channel_id=1, source_target_pairs={{0,2},{2,0},{4,6},{6,4},{8,10},{10,8},{12,14},{14,12},{16,18},{18,... | collective-permute-start | bytes 516104 | tf_op jit(solution)/shard_map/ppermute | solution.py:455
  62.5 0.1 fusion.9
  62.6 0.7 collective-permute-start.3
  63.3 5.6 %collective-permute-done.5 = bf16[2,864,128]{2,1,0:T(8,128)(2,1)S(1)} collective-permute-done((bf16[2,864,128]{2,1,0:T(8,128)(2,1)S(1)}, bf16[2,864,128]{2,1,0:T(8,128)(2,1)S(1)}, u32[]{:S(2)}, u32[]{:S(2)}) %collective-permute-start.5) | collective-permute-done | bytes 442400 | tf_op jit(solution)/shard_map/ppermute | solution.py:455
  68.9 0.2 bitcast_add_fusion
  69.1 0.1 chunk_sum.1
  69.2 2.7 %collective-permute-start.33 = (bf16[16,2560]{1,0:T(8,128)(2,1)S(1)}, bf16[16,2560]{1,0:T(8,128)(2,1)S(1)}, u32[]{:S(2)}, u32[]{:S(2)}) collective-permute-start(bf16[16,2560]{1,0:T(8,128)(2,1)S(1)} %get-tuple-element.35), channel_id=1, source_target_pairs={{0,24},{2,28},{4,26},{6,30},{8,16},{10,20},{12,18},{14,22},{16,8},... | collective-permute-start | bytes 245768 | tf_op jit(solution)/shard_map/ppermute | solution.py:455
  71.9 0.8 collective-permute-start.32
  72.7 0.9 collective-permute-start.31
  73.6 0.7 collective-permute-start.30
  74.3 4.1 %collective-permute-done.33 = bf16[16,2560]{1,0:T(8,128)(2,1)S(1)} collective-permute-done((bf16[16,2560]{1,0:T(8,128)(2,1)S(1)}, bf16[16,2560]{1,0:T(8,128)(2,1)S(1)}, u32[]{:S(2)}, u32[]{:S(2)}) %collective-permute-start.33) | collective-permute-done | bytes 81952 | tf_op jit(solution)/shard_map/ppermute | solution.py:455
  78.4 1.3 %collective-permute-start.6 = (bf16[864,128]{1,0:T(8,128)(2,1)S(1)}, bf16[864,128]{1,0:T(8,128)(2,1)S(1)}, u32[]{:S(2)}, u32[]{:S(2)}) collective-permute-start(bf16[864,128]{1,0:T(8,128)(2,1)S(1)} %fusion.10), channel_id=1, source_target_pairs={{0,4},{2,6},{4,0},{6,2},{8,12},{10,14},{12,8},{14,10},{16,20},{18,... | collective-permute-start | bytes 663560 | tf_op jit(solution)/shard_map/ppermute | solution.py:455
  79.7 1.7 %collective-permute-done.32 = bf16[16,2560]{1,0:T(8,128)(2,1)S(1)} collective-permute-done((bf16[16,2560]{1,0:T(8,128)(2,1)S(1)}, bf16[16,2560]{1,0:T(8,128)(2,1)S(1)}, u32[]{:S(2)}, u32[]{:S(2)}) %collective-permute-start.32) | collective-permute-done | bytes 81952 | tf_op jit(solution)/shard_map/ppermute | solution.py:455
  81.5 0.1 collective-permute-start.34
  81.6 3.5 %collective-permute-done.6 = bf16[864,128]{1,0:T(8,128)(2,1)S(1)} collective-permute-done((bf16[864,128]{1,0:T(8,128)(2,1)S(1)}, bf16[864,128]{1,0:T(8,128)(2,1)S(1)}, u32[]{:S(2)}, u32[]{:S(2)}) %collective-permute-start.6) | collective-permute-done | bytes 221216 | tf_op jit(solution)/shard_map/ppermute | solution.py:455
  85.0 0.1 fusion.2
  85.1 2.3 %collective-permute-start.7 = (bf16[864,128]{1,0:T(8,128)(2,1)S(1)}, bf16[864,128]{1,0:T(8,128)(2,1)S(1)}, u32[]{:S(2)}, u32[]{:S(2)}) collective-permute-start(bf16[864,128]{1,0:T(8,128)(2,1)S(1)} %fusion.2), channel_id=1, source_target_pairs={{0,16},{2,18},{4,20},{6,22},{8,24},{10,26},{12,28},{14,30},{16,0},... | collective-permute-start | bytes 663560 | tf_op jit(solution)/shard_map/ppermute | solution.py:455
  87.4 0.5 slice.86
  87.9 9.1 %collective-permute-done.7.far = bf16[864,128]{1,0:T(8,128)(2,1)S(1)} collective-permute-done((bf16[864,128]{1,0:T(8,128)(2,1)S(1)}, bf16[864,128]{1,0:T(8,128)(2,1)S(1)}, u32[]{:S(2)}, u32[]{:S(2)}) %collective-permute-start.7) | collective-permute-done | bytes 221216 | tf_op jit(solution)/shard_map/ppermute | solution.py:455
  97.0 0.9 last_sum.1
  97.8 1.2 %fill.1 = f32[128,2560]{1,0:T(8,128)} custom-call(bf16[4,16,2560]{2,1,0:T(8,128)(2,1)S(1)} %pad_maximum_fusion.1.own, bf16[4,16,2560]{2,1,0:T(8,128)(2,1)S(1)} %collective-permute-done.34.other), custom_call_target="tpu_custom_call" | custom-call | tf_op jit(solution)/shard_map/fill/pallas_call | solution.py:436
  (42 shorter events, 0.2 us)
Async XLA Ops:
  0.6 1.3 %copy-start.1 = (bf16[256,2560]{1,0:T(8,128)(2,1)S(1)}, bf16[256,2560]{1,0:T(8,128)(2,1)}, u32[]{:S(2)}) copy-start(bf16[256,2560]{1,0:T(8,128)(2,1)} %grad.3) | copy-start | bytes 3932164
  0.6 1.5 %copy-start.2 = (bf16[128,2560]{1,0:T(8,128)(2,1)S(1)}, bf16[128,2560]{1,0:T(8,128)(2,1)}, u32[]{:S(2)}) copy-start(bf16[128,2560]{1,0:T(8,128)(2,1)} %factor.1) | copy-start | bytes 1966084
  0.7 11.5 %copy-start = (bf16[256,13824]{1,0:T(8,128)(2,1)S(1)}, bf16[256,13824]{1,0:T(8,128)(2,1)}, u32[]{:S(2)}) copy-start(bf16[256,13824]{1,0:T(8,128)(2,1)} %acts.5) | copy-start | bytes 21233668
  2.1 3.5 %copy-start.3 = (bf16[1,864,128]{2,1,0:T(8,128)(2,1)S(1)}, bf16[1,864,128]{2,1,0:T(8,128)(2,1)}, u32[]{:S(2)}) copy-start(bf16[1,864,128]{2,1,0:T(8,128)(2,1)} %param.9) | copy-start | bytes 663556
  2.1 9.2 %copy-start.4 = (f32[256]{0:T(256)S(1)}, f32[256]{0:T(256)}, u32[]{:S(2)}) copy-start(f32[256]{0:T(256)} %param.11) | copy-start | bytes 3076
  2.1 9.2 %copy-start.5 = (s32[1,16]{1,0:T(1,128)S(1)}, s32[1,16]{1,0:T(1,128)}, u32[]{:S(2)}) copy-start(s32[1,16]{1,0:T(1,128)} %lengths.1) | copy-start | bytes 196
  2.1 9.2 %copy-start.6 = (s32[1,16]{1,0:T(1,128)S(1)}, s32[1,16]{1,0:T(1,128)}, u32[]{:S(2)}) copy-start(s32[1,16]{1,0:T(1,128)} %rewards.1) | copy-start | bytes 196
  2.6 9.5 %collective-permute-start = (f32[256,128]{1,0:T(8,128)S(1)}, f32[256,128]{1,0:T(8,128)S(1)}, u32[]{:S(2)}, u32[]{:S(2)}) collective-permute-start(f32[256,128]{1,0:T(8,128)S(1)} %back.1), channel_id=1, source_target_pairs={{0,1},{1,0},{2,3},{3,2},{4,5},{5,4},{6,7},{7,6},{8,9},{9,8},{10,11... | collective-permute-start | bytes 393224 | tf_op jit(solution)/shard_map/ppermute | solution.py:463
  5.7 12.6 %collective-permute-start.8 = (bf16[864,128]{1,0:T(8,128)(2,1)S(1)}, bf16[864,128]{1,0:T(8,128)(2,1)S(1)}, u32[]{:S(2)}, u32[]{:S(2)}) collective-permute-start(bf16[864,128]{1,0:T(8,128)(2,1)S(1)} %bitcast.41), channel_id=1, source_target_pairs={{0,16},{2,18},{4,20},{6,22},{8,24},{10,26},{12,28},{14,30},{16,0},... | collective-permute-start | bytes 663560 | tf_op jit(solution)/shard_map/ppermute | solution.py:455
  8.2 10.7 %collective-permute-start.14 = (bf16[864,128]{1,0:T(8,128)(2,1)S(1)}, bf16[864,128]{1,0:T(8,128)(2,1)S(1)}, u32[]{:S(2)}, u32[]{:S(2)}) collective-permute-start(bf16[864,128]{1,0:T(8,128)(2,1)S(1)} %bitcast.42), channel_id=1, source_target_pairs={{0,4},{2,6},{4,0},{6,2},{8,12},{10,14},{12,8},{14,10},{16,20},{18,... | collective-permute-start | bytes 663560 | tf_op jit(solution)/shard_map/ppermute | solution.py:455
  9.8 10.0 %collective-permute-start.16 = (bf16[864,128]{1,0:T(8,128)(2,1)S(1)}, bf16[864,128]{1,0:T(8,128)(2,1)S(1)}, u32[]{:S(2)}, u32[]{:S(2)}) collective-permute-start(bf16[864,128]{1,0:T(8,128)(2,1)S(1)} %bitcast.43), channel_id=1, source_target_pairs={{0,8},{2,10},{4,12},{6,14},{8,0},{10,2},{12,4},{14,6},{16,24},{18,... | collective-permute-start | bytes 663560 | tf_op jit(solution)/shard_map/ppermute | solution.py:455
  14.9 30.6 %collective-permute-start.1 = (bf16[2,2,864,128]{3,2,1,0:T(8,128)(2,1)S(1)}, bf16[2,2,864,128]{3,2,1,0:T(8,128)(2,1)S(1)}, u32[]{:S(2)}, u32[]{:S(2)}) collective-permute-start(bf16[2,2,864,128]{3,2,1,0:T(8,128)(2,1)S(1)} %get-tuple-element.22), channel_id=1, source_target_pairs={{0,2},{2,0},{4,6},{6,4},{8,10},{10,8},{12,14},{14,12},{16,18},{18,... | collective-permute-start | bytes 2654216 | tf_op jit(solution)/shard_map/ppermute | solution.py:455
  15.0 4.7 %collective-permute-start.13 = (bf16[864,128]{1,0:T(8,128)(2,1)S(1)}, bf16[864,128]{1,0:T(8,128)(2,1)S(1)}, u32[]{:S(2)}, u32[]{:S(2)}) collective-permute-start(bf16[864,128]{1,0:T(8,128)(2,1)S(1)} %bitcast.44), channel_id=1, source_target_pairs={{0,2},{2,0},{4,6},{6,4},{8,10},{10,8},{12,14},{14,12},{16,18},{18,... | collective-permute-start | bytes 663560 | tf_op jit(solution)/shard_map/ppermute | solution.py:455
  18.3 6.3 %collective-permute-start.9 = (bf16[864,128]{1,0:T(8,128)(2,1)S(1)}, bf16[864,128]{1,0:T(8,128)(2,1)S(1)}, u32[]{:S(2)}, u32[]{:S(2)}) collective-permute-start(bf16[864,128]{1,0:T(8,128)(2,1)S(1)} %collective-permute-done.8.refs_8_), channel_id=1, source_target_pairs={{0,8},{2,10},{4,12},{6,14},{8,0},{10,2},{12,4},{14,6},{16,24},{18,... | collective-permute-start | bytes 663560 | tf_op jit(solution)/shard_map/ppermute | solution.py:455
  18.9 7.2 %collective-permute-start.15 = (bf16[864,128]{1,0:T(8,128)(2,1)S(1)}, bf16[864,128]{1,0:T(8,128)(2,1)S(1)}, u32[]{:S(2)}, u32[]{:S(2)}) collective-permute-start(bf16[864,128]{1,0:T(8,128)(2,1)S(1)} %collective-permute-done.14.refs_2_), channel_id=1, source_target_pairs={{0,2},{2,0},{4,6},{6,4},{8,10},{10,8},{12,14},{14,12},{16,18},{18,... | collective-permute-start | bytes 663560 | tf_op jit(solution)/shard_map/ppermute | solution.py:455
  19.7 6.4 %collective-permute-start.17 = (bf16[864,128]{1,0:T(8,128)(2,1)S(1)}, bf16[864,128]{1,0:T(8,128)(2,1)S(1)}, u32[]{:S(2)}, u32[]{:S(2)}) collective-permute-start(bf16[864,128]{1,0:T(8,128)(2,1)S(1)} %collective-permute-done.16.refs_4_), channel_id=1, source_target_pairs={{0,2},{2,0},{4,6},{6,4},{8,10},{10,8},{12,14},{14,12},{16,18},{18,... | collective-permute-start | bytes 663560 | tf_op jit(solution)/shard_map/ppermute | solution.py:455
  19.7 8.3 %collective-permute-start.18 = (bf16[864,128]{1,0:T(8,128)(2,1)S(1)}, bf16[864,128]{1,0:T(8,128)(2,1)S(1)}, u32[]{:S(2)}, u32[]{:S(2)}) collective-permute-start(bf16[864,128]{1,0:T(8,128)(2,1)S(1)} %collective-permute-done.16.refs_4_), channel_id=1, source_target_pairs={{0,4},{2,6},{4,0},{6,2},{8,12},{10,14},{12,8},{14,10},{16,20},{18,... | collective-permute-start | bytes 663560 | tf_op jit(solution)/shard_map/ppermute | solution.py:455
  24.6 8.3 %collective-permute-start.21 = (bf16[864,128]{1,0:T(8,128)(2,1)S(1)}, bf16[864,128]{1,0:T(8,128)(2,1)S(1)}, u32[]{:S(2)}, u32[]{:S(2)}) collective-permute-start(bf16[864,128]{1,0:T(8,128)(2,1)S(1)} %collective-permute-done.8.refs_8_), channel_id=1, source_target_pairs={{0,4},{2,6},{4,0},{6,2},{8,12},{10,14},{12,8},{14,10},{16,20},{18,... | collective-permute-start | bytes 663560 | tf_op jit(solution)/shard_map/ppermute | solution.py:455
  26.1 6.8 %collective-permute-start.20 = (bf16[864,128]{1,0:T(8,128)(2,1)S(1)}, bf16[864,128]{1,0:T(8,128)(2,1)S(1)}, u32[]{:S(2)}, u32[]{:S(2)}) collective-permute-start(bf16[864,128]{1,0:T(8,128)(2,1)S(1)} %collective-permute-done.8.refs_8_), channel_id=1, source_target_pairs={{0,2},{2,0},{4,6},{6,4},{8,10},{10,8},{12,14},{14,12},{16,18},{18,... | collective-permute-start | bytes 663560 | tf_op jit(solution)/shard_map/ppermute | solution.py:455
  26.1 10.9 %collective-permute-start.11 = (bf16[864,128]{1,0:T(8,128)(2,1)S(1)}, bf16[864,128]{1,0:T(8,128)(2,1)S(1)}, u32[]{:S(2)}, u32[]{:S(2)}) collective-permute-start(bf16[864,128]{1,0:T(8,128)(2,1)S(1)} %collective-permute-done.9.refs_0_), channel_id=1, source_target_pairs={{0,4},{2,6},{4,0},{6,2},{8,12},{10,14},{12,8},{14,10},{16,20},{18,... | collective-permute-start | bytes 663560 | tf_op jit(solution)/shard_map/ppermute | solution.py:455
  28.0 9.0 %collective-permute-start.19 = (bf16[864,128]{1,0:T(8,128)(2,1)S(1)}, bf16[864,128]{1,0:T(8,128)(2,1)S(1)}, u32[]{:S(2)}, u32[]{:S(2)}) collective-permute-start(bf16[864,128]{1,0:T(8,128)(2,1)S(1)} %collective-permute-done.18.refs_6_), channel_id=1, source_target_pairs={{0,2},{2,0},{4,6},{6,4},{8,10},{10,8},{12,14},{14,12},{16,18},{18,... | collective-permute-start | bytes 663560 | tf_op jit(solution)/shard_map/ppermute | solution.py:455
  32.9 4.7 %collective-permute-start.22 = (bf16[864,128]{1,0:T(8,128)(2,1)S(1)}, bf16[864,128]{1,0:T(8,128)(2,1)S(1)}, u32[]{:S(2)}, u32[]{:S(2)}) collective-permute-start(bf16[864,128]{1,0:T(8,128)(2,1)S(1)} %collective-permute-done.21.refs_10_), channel_id=1, source_target_pairs={{0,2},{2,0},{4,6},{6,4},{8,10},{10,8},{12,14},{14,12},{16,18},{18,... | collective-permute-start | bytes 663560 | tf_op jit(solution)/shard_map/ppermute | solution.py:455
  32.9 7.1 %collective-permute-start.10 = (bf16[864,128]{1,0:T(8,128)(2,1)S(1)}, bf16[864,128]{1,0:T(8,128)(2,1)S(1)}, u32[]{:S(2)}, u32[]{:S(2)}) collective-permute-start(bf16[864,128]{1,0:T(8,128)(2,1)S(1)} %collective-permute-done.9.refs_0_), channel_id=1, source_target_pairs={{0,2},{2,0},{4,6},{6,4},{8,10},{10,8},{12,14},{14,12},{16,18},{18,... | collective-permute-start | bytes 663560 | tf_op jit(solution)/shard_map/ppermute | solution.py:455
  37.0 2.9 %collective-permute-start.12 = (bf16[864,128]{1,0:T(8,128)(2,1)S(1)}, bf16[864,128]{1,0:T(8,128)(2,1)S(1)}, u32[]{:S(2)}, u32[]{:S(2)}) collective-permute-start(bf16[864,128]{1,0:T(8,128)(2,1)S(1)} %collective-permute-done.11.refs_2_), channel_id=1, source_target_pairs={{0,2},{2,0},{4,6},{6,4},{8,10},{10,8},{12,14},{14,12},{16,18},{18,... | collective-permute-start | bytes 663560 | tf_op jit(solution)/shard_map/ppermute | solution.py:455
  37.1 14.7 %collective-permute-start.4 = (bf16[2,2,864,128]{3,2,1,0:T(8,128)(2,1)S(1)}, bf16[2,2,864,128]{3,2,1,0:T(8,128)(2,1)S(1)}, u32[]{:S(2)}, u32[]{:S(2)}) collective-permute-start(bf16[2,2,864,128]{3,2,1,0:T(8,128)(2,1)S(1)} %get-tuple-element.24), channel_id=1, source_target_pairs={{0,2},{2,0},{4,6},{6,4},{8,10},{10,8},{12,14},{14,12},{16,18},{18,... | collective-permute-start | bytes 2654216 | tf_op jit(solution)/shard_map/ppermute | solution.py:455
  40.6 4.3 %collective-permute-start.23 = (bf16[256,128]{1,0:T(8,128)(2,1)S(1)}, bf16[256,128]{1,0:T(8,128)(2,1)S(1)}, u32[]{:S(2)}, u32[]{:S(2)}) collective-permute-start(bf16[256,128]{1,0:T(8,128)(2,1)S(1)} %get-tuple-element.28), channel_id=1, source_target_pairs={{0,1},{1,0},{2,3},{3,2},{4,5},{5,4},{6,7},{7,6},{8,9},{9,8},{10,11... | collective-permute-start | bytes 196616 | tf_op jit(solution)/shard_map/ppermute | solution.py:463
  45.5 1.7 %collective-permute-start.24 = (bf16[4,16,2688]{2,1,0:T(8,128)(2,1)S(1)}, bf16[4,16,2688]{2,1,0:T(8,128)(2,1)S(1)}, u32[]{:S(2)}, u32[]{:S(2)}) collective-permute-start(bf16[4,16,2688]{2,1,0:T(8,128)(2,1)S(1)} %get-tuple-element.30), channel_id=1, source_target_pairs={{0,2},{2,0},{4,6},{6,4},{8,10},{10,8},{12,14},{14,12},{16,18},{18,... | collective-permute-start | bytes 1032200 | tf_op jit(solution)/shard_map/ppermute | solution.py:455
  45.9 16.5 %collective-permute-start.2 = (bf16[2,864,128]{2,1,0:T(8,128)(2,1)S(1)}, bf16[2,864,128]{2,1,0:T(8,128)(2,1)S(1)}, u32[]{:S(2)}, u32[]{:S(2)}) collective-permute-start(bf16[2,864,128]{2,1,0:T(8,128)(2,1)S(1)} %pad_maximum_fusion), channel_id=1, source_target_pairs={{0,4},{2,6},{4,0},{6,2},{8,12},{10,14},{12,8},{14,10},{16,20},{18,... | collective-permute-start | bytes 1327112 | tf_op jit(solution)/shard_map/ppermute | solution.py:455
  47.3 7.0 %collective-permute-start.28 = (bf16[16,2688]{1,0:T(8,128)(2,1)S(1)}, bf16[16,2688]{1,0:T(8,128)(2,1)S(1)}, u32[]{:S(2)}, u32[]{:S(2)}) collective-permute-start(bf16[16,2688]{1,0:T(8,128)(2,1)S(1)} %get-tuple-element.34), channel_id=1, source_target_pairs={{0,24},{2,28},{4,26},{6,30},{8,16},{10,20},{12,18},{14,22},{16,8},... | collective-permute-start | bytes 258056 | tf_op jit(solution)/shard_map/ppermute | solution.py:455
  50.9 7.9 %collective-permute-start.27 = (bf16[16,2688]{1,0:T(8,128)(2,1)S(1)}, bf16[16,2688]{1,0:T(8,128)(2,1)S(1)}, u32[]{:S(2)}, u32[]{:S(2)}) collective-permute-start(bf16[16,2688]{1,0:T(8,128)(2,1)S(1)} %get-tuple-element.33), channel_id=1, source_target_pairs={{0,16},{2,20},{4,18},{6,22},{8,24},{10,28},{12,26},{14,30},{16,0},... | collective-permute-start | bytes 258056 | tf_op jit(solution)/shard_map/ppermute | solution.py:455
  50.9 7.9 %collective-permute-start.26 = (bf16[16,2688]{1,0:T(8,128)(2,1)S(1)}, bf16[16,2688]{1,0:T(8,128)(2,1)S(1)}, u32[]{:S(2)}, u32[]{:S(2)}) collective-permute-start(bf16[16,2688]{1,0:T(8,128)(2,1)S(1)} %get-tuple-element.32), channel_id=1, source_target_pairs={{0,8},{2,12},{4,10},{6,14},{8,0},{10,4},{12,2},{14,6},{16,24},{18,... | collective-permute-start | bytes 258056 | tf_op jit(solution)/shard_map/ppermute | solution.py:455
  51.8 7.1 %collective-permute-start.25 = (bf16[16,2688]{1,0:T(8,128)(2,1)S(1)}, bf16[16,2688]{1,0:T(8,128)(2,1)S(1)}, u32[]{:S(2)}, u32[]{:S(2)}) collective-permute-start(bf16[16,2688]{1,0:T(8,128)(2,1)S(1)} %get-tuple-element.31), channel_id=1, source_target_pairs={{0,0},{2,4},{4,2},{6,6},{8,8},{10,12},{12,10},{14,14},{16,16},{18,... | collective-permute-start | bytes 258056 | tf_op jit(solution)/shard_map/ppermute | solution.py:455
  54.3 14.6 %collective-permute-start.5 = (bf16[2,864,128]{2,1,0:T(8,128)(2,1)S(1)}, bf16[2,864,128]{2,1,0:T(8,128)(2,1)S(1)}, u32[]{:S(2)}, u32[]{:S(2)}) collective-permute-start(bf16[2,864,128]{2,1,0:T(8,128)(2,1)S(1)} %fusion), channel_id=1, source_target_pairs={{0,8},{2,10},{4,12},{6,14},{8,0},{10,2},{12,4},{14,6},{16,24},{18,... | collective-permute-start | bytes 1327112 | tf_op jit(solution)/shard_map/ppermute | solution.py:455
  58.9 10.2 %collective-permute-start.29 = (f32[16,2688]{1,0:T(8,128)S(1)}, f32[16,2688]{1,0:T(8,128)S(1)}, u32[]{:S(2)}, u32[]{:S(2)}) collective-permute-start(f32[16,2688]{1,0:T(8,128)S(1)} %convert_add_fusion.2.own), channel_id=1, source_target_pairs={{0,2},{2,0},{4,6},{6,4},{8,10},{10,8},{12,14},{14,12},{16,18},{18,... | collective-permute-start | bytes 516104 | tf_op jit(solution)/shard_map/ppermute | solution.py:455
  62.6 25.4 %collective-permute-start.3 = (bf16[864,128]{1,0:T(8,128)(2,1)S(1)}, bf16[864,128]{1,0:T(8,128)(2,1)S(1)}, u32[]{:S(2)}, u32[]{:S(2)}) collective-permute-start(bf16[864,128]{1,0:T(8,128)(2,1)S(1)} %get-tuple-element.39), channel_id=1, source_target_pairs={{0,8},{2,10},{4,12},{6,14},{8,0},{10,2},{12,4},{14,6},{16,24},{18,... | collective-permute-start | bytes 663560 | tf_op jit(solution)/shard_map/ppermute | solution.py:455
  69.2 9.2 %collective-permute-start.33 = (bf16[16,2560]{1,0:T(8,128)(2,1)S(1)}, bf16[16,2560]{1,0:T(8,128)(2,1)S(1)}, u32[]{:S(2)}, u32[]{:S(2)}) collective-permute-start(bf16[16,2560]{1,0:T(8,128)(2,1)S(1)} %get-tuple-element.35), channel_id=1, source_target_pairs={{0,24},{2,28},{4,26},{6,30},{8,16},{10,20},{12,18},{14,22},{16,8},... | collective-permute-start | bytes 245768 | tf_op jit(solution)/shard_map/ppermute | solution.py:455
  71.9 9.6 %collective-permute-start.32 = (bf16[16,2560]{1,0:T(8,128)(2,1)S(1)}, bf16[16,2560]{1,0:T(8,128)(2,1)S(1)}, u32[]{:S(2)}, u32[]{:S(2)}) collective-permute-start(bf16[16,2560]{1,0:T(8,128)(2,1)S(1)} %get-tuple-element.35), channel_id=1, source_target_pairs={{0,16},{2,20},{4,18},{6,22},{8,24},{10,28},{12,26},{14,30},{16,0},... | collective-permute-start | bytes 245768 | tf_op jit(solution)/shard_map/ppermute | solution.py:455
  72.7 8.8 %collective-permute-start.31 = (bf16[16,2560]{1,0:T(8,128)(2,1)S(1)}, bf16[16,2560]{1,0:T(8,128)(2,1)S(1)}, u32[]{:S(2)}, u32[]{:S(2)}) collective-permute-start(bf16[16,2560]{1,0:T(8,128)(2,1)S(1)} %get-tuple-element.35), channel_id=1, source_target_pairs={{0,8},{2,12},{4,10},{6,14},{8,0},{10,4},{12,2},{14,6},{16,24},{18,... | collective-permute-start | bytes 245768 | tf_op jit(solution)/shard_map/ppermute | solution.py:455
  73.6 7.8 %collective-permute-start.30 = (bf16[16,2560]{1,0:T(8,128)(2,1)S(1)}, bf16[16,2560]{1,0:T(8,128)(2,1)S(1)}, u32[]{:S(2)}, u32[]{:S(2)}) collective-permute-start(bf16[16,2560]{1,0:T(8,128)(2,1)S(1)} %get-tuple-element.35), channel_id=1, source_target_pairs={{0,0},{2,4},{4,2},{6,6},{8,8},{10,12},{12,10},{14,14},{16,16},{18,... | collective-permute-start | bytes 245768 | tf_op jit(solution)/shard_map/ppermute | solution.py:455
  78.4 6.6 %collective-permute-start.6 = (bf16[864,128]{1,0:T(8,128)(2,1)S(1)}, bf16[864,128]{1,0:T(8,128)(2,1)S(1)}, u32[]{:S(2)}, u32[]{:S(2)}) collective-permute-start(bf16[864,128]{1,0:T(8,128)(2,1)S(1)} %fusion.10), channel_id=1, source_target_pairs={{0,4},{2,6},{4,0},{6,2},{8,12},{10,14},{12,8},{14,10},{16,20},{18,... | collective-permute-start | bytes 663560 | tf_op jit(solution)/shard_map/ppermute | solution.py:455
  81.5 16.4 %collective-permute-start.34 = (bf16[4,16,2560]{2,1,0:T(8,128)(2,1)S(1)}, bf16[4,16,2560]{2,1,0:T(8,128)(2,1)S(1)}, u32[]{:S(2)}, u32[]{:S(2)}) collective-permute-start(bf16[4,16,2560]{2,1,0:T(8,128)(2,1)S(1)} %pad_maximum_fusion.1.own), channel_id=1, source_target_pairs={{0,2},{2,0},{4,6},{6,4},{8,10},{10,8},{12,14},{14,12},{16,18},{18,... | collective-permute-start | bytes 983048 | tf_op jit(solution)/shard_map/ppermute | solution.py:455
  85.1 11.9 %collective-permute-start.7 = (bf16[864,128]{1,0:T(8,128)(2,1)S(1)}, bf16[864,128]{1,0:T(8,128)(2,1)S(1)}, u32[]{:S(2)}, u32[]{:S(2)}) collective-permute-start(bf16[864,128]{1,0:T(8,128)(2,1)S(1)} %fusion.2), channel_id=1, source_target_pairs={{0,16},{2,18},{4,20},{6,22},{8,24},{10,26},{12,28},{14,30},{16,0},... | collective-permute-start | bytes 663560 | tf_op jit(solution)/shard_map/ppermute | solution.py:455

commit v2 on v1

--- a/solution.py
+++ b/solution.py
@@ -210,7 +210,7 @@
 def low_rank_kernel(rounds, chained, acts, *refs):
     count = len(rounds)
     slices = refs[: 4 * count]
-    out, sent, whole = refs[-3:]
+    outs, whole = refs[4 * count + chained : -1], refs[-1]
     rows = slices[0].shape[0]
     width = 4 * rows
     tile = tile_of(width)
@@ -226,11 +226,11 @@
                 preferred_element_type=jnp.float32,
             )
             total = part if total is None else total + part
-    out[...] = total
-    sent[...] = total.astype(sent.dtype)
-
-
-def low_rank_part(activations, rounds, slices, before=None):
+    for out in outs:
+        out[...] = total.astype(out.dtype)
+
+
+def low_rank_part(activations, rounds, slices, kinds, before=None):
     tokens = activations.shape[0]
     rows, rank = slices[0].shape
     width = 4 * rows
@@ -239,12 +239,9 @@
     return pl.pallas_call(
         functools.partial(low_rank_kernel, rounds, before is not None),
         in_specs=[vmem] * (1 + len(slices) + len(extra)),
-        out_specs=[vmem] * 2,
+        out_specs=[vmem] * len(kinds),
         scratch_shapes=[pltpu.VMEM((count, width, rank), jnp.bfloat16)],
-        out_shape=[
-            jax.ShapeDtypeStruct((tokens, rank), jnp.float32),
-            jax.ShapeDtypeStruct((tokens, rank), jnp.bfloat16),
-        ],
+        out_shape=[jax.ShapeDtypeStruct((tokens, rank), kind) for kind in kinds],
         cost_estimate=pl.CostEstimate(
             flops=2 * tokens * width * rank * count,
             bytes_accessed=2 * (tokens + rank) * width * count,
@@ -505,8 +502,16 @@
     grad_a = last_sum(own, near, last, stats)
 
     cut = depth - 1
-    low, _ = low_rank_part(activations, list(range(cut)), sum(slices[:cut], []))
-    low, low_sent = low_rank_part(activations, list(range(cut, depth)), sum(slices[cut:], []), low)
+    (low,) = low_rank_part(
+        activations, list(range(cut)), sum(slices[:cut], []), [jnp.float32]
+    )
+    low, low_sent = low_rank_part(
+        activations,
+        list(range(cut, depth)),
+        sum(slices[cut:], []),
+        [jnp.float32, jnp.bfloat16],
+        low,
+    )
     other = other_tensor(low_sent)
     keep, send = grad_b_part(low, other, coefficient, stats, output_gradient, depth)
     got = to_core(send)

time: 99.2 us -> 98.6 us (level)
  no operation moved by 1% of the time
where the time goes in v2:
time: 98.6 us; the launch traced here: 98.4 us
  waiting for transfers between devices  47.5 us (48%)
  starting transfers between devices  38 us (39%)
  Pallas kernels  9.15 us (9%)
  local copies, waits for them, and re-layouts  2.06 us (2%)
    ppermute x33, waiting for transfers between devices, move(): return lax.ppermute(value, 'dp', pairs)  44.5 us
    ppermute x33, starting transfers between devices, move(): return lax.ppermute(value, 'dp', pairs)  33.6 us
    ppermute x2, starting transfers between devices, other_tensor(): return lax.ppermute(value, 'tensor', [(0, 1), (1, 0)])  4.38 us
    ppermute x2, waiting for transfers between devices, other_tensor(): return lax.ppermute(value, 'tensor', [(0, 1), (1, 0)])  2.99 us
    pallas_call x1, Pallas kernels, grad_a_part(): pl.pallas_call(functools.partial(grad_a_kernel, order), in_specs=[vmem] *...  2.78 us
    pallas_call x2, Pallas kernels, low_rank_part(): pl.pallas_call(functools.partial(low_rank_kernel, rounds, before is not N...  2.43 us
  transfers between devices with their start and end apart: 35, of which 15 were waited for; matrix products, arithmetic and copies ran while one was open for 1% of the time, Pallas kernels for 8%

profile of v2, /device:TPU:0, one launch (start us, length us, event | category | flops | bytes accessed | tf_op | source)
XLA Modules:
  0.0 98.4 jit_solution(11565786747358059524)
XLA Ops:
  0.7 1.3 %copy-done.1 = bf16[256,2560]{1,0:T(8,128)(2,1)S(1)} copy-done((bf16[256,2560]{1,0:T(8,128)(2,1)S(1)}, bf16[256,2560]{1,0:T(8,128)(2,1)}, u32[]{:S(2)}) %copy-start.1) | copy-done | bytes 1310744
  1.9 0.2 copy-done.2
  2.1 0.5 back.1
  2.6 3.0 %collective-permute-start = (f32[256,128]{1,0:T(8,128)S(1)}, f32[256,128]{1,0:T(8,128)S(1)}, u32[]{:S(2)}, u32[]{:S(2)}) collective-permute-start(f32[256,128]{1,0:T(8,128)S(1)} %back.1), channel_id=1, source_target_pairs={{0,1},{1,0},{2,3},{3,2},{4,5},{5,4},{6,7},{7,6},{8,9},{9,8},{10,11... | collective-permute-start | bytes 393224 | tf_op jit(solution)/shard_map/ppermute | solution.py:460
  5.7 2.6 %collective-permute-start.8 = (bf16[864,128]{1,0:T(8,128)(2,1)S(1)}, bf16[864,128]{1,0:T(8,128)(2,1)S(1)}, u32[]{:S(2)}, u32[]{:S(2)}) collective-permute-start(bf16[864,128]{1,0:T(8,128)(2,1)S(1)} %bitcast.41), channel_id=1, source_target_pairs={{0,16},{2,18},{4,20},{6,22},{8,24},{10,26},{12,28},{14,30},{16,0},... | collective-permute-start | bytes 663560 | tf_op jit(solution)/shard_map/ppermute | solution.py:452
  8.2 1.5 %collective-permute-start.14 = (bf16[864,128]{1,0:T(8,128)(2,1)S(1)}, bf16[864,128]{1,0:T(8,128)(2,1)S(1)}, u32[]{:S(2)}, u32[]{:S(2)}) collective-permute-start(bf16[864,128]{1,0:T(8,128)(2,1)S(1)} %bitcast.42), channel_id=1, source_target_pairs={{0,4},{2,6},{4,0},{6,2},{8,12},{10,14},{12,8},{14,10},{16,20},{18,... | collective-permute-start | bytes 663560 | tf_op jit(solution)/shard_map/ppermute | solution.py:452
  9.8 1.6 %collective-permute-start.16 = (bf16[864,128]{1,0:T(8,128)(2,1)S(1)}, bf16[864,128]{1,0:T(8,128)(2,1)S(1)}, u32[]{:S(2)}, u32[]{:S(2)}) collective-permute-start(bf16[864,128]{1,0:T(8,128)(2,1)S(1)} %bitcast.43), channel_id=1, source_target_pairs={{0,8},{2,10},{4,12},{6,14},{8,0},{10,2},{12,4},{14,6},{16,24},{18,... | collective-permute-start | bytes 663560 | tf_op jit(solution)/shard_map/ppermute | solution.py:452
  11.3 0.8 terms.1
  12.1 2.8 %grad_a.1 = (bf16[2,2,864,128]{3,2,1,0:T(8,128)(2,1)S(1)}, bf16[2,2,864,128]{3,2,1,0:T(8,128)(2,1)S(1)}, bf16[2,2,864,128]{3,2,1,0:T(8,128)(2,1)S(1)}, bf16[2,2,864,128]{3,2,1,0:T(8,128)(2,1)S(1)}) custom-call(bf16[256,13824]{1,0:T(8,128)(2,1)S(1)} %copy-done, f32[256,128]{1,0:T(8,128)S(1)} %get-tuple-element.19.coefficient, f32[256,128]{1,0:T(8,128)S(1)} %back.1, ...), custom_call_target="tpu_custom_call" | custom-call | flops 905969664 | bytes 10616832 | tf_op jit(solution)/shard_map/grad_a/pallas_call | solution.py:285
  14.9 0.1 collective-permute-start.1
  15.0 0.5 collective-permute-start.13
  15.5 2.8 %collective-permute-done.8.refs_8_ = bf16[864,128]{1,0:T(8,128)(2,1)S(1)} collective-permute-done((bf16[864,128]{1,0:T(8,128)(2,1)S(1)}, bf16[864,128]{1,0:T(8,128)(2,1)S(1)}, u32[]{:S(2)}, u32[]{:S(2)}) %collective-permute-start.8) | collective-permute-done | bytes 221216 | tf_op jit(solution)/shard_map/ppermute | solution.py:452
  18.3 0.6 collective-permute-start.9
  18.9 0.8 collective-permute-done.16.refs_4_
  19.7 1.2 %collective-permute-start.18 = (bf16[864,128]{1,0:T(8,128)(2,1)S(1)}, bf16[864,128]{1,0:T(8,128)(2,1)S(1)}, u32[]{:S(2)}, u32[]{:S(2)}) collective-permute-start(bf16[864,128]{1,0:T(8,128)(2,1)S(1)} %collective-permute-done.16.refs_4_), channel_id=1, source_target_pairs={{0,4},{2,6},{4,0},{6,2},{8,12},{10,14},{12,8},{14,10},{16,20},{18,... | collective-permute-start | bytes 663560 | tf_op jit(solution)/shard_map/ppermute | solution.py:452
  20.9 3.7 %collective-permute-done.9.refs_0_ = bf16[864,128]{1,0:T(8,128)(2,1)S(1)} collective-permute-done((bf16[864,128]{1,0:T(8,128)(2,1)S(1)}, bf16[864,128]{1,0:T(8,128)(2,1)S(1)}, u32[]{:S(2)}, u32[]{:S(2)}) %collective-permute-start.9) | collective-permute-done | bytes 221216 | tf_op jit(solution)/shard_map/ppermute | solution.py:452
  24.6 1.5 %collective-permute-start.21 = (bf16[864,128]{1,0:T(8,128)(2,1)S(1)}, bf16[864,128]{1,0:T(8,128)(2,1)S(1)}, u32[]{:S(2)}, u32[]{:S(2)}) collective-permute-start(bf16[864,128]{1,0:T(8,128)(2,1)S(1)} %collective-permute-done.8.refs_8_), channel_id=1, source_target_pairs={{0,4},{2,6},{4,0},{6,2},{8,12},{10,14},{12,8},{14,10},{16,20},{18,... | collective-permute-start | bytes 663560 | tf_op jit(solution)/shard_map/ppermute | solution.py:452
  26.1 0.0 collective-permute-done.15.refs_3_
  26.1 0.0 collective-permute-start.20
  26.1 0.6 collective-permute-start.11
  26.7 1.4 %collective-permute-done.18.refs_6_ = bf16[864,128]{1,0:T(8,128)(2,1)S(1)} collective-permute-done((bf16[864,128]{1,0:T(8,128)(2,1)S(1)}, bf16[864,128]{1,0:T(8,128)(2,1)S(1)}, u32[]{:S(2)}, u32[]{:S(2)}) %collective-permute-start.18) | collective-permute-done | bytes 221216 | tf_op jit(solution)/shard_map/ppermute | solution.py:452
  28.0 4.8 %collective-permute-done.21.refs_10_ = bf16[864,128]{1,0:T(8,128)(2,1)S(1)} collective-permute-done((bf16[864,128]{1,0:T(8,128)(2,1)S(1)}, bf16[864,128]{1,0:T(8,128)(2,1)S(1)}, u32[]{:S(2)}, u32[]{:S(2)}) %collective-permute-start.21) | collective-permute-done | bytes 221216 | tf_op jit(solution)/shard_map/ppermute | solution.py:452
  32.9 0.5 collective-permute-start.10
  33.4 3.7 %collective-permute-done.11.refs_2_ = bf16[864,128]{1,0:T(8,128)(2,1)S(1)} collective-permute-done((bf16[864,128]{1,0:T(8,128)(2,1)S(1)}, bf16[864,128]{1,0:T(8,128)(2,1)S(1)}, u32[]{:S(2)}, u32[]{:S(2)}) %collective-permute-start.11) | collective-permute-done | bytes 221216 | tf_op jit(solution)/shard_map/ppermute | solution.py:452
  37.1 0.5 collective-permute-start.4
  37.6 1.7 %low_rank.2.refs_4_ = f32[256,128]{1,0:T(8,128)S(1)} custom-call(bf16[256,13824]{1,0:T(8,128)(2,1)S(1)} %copy-done, bf16[864,128]{1,0:T(8,128)(2,1)S(1)} %bitcast.45, bf16[864,128]{1,0:T(8,128)(2,1)S(1)} %collective-permute-done.13.refs_1_, bf16[864,128]{1,0:T(8,128)(2,1)S(1)} %collective-permute-done.14.refs_2_, ...), custom_call_target="tpu_custom_call" | custom-call | flops 679477248 | bytes 7962624 | tf_op jit(solution)/shard_map/low_rank/pallas_call | solution.py:239
  39.3 0.7 low_rank.3
  40.0 1.3 %collective-permute-start.23 = (bf16[256,128]{1,0:T(8,128)(2,1)S(1)}, bf16[256,128]{1,0:T(8,128)(2,1)S(1)}, u32[]{:S(2)}, u32[]{:S(2)}) collective-permute-start(bf16[256,128]{1,0:T(8,128)(2,1)S(1)} %get-tuple-element.26), channel_id=1, source_target_pairs={{0,1},{1,0},{2,3},{3,2},{4,5},{5,4},{6,7},{7,6},{8,9},{9,8},{10,11... | collective-permute-start | bytes 196616 | tf_op jit(solution)/shard_map/ppermute | solution.py:460
  41.4 3.0 %collective-permute-done.23.other = bf16[256,128]{1,0:T(8,128)(2,1)S(1)} collective-permute-done((bf16[256,128]{1,0:T(8,128)(2,1)S(1)}, bf16[256,128]{1,0:T(8,128)(2,1)S(1)}, u32[]{:S(2)}, u32[]{:S(2)}) %collective-permute-start.23) | collective-permute-done | bytes 65568 | tf_op jit(solution)/shard_map/ppermute | solution.py:460
  44.4 0.5 grad_b.1
  44.9 0.1 collective-permute-start.24
  44.9 0.2 convert_add_fusion
  45.1 0.1 fusion.7
  45.2 0.8 collective-permute-start.2
  46.0 0.5 collective-permute-done.24.got
  46.6 0.1 chip_sum.1
  46.7 3.5 %collective-permute-start.28 = (bf16[16,2688]{1,0:T(8,128)(2,1)S(1)}, bf16[16,2688]{1,0:T(8,128)(2,1)S(1)}, u32[]{:S(2)}, u32[]{:S(2)}) collective-permute-start(bf16[16,2688]{1,0:T(8,128)(2,1)S(1)} %get-tuple-element.32), channel_id=1, source_target_pairs={{0,24},{2,28},{4,26},{6,30},{8,16},{10,20},{12,18},{14,22},{16,8},... | collective-permute-start | bytes 258056 | tf_op jit(solution)/shard_map/ppermute | solution.py:452
  50.2 0.9 collective-permute-start.26
  51.1 0.7 collective-permute-start.25
  51.8 0.1 fusion
  51.9 1.8 %collective-permute-done.28 = bf16[16,2688]{1,0:T(8,128)(2,1)S(1)} collective-permute-done((bf16[16,2688]{1,0:T(8,128)(2,1)S(1)}, bf16[16,2688]{1,0:T(8,128)(2,1)S(1)}, u32[]{:S(2)}, u32[]{:S(2)}) %collective-permute-start.28) | collective-permute-done | bytes 86048 | tf_op jit(solution)/shard_map/ppermute | solution.py:452
  53.7 3.5 %collective-permute-start.5 = (bf16[2,864,128]{2,1,0:T(8,128)(2,1)S(1)}, bf16[2,864,128]{2,1,0:T(8,128)(2,1)S(1)}, u32[]{:S(2)}, u32[]{:S(2)}) collective-permute-start(bf16[2,864,128]{2,1,0:T(8,128)(2,1)S(1)} %fusion), channel_id=1, source_target_pairs={{0,8},{2,10},{4,12},{6,14},{8,0},{10,2},{12,4},{14,6},{16,24},{18,... | collective-permute-start | bytes 1327112 | tf_op jit(solution)/shard_map/ppermute | solution.py:452
  57.2 0.9 collective-permute-done.27
  58.2 3.6 %collective-permute-start.29 = (f32[16,2688]{1,0:T(8,128)S(1)}, f32[16,2688]{1,0:T(8,128)S(1)}, u32[]{:S(2)}, u32[]{:S(2)}) collective-permute-start(f32[16,2688]{1,0:T(8,128)S(1)} %convert_add_fusion.2.own), channel_id=1, source_target_pairs={{0,2},{2,0},{4,6},{6,4},{8,10},{10,8},{12,14},{14,12},{16,18},{18,... | collective-permute-start | bytes 516104 | tf_op jit(solution)/shard_map/ppermute | solution.py:452
  61.8 0.1 fusion.9
  61.9 0.7 collective-permute-start.3
  62.6 5.6 %collective-permute-done.5 = bf16[2,864,128]{2,1,0:T(8,128)(2,1)S(1)} collective-permute-done((bf16[2,864,128]{2,1,0:T(8,128)(2,1)S(1)}, bf16[2,864,128]{2,1,0:T(8,128)(2,1)S(1)}, u32[]{:S(2)}, u32[]{:S(2)}) %collective-permute-start.5) | collective-permute-done | bytes 442400 | tf_op jit(solution)/shard_map/ppermute | solution.py:452
  68.2 0.2 bitcast_add_fusion
  68.4 0.1 chunk_sum.1
  68.5 2.6 %collective-permute-start.33 = (bf16[16,2560]{1,0:T(8,128)(2,1)S(1)}, bf16[16,2560]{1,0:T(8,128)(2,1)S(1)}, u32[]{:S(2)}, u32[]{:S(2)}) collective-permute-start(bf16[16,2560]{1,0:T(8,128)(2,1)S(1)} %get-tuple-element.33), channel_id=1, source_target_pairs={{0,24},{2,28},{4,26},{6,30},{8,16},{10,20},{12,18},{14,22},{16,8},... | collective-permute-start | bytes 245768 | tf_op jit(solution)/shard_map/ppermute | solution.py:452
  71.1 0.9 collective-permute-start.32
  72.0 0.9 collective-permute-start.31
  72.9 0.7 collective-permute-start.30
  73.6 4.1 %collective-permute-done.33 = bf16[16,2560]{1,0:T(8,128)(2,1)S(1)} collective-permute-done((bf16[16,2560]{1,0:T(8,128)(2,1)S(1)}, bf16[16,2560]{1,0:T(8,128)(2,1)S(1)}, u32[]{:S(2)}, u32[]{:S(2)}) %collective-permute-start.33) | collective-permute-done | bytes 81952 | tf_op jit(solution)/shard_map/ppermute | solution.py:452
  77.7 1.4 %collective-permute-start.6 = (bf16[864,128]{1,0:T(8,128)(2,1)S(1)}, bf16[864,128]{1,0:T(8,128)(2,1)S(1)}, u32[]{:S(2)}, u32[]{:S(2)}) collective-permute-start(bf16[864,128]{1,0:T(8,128)(2,1)S(1)} %fusion.10), channel_id=1, source_target_pairs={{0,4},{2,6},{4,0},{6,2},{8,12},{10,14},{12,8},{14,10},{16,20},{18,... | collective-permute-start | bytes 663560 | tf_op jit(solution)/shard_map/ppermute | solution.py:452
  79.1 1.5 %collective-permute-done.32 = bf16[16,2560]{1,0:T(8,128)(2,1)S(1)} collective-permute-done((bf16[16,2560]{1,0:T(8,128)(2,1)S(1)}, bf16[16,2560]{1,0:T(8,128)(2,1)S(1)}, u32[]{:S(2)}, u32[]{:S(2)}) %collective-permute-start.32) | collective-permute-done | bytes 81952 | tf_op jit(solution)/shard_map/ppermute | solution.py:452
  80.6 0.2 collective-permute-start.34
  80.8 3.8 %collective-permute-done.6 = bf16[864,128]{1,0:T(8,128)(2,1)S(1)} collective-permute-done((bf16[864,128]{1,0:T(8,128)(2,1)S(1)}, bf16[864,128]{1,0:T(8,128)(2,1)S(1)}, u32[]{:S(2)}, u32[]{:S(2)}) %collective-permute-start.6) | collective-permute-done | bytes 221216 | tf_op jit(solution)/shard_map/ppermute | solution.py:452
  84.6 0.1 fusion.2
  84.6 2.0 %collective-permute-start.7 = (bf16[864,128]{1,0:T(8,128)(2,1)S(1)}, bf16[864,128]{1,0:T(8,128)(2,1)S(1)}, u32[]{:S(2)}, u32[]{:S(2)}) collective-permute-start(bf16[864,128]{1,0:T(8,128)(2,1)S(1)} %fusion.2), channel_id=1, source_target_pairs={{0,16},{2,18},{4,20},{6,22},{8,24},{10,26},{12,28},{14,30},{16,0},... | collective-permute-start | bytes 663560 | tf_op jit(solution)/shard_map/ppermute | solution.py:452
  86.7 0.5 slice.86
  87.2 9.2 %collective-permute-done.7.far = bf16[864,128]{1,0:T(8,128)(2,1)S(1)} collective-permute-done((bf16[864,128]{1,0:T(8,128)(2,1)S(1)}, bf16[864,128]{1,0:T(8,128)(2,1)S(1)}, u32[]{:S(2)}, u32[]{:S(2)}) %collective-permute-start.7) | collective-permute-done | bytes 221216 | tf_op jit(solution)/shard_map/ppermute | solution.py:452
  96.4 0.9 last_sum.1
  97.2 1.2 %fill.1 = f32[128,2560]{1,0:T(8,128)} custom-call(bf16[4,16,2560]{2,1,0:T(8,128)(2,1)S(1)} %pad_maximum_fusion.1.own, bf16[4,16,2560]{2,1,0:T(8,128)(2,1)S(1)} %collective-permute-done.34.other), custom_call_target="tpu_custom_call" | custom-call | tf_op jit(solution)/shard_map/fill/pallas_call | solution.py:433
  (42 shorter events, 0.3 us)
Async XLA Ops:
  0.6 1.3 %copy-start.1 = (bf16[256,2560]{1,0:T(8,128)(2,1)S(1)}, bf16[256,2560]{1,0:T(8,128)(2,1)}, u32[]{:S(2)}) copy-start(bf16[256,2560]{1,0:T(8,128)(2,1)} %grad.3) | copy-start | bytes 3932164
  0.6 1.5 %copy-start.2 = (bf16[128,2560]{1,0:T(8,128)(2,1)S(1)}, bf16[128,2560]{1,0:T(8,128)(2,1)}, u32[]{:S(2)}) copy-start(bf16[128,2560]{1,0:T(8,128)(2,1)} %factor.1) | copy-start | bytes 1966084
  0.7 11.5 %copy-start = (bf16[256,13824]{1,0:T(8,128)(2,1)S(1)}, bf16[256,13824]{1,0:T(8,128)(2,1)}, u32[]{:S(2)}) copy-start(bf16[256,13824]{1,0:T(8,128)(2,1)} %acts.5) | copy-start | bytes 21233668
  2.1 3.5 %copy-start.3 = (bf16[1,864,128]{2,1,0:T(8,128)(2,1)S(1)}, bf16[1,864,128]{2,1,0:T(8,128)(2,1)}, u32[]{:S(2)}) copy-start(bf16[1,864,128]{2,1,0:T(8,128)(2,1)} %param.9) | copy-start | bytes 663556
  2.1 9.2 %copy-start.4 = (f32[256]{0:T(256)S(1)}, f32[256]{0:T(256)}, u32[]{:S(2)}) copy-start(f32[256]{0:T(256)} %param.11) | copy-start | bytes 3076
  2.1 9.2 %copy-start.5 = (s32[1,16]{1,0:T(1,128)S(1)}, s32[1,16]{1,0:T(1,128)}, u32[]{:S(2)}) copy-start(s32[1,16]{1,0:T(1,128)} %lengths.1) | copy-start | bytes 196
  2.1 9.2 %copy-start.6 = (s32[1,16]{1,0:T(1,128)S(1)}, s32[1,16]{1,0:T(1,128)}, u32[]{:S(2)}) copy-start(s32[1,16]{1,0:T(1,128)} %rewards.1) | copy-start | bytes 196
  2.6 9.5 %collective-permute-start = (f32[256,128]{1,0:T(8,128)S(1)}, f32[256,128]{1,0:T(8,128)S(1)}, u32[]{:S(2)}, u32[]{:S(2)}) collective-permute-start(f32[256,128]{1,0:T(8,128)S(1)} %back.1), channel_id=1, source_target_pairs={{0,1},{1,0},{2,3},{3,2},{4,5},{5,4},{6,7},{7,6},{8,9},{9,8},{10,11... | collective-permute-start | bytes 393224 | tf_op jit(solution)/shard_map/ppermute | solution.py:460
  5.7 12.6 %collective-permute-start.8 = (bf16[864,128]{1,0:T(8,128)(2,1)S(1)}, bf16[864,128]{1,0:T(8,128)(2,1)S(1)}, u32[]{:S(2)}, u32[]{:S(2)}) collective-permute-start(bf16[864,128]{1,0:T(8,128)(2,1)S(1)} %bitcast.41), channel_id=1, source_target_pairs={{0,16},{2,18},{4,20},{6,22},{8,24},{10,26},{12,28},{14,30},{16,0},... | collective-permute-start | bytes 663560 | tf_op jit(solution)/shard_map/ppermute | solution.py:452
  8.2 10.7 %collective-permute-start.14 = (bf16[864,128]{1,0:T(8,128)(2,1)S(1)}, bf16[864,128]{1,0:T(8,128)(2,1)S(1)}, u32[]{:S(2)}, u32[]{:S(2)}) collective-permute-start(bf16[864,128]{1,0:T(8,128)(2,1)S(1)} %bitcast.42), channel_id=1, source_target_pairs={{0,4},{2,6},{4,0},{6,2},{8,12},{10,14},{12,8},{14,10},{16,20},{18,... | collective-permute-start | bytes 663560 | tf_op jit(solution)/shard_map/ppermute | solution.py:452
  9.8 10.0 %collective-permute-start.16 = (bf16[864,128]{1,0:T(8,128)(2,1)S(1)}, bf16[864,128]{1,0:T(8,128)(2,1)S(1)}, u32[]{:S(2)}, u32[]{:S(2)}) collective-permute-start(bf16[864,128]{1,0:T(8,128)(2,1)S(1)} %bitcast.43), channel_id=1, source_target_pairs={{0,8},{2,10},{4,12},{6,14},{8,0},{10,2},{12,4},{14,6},{16,24},{18,... | collective-permute-start | bytes 663560 | tf_op jit(solution)/shard_map/ppermute | solution.py:452
  14.9 30.0 %collective-permute-start.1 = (bf16[2,2,864,128]{3,2,1,0:T(8,128)(2,1)S(1)}, bf16[2,2,864,128]{3,2,1,0:T(8,128)(2,1)S(1)}, u32[]{:S(2)}, u32[]{:S(2)}) collective-permute-start(bf16[2,2,864,128]{3,2,1,0:T(8,128)(2,1)S(1)} %get-tuple-element.21), channel_id=1, source_target_pairs={{0,2},{2,0},{4,6},{6,4},{8,10},{10,8},{12,14},{14,12},{16,18},{18,... | collective-permute-start | bytes 2654216 | tf_op jit(solution)/shard_map/ppermute | solution.py:452
  15.0 4.7 %collective-permute-start.13 = (bf16[864,128]{1,0:T(8,128)(2,1)S(1)}, bf16[864,128]{1,0:T(8,128)(2,1)S(1)}, u32[]{:S(2)}, u32[]{:S(2)}) collective-permute-start(bf16[864,128]{1,0:T(8,128)(2,1)S(1)} %bitcast.44), channel_id=1, source_target_pairs={{0,2},{2,0},{4,6},{6,4},{8,10},{10,8},{12,14},{14,12},{16,18},{18,... | collective-permute-start | bytes 663560 | tf_op jit(solution)/shard_map/ppermute | solution.py:452
  18.3 6.3 %collective-permute-start.9 = (bf16[864,128]{1,0:T(8,128)(2,1)S(1)}, bf16[864,128]{1,0:T(8,128)(2,1)S(1)}, u32[]{:S(2)}, u32[]{:S(2)}) collective-permute-start(bf16[864,128]{1,0:T(8,128)(2,1)S(1)} %collective-permute-done.8.refs_8_), channel_id=1, source_target_pairs={{0,8},{2,10},{4,12},{6,14},{8,0},{10,2},{12,4},{14,6},{16,24},{18,... | collective-permute-start | bytes 663560 | tf_op jit(solution)/shard_map/ppermute | solution.py:452
  18.9 7.2 %collective-permute-start.15 = (bf16[864,128]{1,0:T(8,128)(2,1)S(1)}, bf16[864,128]{1,0:T(8,128)(2,1)S(1)}, u32[]{:S(2)}, u32[]{:S(2)}) collective-permute-start(bf16[864,128]{1,0:T(8,128)(2,1)S(1)} %collective-permute-done.14.refs_2_), channel_id=1, source_target_pairs={{0,2},{2,0},{4,6},{6,4},{8,10},{10,8},{12,14},{14,12},{16,18},{18,... | collective-permute-start | bytes 663560 | tf_op jit(solution)/shard_map/ppermute | solution.py:452
  19.7 6.4 %collective-permute-start.17 = (bf16[864,128]{1,0:T(8,128)(2,1)S(1)}, bf16[864,128]{1,0:T(8,128)(2,1)S(1)}, u32[]{:S(2)}, u32[]{:S(2)}) collective-permute-start(bf16[864,128]{1,0:T(8,128)(2,1)S(1)} %collective-permute-done.16.refs_4_), channel_id=1, source_target_pairs={{0,2},{2,0},{4,6},{6,4},{8,10},{10,8},{12,14},{14,12},{16,18},{18,... | collective-permute-start | bytes 663560 | tf_op jit(solution)/shard_map/ppermute | solution.py:452
  19.7 8.3 %collective-permute-start.18 = (bf16[864,128]{1,0:T(8,128)(2,1)S(1)}, bf16[864,128]{1,0:T(8,128)(2,1)S(1)}, u32[]{:S(2)}, u32[]{:S(2)}) collective-permute-start(bf16[864,128]{1,0:T(8,128)(2,1)S(1)} %collective-permute-done.16.refs_4_), channel_id=1, source_target_pairs={{0,4},{2,6},{4,0},{6,2},{8,12},{10,14},{12,8},{14,10},{16,20},{18,... | collective-permute-start | bytes 663560 | tf_op jit(solution)/shard_map/ppermute | solution.py:452
  24.6 8.3 %collective-permute-start.21 = (bf16[864,128]{1,0:T(8,128)(2,1)S(1)}, bf16[864,128]{1,0:T(8,128)(2,1)S(1)}, u32[]{:S(2)}, u32[]{:S(2)}) collective-permute-start(bf16[864,128]{1,0:T(8,128)(2,1)S(1)} %collective-permute-done.8.refs_8_), channel_id=1, source_target_pairs={{0,4},{2,6},{4,0},{6,2},{8,12},{10,14},{12,8},{14,10},{16,20},{18,... | collective-permute-start | bytes 663560 | tf_op jit(solution)/shard_map/ppermute | solution.py:452
  26.1 6.8 %collective-permute-start.20 = (bf16[864,128]{1,0:T(8,128)(2,1)S(1)}, bf16[864,128]{1,0:T(8,128)(2,1)S(1)}, u32[]{:S(2)}, u32[]{:S(2)}) collective-permute-start(bf16[864,128]{1,0:T(8,128)(2,1)S(1)} %collective-permute-done.8.refs_8_), channel_id=1, source_target_pairs={{0,2},{2,0},{4,6},{6,4},{8,10},{10,8},{12,14},{14,12},{16,18},{18,... | collective-permute-start | bytes 663560 | tf_op jit(solution)/shard_map/ppermute | solution.py:452
  26.1 10.9 %collective-permute-start.11 = (bf16[864,128]{1,0:T(8,128)(2,1)S(1)}, bf16[864,128]{1,0:T(8,128)(2,1)S(1)}, u32[]{:S(2)}, u32[]{:S(2)}) collective-permute-start(bf16[864,128]{1,0:T(8,128)(2,1)S(1)} %collective-permute-done.9.refs_0_), channel_id=1, source_target_pairs={{0,4},{2,6},{4,0},{6,2},{8,12},{10,14},{12,8},{14,10},{16,20},{18,... | collective-permute-start | bytes 663560 | tf_op jit(solution)/shard_map/ppermute | solution.py:452
  28.0 9.0 %collective-permute-start.19 = (bf16[864,128]{1,0:T(8,128)(2,1)S(1)}, bf16[864,128]{1,0:T(8,128)(2,1)S(1)}, u32[]{:S(2)}, u32[]{:S(2)}) collective-permute-start(bf16[864,128]{1,0:T(8,128)(2,1)S(1)} %collective-permute-done.18.refs_6_), channel_id=1, source_target_pairs={{0,2},{2,0},{4,6},{6,4},{8,10},{10,8},{12,14},{14,12},{16,18},{18,... | collective-permute-start | bytes 663560 | tf_op jit(solution)/shard_map/ppermute | solution.py:452
  32.9 4.7 %collective-permute-start.22 = (bf16[864,128]{1,0:T(8,128)(2,1)S(1)}, bf16[864,128]{1,0:T(8,128)(2,1)S(1)}, u32[]{:S(2)}, u32[]{:S(2)}) collective-permute-start(bf16[864,128]{1,0:T(8,128)(2,1)S(1)} %collective-permute-done.21.refs_10_), channel_id=1, source_target_pairs={{0,2},{2,0},{4,6},{6,4},{8,10},{10,8},{12,14},{14,12},{16,18},{18,... | collective-permute-start | bytes 663560 | tf_op jit(solution)/shard_map/ppermute | solution.py:452
  32.9 6.4 %collective-permute-start.10 = (bf16[864,128]{1,0:T(8,128)(2,1)S(1)}, bf16[864,128]{1,0:T(8,128)(2,1)S(1)}, u32[]{:S(2)}, u32[]{:S(2)}) collective-permute-start(bf16[864,128]{1,0:T(8,128)(2,1)S(1)} %collective-permute-done.9.refs_0_), channel_id=1, source_target_pairs={{0,2},{2,0},{4,6},{6,4},{8,10},{10,8},{12,14},{14,12},{16,18},{18,... | collective-permute-start | bytes 663560 | tf_op jit(solution)/shard_map/ppermute | solution.py:452
  37.0 2.2 %collective-permute-start.12 = (bf16[864,128]{1,0:T(8,128)(2,1)S(1)}, bf16[864,128]{1,0:T(8,128)(2,1)S(1)}, u32[]{:S(2)}, u32[]{:S(2)}) collective-permute-start(bf16[864,128]{1,0:T(8,128)(2,1)S(1)} %collective-permute-done.11.refs_2_), channel_id=1, source_target_pairs={{0,2},{2,0},{4,6},{6,4},{8,10},{10,8},{12,14},{14,12},{16,18},{18,... | collective-permute-start | bytes 663560 | tf_op jit(solution)/shard_map/ppermute | solution.py:452
  37.1 14.1 %collective-permute-start.4 = (bf16[2,2,864,128]{3,2,1,0:T(8,128)(2,1)S(1)}, bf16[2,2,864,128]{3,2,1,0:T(8,128)(2,1)S(1)}, u32[]{:S(2)}, u32[]{:S(2)}) collective-permute-start(bf16[2,2,864,128]{3,2,1,0:T(8,128)(2,1)S(1)} %get-tuple-element.23), channel_id=1, source_target_pairs={{0,2},{2,0},{4,6},{6,4},{8,10},{10,8},{12,14},{14,12},{16,18},{18,... | collective-permute-start | bytes 2654216 | tf_op jit(solution)/shard_map/ppermute | solution.py:452
  40.0 4.3 %collective-permute-start.23 = (bf16[256,128]{1,0:T(8,128)(2,1)S(1)}, bf16[256,128]{1,0:T(8,128)(2,1)S(1)}, u32[]{:S(2)}, u32[]{:S(2)}) collective-permute-start(bf16[256,128]{1,0:T(8,128)(2,1)S(1)} %get-tuple-element.26), channel_id=1, source_target_pairs={{0,1},{1,0},{2,3},{3,2},{4,5},{5,4},{6,7},{7,6},{8,9},{9,8},{10,11... | collective-permute-start | bytes 196616 | tf_op jit(solution)/shard_map/ppermute | solution.py:460
  44.9 1.7 %collective-permute-start.24 = (bf16[4,16,2688]{2,1,0:T(8,128)(2,1)S(1)}, bf16[4,16,2688]{2,1,0:T(8,128)(2,1)S(1)}, u32[]{:S(2)}, u32[]{:S(2)}) collective-permute-start(bf16[4,16,2688]{2,1,0:T(8,128)(2,1)S(1)} %get-tuple-element.28), channel_id=1, source_target_pairs={{0,2},{2,0},{4,6},{6,4},{8,10},{10,8},{12,14},{14,12},{16,18},{18,... | collective-permute-start | bytes 1032200 | tf_op jit(solution)/shard_map/ppermute | solution.py:452
  45.2 16.5 %collective-permute-start.2 = (bf16[2,864,128]{2,1,0:T(8,128)(2,1)S(1)}, bf16[2,864,128]{2,1,0:T(8,128)(2,1)S(1)}, u32[]{:S(2)}, u32[]{:S(2)}) collective-permute-start(bf16[2,864,128]{2,1,0:T(8,128)(2,1)S(1)} %pad_maximum_fusion), channel_id=1, source_target_pairs={{0,4},{2,6},{4,0},{6,2},{8,12},{10,14},{12,8},{14,10},{16,20},{18,... | collective-permute-start | bytes 1327112 | tf_op jit(solution)/shard_map/ppermute | solution.py:452
  46.7 7.0 %collective-permute-start.28 = (bf16[16,2688]{1,0:T(8,128)(2,1)S(1)}, bf16[16,2688]{1,0:T(8,128)(2,1)S(1)}, u32[]{:S(2)}, u32[]{:S(2)}) collective-permute-start(bf16[16,2688]{1,0:T(8,128)(2,1)S(1)} %get-tuple-element.32), channel_id=1, source_target_pairs={{0,24},{2,28},{4,26},{6,30},{8,16},{10,20},{12,18},{14,22},{16,8},... | collective-permute-start | bytes 258056 | tf_op jit(solution)/shard_map/ppermute | solution.py:452
  50.2 8.0 %collective-permute-start.27 = (bf16[16,2688]{1,0:T(8,128)(2,1)S(1)}, bf16[16,2688]{1,0:T(8,128)(2,1)S(1)}, u32[]{:S(2)}, u32[]{:S(2)}) collective-permute-start(bf16[16,2688]{1,0:T(8,128)(2,1)S(1)} %get-tuple-element.31), channel_id=1, source_target_pairs={{0,16},{2,20},{4,18},{6,22},{8,24},{10,28},{12,26},{14,30},{16,0},... | collective-permute-start | bytes 258056 | tf_op jit(solution)/shard_map/ppermute | solution.py:452
  50.2 8.0 %collective-permute-start.26 = (bf16[16,2688]{1,0:T(8,128)(2,1)S(1)}, bf16[16,2688]{1,0:T(8,128)(2,1)S(1)}, u32[]{:S(2)}, u32[]{:S(2)}) collective-permute-start(bf16[16,2688]{1,0:T(8,128)(2,1)S(1)} %get-tuple-element.30), channel_id=1, source_target_pairs={{0,8},{2,12},{4,10},{6,14},{8,0},{10,4},{12,2},{14,6},{16,24},{18,... | collective-permute-start | bytes 258056 | tf_op jit(solution)/shard_map/ppermute | solution.py:452
  51.1 7.0 %collective-permute-start.25 = (bf16[16,2688]{1,0:T(8,128)(2,1)S(1)}, bf16[16,2688]{1,0:T(8,128)(2,1)S(1)}, u32[]{:S(2)}, u32[]{:S(2)}) collective-permute-start(bf16[16,2688]{1,0:T(8,128)(2,1)S(1)} %get-tuple-element.29), channel_id=1, source_target_pairs={{0,0},{2,4},{4,2},{6,6},{8,8},{10,12},{12,10},{14,14},{16,16},{18,... | collective-permute-start | bytes 258056 | tf_op jit(solution)/shard_map/ppermute | solution.py:452
  53.7 14.6 %collective-permute-start.5 = (bf16[2,864,128]{2,1,0:T(8,128)(2,1)S(1)}, bf16[2,864,128]{2,1,0:T(8,128)(2,1)S(1)}, u32[]{:S(2)}, u32[]{:S(2)}) collective-permute-start(bf16[2,864,128]{2,1,0:T(8,128)(2,1)S(1)} %fusion), channel_id=1, source_target_pairs={{0,8},{2,10},{4,12},{6,14},{8,0},{10,2},{12,4},{14,6},{16,24},{18,... | collective-permute-start | bytes 1327112 | tf_op jit(solution)/shard_map/ppermute | solution.py:452
  58.2 10.2 %collective-permute-start.29 = (f32[16,2688]{1,0:T(8,128)S(1)}, f32[16,2688]{1,0:T(8,128)S(1)}, u32[]{:S(2)}, u32[]{:S(2)}) collective-permute-start(f32[16,2688]{1,0:T(8,128)S(1)} %convert_add_fusion.2.own), channel_id=1, source_target_pairs={{0,2},{2,0},{4,6},{6,4},{8,10},{10,8},{12,14},{14,12},{16,18},{18,... | collective-permute-start | bytes 516104 | tf_op jit(solution)/shard_map/ppermute | solution.py:452
  61.9 25.3 %collective-permute-start.3 = (bf16[864,128]{1,0:T(8,128)(2,1)S(1)}, bf16[864,128]{1,0:T(8,128)(2,1)S(1)}, u32[]{:S(2)}, u32[]{:S(2)}) collective-permute-start(bf16[864,128]{1,0:T(8,128)(2,1)S(1)} %get-tuple-element.37), channel_id=1, source_target_pairs={{0,8},{2,10},{4,12},{6,14},{8,0},{10,2},{12,4},{14,6},{16,24},{18,... | collective-permute-start | bytes 663560 | tf_op jit(solution)/shard_map/ppermute | solution.py:452
  68.5 9.2 %collective-permute-start.33 = (bf16[16,2560]{1,0:T(8,128)(2,1)S(1)}, bf16[16,2560]{1,0:T(8,128)(2,1)S(1)}, u32[]{:S(2)}, u32[]{:S(2)}) collective-permute-start(bf16[16,2560]{1,0:T(8,128)(2,1)S(1)} %get-tuple-element.33), channel_id=1, source_target_pairs={{0,24},{2,28},{4,26},{6,30},{8,16},{10,20},{12,18},{14,22},{16,8},... | collective-permute-start | bytes 245768 | tf_op jit(solution)/shard_map/ppermute | solution.py:452
  71.1 9.5 %collective-permute-start.32 = (bf16[16,2560]{1,0:T(8,128)(2,1)S(1)}, bf16[16,2560]{1,0:T(8,128)(2,1)S(1)}, u32[]{:S(2)}, u32[]{:S(2)}) collective-permute-start(bf16[16,2560]{1,0:T(8,128)(2,1)S(1)} %get-tuple-element.33), channel_id=1, source_target_pairs={{0,16},{2,20},{4,18},{6,22},{8,24},{10,28},{12,26},{14,30},{16,0},... | collective-permute-start | bytes 245768 | tf_op jit(solution)/shard_map/ppermute | solution.py:452
  72.0 8.6 %collective-permute-start.31 = (bf16[16,2560]{1,0:T(8,128)(2,1)S(1)}, bf16[16,2560]{1,0:T(8,128)(2,1)S(1)}, u32[]{:S(2)}, u32[]{:S(2)}) collective-permute-start(bf16[16,2560]{1,0:T(8,128)(2,1)S(1)} %get-tuple-element.33), channel_id=1, source_target_pairs={{0,8},{2,12},{4,10},{6,14},{8,0},{10,4},{12,2},{14,6},{16,24},{18,... | collective-permute-start | bytes 245768 | tf_op jit(solution)/shard_map/ppermute | solution.py:452
  72.9 7.7 %collective-permute-start.30 = (bf16[16,2560]{1,0:T(8,128)(2,1)S(1)}, bf16[16,2560]{1,0:T(8,128)(2,1)S(1)}, u32[]{:S(2)}, u32[]{:S(2)}) collective-permute-start(bf16[16,2560]{1,0:T(8,128)(2,1)S(1)} %get-tuple-element.33), channel_id=1, source_target_pairs={{0,0},{2,4},{4,2},{6,6},{8,8},{10,12},{12,10},{14,14},{16,16},{18,... | collective-permute-start | bytes 245768 | tf_op jit(solution)/shard_map/ppermute | solution.py:452
  77.7 6.9 %collective-permute-start.6 = (bf16[864,128]{1,0:T(8,128)(2,1)S(1)}, bf16[864,128]{1,0:T(8,128)(2,1)S(1)}, u32[]{:S(2)}, u32[]{:S(2)}) collective-permute-start(bf16[864,128]{1,0:T(8,128)(2,1)S(1)} %fusion.10), channel_id=1, source_target_pairs={{0,4},{2,6},{4,0},{6,2},{8,12},{10,14},{12,8},{14,10},{16,20},{18,... | collective-permute-start | bytes 663560 | tf_op jit(solution)/shard_map/ppermute | solution.py:452
  80.6 16.6 %collective-permute-start.34 = (bf16[4,16,2560]{2,1,0:T(8,128)(2,1)S(1)}, bf16[4,16,2560]{2,1,0:T(8,128)(2,1)S(1)}, u32[]{:S(2)}, u32[]{:S(2)}) collective-permute-start(bf16[4,16,2560]{2,1,0:T(8,128)(2,1)S(1)} %pad_maximum_fusion.1.own), channel_id=1, source_target_pairs={{0,2},{2,0},{4,6},{6,4},{8,10},{10,8},{12,14},{14,12},{16,18},{18,... | collective-permute-start | bytes 983048 | tf_op jit(solution)/shard_map/ppermute | solution.py:452
  84.6 11.7 %collective-permute-start.7 = (bf16[864,128]{1,0:T(8,128)(2,1)S(1)}, bf16[864,128]{1,0:T(8,128)(2,1)S(1)}, u32[]{:S(2)}, u32[]{:S(2)}) collective-permute-start(bf16[864,128]{1,0:T(8,128)(2,1)S(1)} %fusion.2), channel_id=1, source_target_pairs={{0,16},{2,18},{4,20},{6,22},{8,24},{10,26},{12,28},{14,30},{16,0},... | collective-permute-start | bytes 663560 | tf_op jit(solution)/shard_map/ppermute | solution.py:452

commit v3 on v2

--- a/solution.py
+++ b/solution.py
@@ -419,23 +419,41 @@
     )(own, near, far, stats)
 
 
-def fill_kernel(own, other, out):
-    depth, rows = own.shape[:2]
+def fill_kernel(dk, *refs):
+    source, out, wide, sems = refs[0], *refs[-3:]
+    depth, rows = source.shape[:2]
     z, _, k = place()
-    for dk, source in enumerate((own, other)):
-        for r in range(depth):
-            at = (lax.bitwise_xor(z, r) * 2 + lax.bitwise_xor(k, dk)) * rows
-            out[pl.ds(pl.multiple_of(at, rows), rows), :] = source[r].astype(jnp.float32)
-
-
-def fill(own, other):
-    depth, rows, width = own.shape
-    return pl.pallas_call(
-        fill_kernel,
+    copies = []
+    for r in range(depth):
+        wide[r] = source[r].astype(jnp.float32)
+        at = (lax.bitwise_xor(z, r) * 2 + lax.bitwise_xor(k, dk)) * rows
+        copy = pltpu.make_async_copy(
+            wide.at[r], out.at[pl.ds(pl.multiple_of(at, rows), rows)], sems.at[r]
+        )
+        copy.start()
+        copies.append(copy)
+    for copy in copies:
+        copy.wait()
+
+
+def fill(dk, source, *before):
+    depth, rows, width = source.shape
+    anywhere = pl.BlockSpec(memory_space=pl.ANY)
+    return pl.pallas_call(
+        functools.partial(fill_kernel, dk),
+        in_specs=[vmem] + [anywhere] * len(before),
+        out_specs=anywhere,
         out_shape=jax.ShapeDtypeStruct((2 * depth * rows, width), jnp.float32),
+        scratch_shapes=[
+            pltpu.VMEM((depth, rows, width), jnp.float32),
+            pltpu.SemaphoreType.DMA((depth,)),
+        ],
+        input_output_aliases={1: 0} if before else {},
         name="fill",
-        compiler_params=pltpu.CompilerParams(vmem_limit_bytes=limit(6 * 2**20)),
-    )(own, other)
+        compiler_params=pltpu.CompilerParams(
+            vmem_limit_bytes=limit(8 * depth * rows * width)
+        ),
+    )(source, *before)
 
 
 def placed(activations, output_gradient, adapter_a, adapter_b, log_ratio, lengths, rewards):
@@ -522,7 +540,9 @@
     got = to_core(total)
     chunk, loss = chunk_sum(total, got, stats)
     own = jnp.stack([across(chunk, r) for r in range(depth)])
-    grad_b = fill(own, to_core(own))
+    other = to_core(own)
+    grad_b = fill(0, own)
+    grad_b = fill(1, other, grad_b)
     return (grad_a, grad_b, loss[0, 0])
 
 

time: 98.6 us -> 98.3 us (level)
  transfers between devices with their start and end apart: 35 -> 35, of which waited for: 15 -> 15; matrix products, arithmetic and copies ran while one was open for 1% -> 1% of each run, Pallas kernels for 8% -> 9%
where the time goes in v3:
time: 98.3 us; the launch traced here: 98.1 us
  waiting for transfers between devices  46.6 us (47%)
  starting transfers between devices  38 us (39%)
  Pallas kernels  9.75 us (10%)
  local copies, waits for them, and re-layouts  2.06 us (2%)
    ppermute x33, waiting for transfers between devices, move(): return lax.ppermute(value, 'dp', pairs)  43.6 us
    ppermute x33, starting transfers between devices, move(): return lax.ppermute(value, 'dp', pairs)  33.6 us
    ppermute x2, starting transfers between devices, other_tensor(): return lax.ppermute(value, 'tensor', [(0, 1), (1, 0)])  4.38 us
    ppermute x2, waiting for transfers between devices, other_tensor(): return lax.ppermute(value, 'tensor', [(0, 1), (1, 0)])  2.99 us
    pallas_call x1, Pallas kernels, grad_a_part(): pl.pallas_call(functools.partial(grad_a_kernel, order), in_specs=[vmem] *...  2.78 us
    pallas_call x2, Pallas kernels, low_rank_part(): pl.pallas_call(functools.partial(low_rank_kernel, rounds, before is not N...  2.43 us
  transfers between devices with their start and end apart: 35, of which 15 were waited for; matrix products, arithmetic and copies ran while one was open for 1% of the time, Pallas kernels for 9%

profile of v3, /device:TPU:0, one launch (start us, length us, event | category | flops | bytes accessed | tf_op | source)
XLA Modules:
  0.0 98.1 jit_solution(13439004224616495626)
XLA Ops:
  0.7 1.3 %copy-done.1 = bf16[256,2560]{1,0:T(8,128)(2,1)S(1)} copy-done((bf16[256,2560]{1,0:T(8,128)(2,1)S(1)}, bf16[256,2560]{1,0:T(8,128)(2,1)}, u32[]{:S(2)}) %copy-start.1) | copy-done | bytes 1310744
  1.9 0.2 copy-done.2
  2.1 0.5 back.1
  2.6 3.0 %collective-permute-start = (f32[256,128]{1,0:T(8,128)S(1)}, f32[256,128]{1,0:T(8,128)S(1)}, u32[]{:S(2)}, u32[]{:S(2)}) collective-permute-start(f32[256,128]{1,0:T(8,128)S(1)} %back.1), channel_id=1, source_target_pairs={{0,1},{1,0},{2,3},{3,2},{4,5},{5,4},{6,7},{7,6},{8,9},{9,8},{10,11... | collective-permute-start | bytes 393224 | tf_op jit(solution)/shard_map/ppermute | solution.py:478
  5.7 2.6 %collective-permute-start.8 = (bf16[864,128]{1,0:T(8,128)(2,1)S(1)}, bf16[864,128]{1,0:T(8,128)(2,1)S(1)}, u32[]{:S(2)}, u32[]{:S(2)}) collective-permute-start(bf16[864,128]{1,0:T(8,128)(2,1)S(1)} %bitcast.41), channel_id=1, source_target_pairs={{0,16},{2,18},{4,20},{6,22},{8,24},{10,26},{12,28},{14,30},{16,0},... | collective-permute-start | bytes 663560 | tf_op jit(solution)/shard_map/ppermute | solution.py:470
  8.2 1.5 %collective-permute-start.14 = (bf16[864,128]{1,0:T(8,128)(2,1)S(1)}, bf16[864,128]{1,0:T(8,128)(2,1)S(1)}, u32[]{:S(2)}, u32[]{:S(2)}) collective-permute-start(bf16[864,128]{1,0:T(8,128)(2,1)S(1)} %bitcast.42), channel_id=1, source_target_pairs={{0,4},{2,6},{4,0},{6,2},{8,12},{10,14},{12,8},{14,10},{16,20},{18,... | collective-permute-start | bytes 663560 | tf_op jit(solution)/shard_map/ppermute | solution.py:470
  9.8 1.6 %collective-permute-start.16 = (bf16[864,128]{1,0:T(8,128)(2,1)S(1)}, bf16[864,128]{1,0:T(8,128)(2,1)S(1)}, u32[]{:S(2)}, u32[]{:S(2)}) collective-permute-start(bf16[864,128]{1,0:T(8,128)(2,1)S(1)} %bitcast.43), channel_id=1, source_target_pairs={{0,8},{2,10},{4,12},{6,14},{8,0},{10,2},{12,4},{14,6},{16,24},{18,... | collective-permute-start | bytes 663560 | tf_op jit(solution)/shard_map/ppermute | solution.py:470
  11.3 0.8 terms.1
  12.1 2.8 %grad_a.1 = (bf16[2,2,864,128]{3,2,1,0:T(8,128)(2,1)S(1)}, bf16[2,2,864,128]{3,2,1,0:T(8,128)(2,1)S(1)}, bf16[2,2,864,128]{3,2,1,0:T(8,128)(2,1)S(1)}, bf16[2,2,864,128]{3,2,1,0:T(8,128)(2,1)S(1)}) custom-call(bf16[256,13824]{1,0:T(8,128)(2,1)S(1)} %copy-done, f32[256,128]{1,0:T(8,128)S(1)} %get-tuple-element.19.coefficient, f32[256,128]{1,0:T(8,128)S(1)} %back.1, ...), custom_call_target="tpu_custom_call" | custom-call | flops 905969664 | bytes 10616832 | tf_op jit(solution)/shard_map/grad_a/pallas_call | solution.py:285
  14.9 0.1 collective-permute-start.1
  15.0 0.5 collective-permute-start.13
  15.5 2.8 %collective-permute-done.8.refs_8_ = bf16[864,128]{1,0:T(8,128)(2,1)S(1)} collective-permute-done((bf16[864,128]{1,0:T(8,128)(2,1)S(1)}, bf16[864,128]{1,0:T(8,128)(2,1)S(1)}, u32[]{:S(2)}, u32[]{:S(2)}) %collective-permute-start.8) | collective-permute-done | bytes 221216 | tf_op jit(solution)/shard_map/ppermute | solution.py:470
  18.3 0.6 collective-permute-start.9
  18.9 0.8 collective-permute-done.16.refs_4_
  19.7 1.2 %collective-permute-start.18 = (bf16[864,128]{1,0:T(8,128)(2,1)S(1)}, bf16[864,128]{1,0:T(8,128)(2,1)S(1)}, u32[]{:S(2)}, u32[]{:S(2)}) collective-permute-start(bf16[864,128]{1,0:T(8,128)(2,1)S(1)} %collective-permute-done.16.refs_4_), channel_id=1, source_target_pairs={{0,4},{2,6},{4,0},{6,2},{8,12},{10,14},{12,8},{14,10},{16,20},{18,... | collective-permute-start | bytes 663560 | tf_op jit(solution)/shard_map/ppermute | solution.py:470
  20.9 3.7 %collective-permute-done.9.refs_0_ = bf16[864,128]{1,0:T(8,128)(2,1)S(1)} collective-permute-done((bf16[864,128]{1,0:T(8,128)(2,1)S(1)}, bf16[864,128]{1,0:T(8,128)(2,1)S(1)}, u32[]{:S(2)}, u32[]{:S(2)}) %collective-permute-start.9) | collective-permute-done | bytes 221216 | tf_op jit(solution)/shard_map/ppermute | solution.py:470
  24.6 1.5 %collective-permute-start.21 = (bf16[864,128]{1,0:T(8,128)(2,1)S(1)}, bf16[864,128]{1,0:T(8,128)(2,1)S(1)}, u32[]{:S(2)}, u32[]{:S(2)}) collective-permute-start(bf16[864,128]{1,0:T(8,128)(2,1)S(1)} %collective-permute-done.8.refs_8_), channel_id=1, source_target_pairs={{0,4},{2,6},{4,0},{6,2},{8,12},{10,14},{12,8},{14,10},{16,20},{18,... | collective-permute-start | bytes 663560 | tf_op jit(solution)/shard_map/ppermute | solution.py:470
  26.1 0.0 collective-permute-done.15.refs_3_
  26.1 0.6 collective-permute-start.11
  26.7 1.4 %collective-permute-done.18.refs_6_ = bf16[864,128]{1,0:T(8,128)(2,1)S(1)} collective-permute-done((bf16[864,128]{1,0:T(8,128)(2,1)S(1)}, bf16[864,128]{1,0:T(8,128)(2,1)S(1)}, u32[]{:S(2)}, u32[]{:S(2)}) %collective-permute-start.18) | collective-permute-done | bytes 221216 | tf_op jit(solution)/shard_map/ppermute | solution.py:470
  28.0 4.8 %collective-permute-done.21.refs_10_ = bf16[864,128]{1,0:T(8,128)(2,1)S(1)} collective-permute-done((bf16[864,128]{1,0:T(8,128)(2,1)S(1)}, bf16[864,128]{1,0:T(8,128)(2,1)S(1)}, u32[]{:S(2)}, u32[]{:S(2)}) %collective-permute-start.21) | collective-permute-done | bytes 221216 | tf_op jit(solution)/shard_map/ppermute | solution.py:470
  32.9 0.5 collective-permute-start.10
  33.4 3.7 %collective-permute-done.11.refs_2_ = bf16[864,128]{1,0:T(8,128)(2,1)S(1)} collective-permute-done((bf16[864,128]{1,0:T(8,128)(2,1)S(1)}, bf16[864,128]{1,0:T(8,128)(2,1)S(1)}, u32[]{:S(2)}, u32[]{:S(2)}) %collective-permute-start.11) | collective-permute-done | bytes 221216 | tf_op jit(solution)/shard_map/ppermute | solution.py:470
  37.1 0.5 collective-permute-start.4
  37.6 1.7 %low_rank.2.refs_4_ = f32[256,128]{1,0:T(8,128)S(1)} custom-call(bf16[256,13824]{1,0:T(8,128)(2,1)S(1)} %copy-done, bf16[864,128]{1,0:T(8,128)(2,1)S(1)} %bitcast.45, bf16[864,128]{1,0:T(8,128)(2,1)S(1)} %collective-permute-done.13.refs_1_, bf16[864,128]{1,0:T(8,128)(2,1)S(1)} %collective-permute-done.14.refs_2_, ...), custom_call_target="tpu_custom_call" | custom-call | flops 679477248 | bytes 7962624 | tf_op jit(solution)/shard_map/low_rank/pallas_call | solution.py:239
  39.3 0.7 low_rank.3
  40.0 1.3 %collective-permute-start.23 = (bf16[256,128]{1,0:T(8,128)(2,1)S(1)}, bf16[256,128]{1,0:T(8,128)(2,1)S(1)}, u32[]{:S(2)}, u32[]{:S(2)}) collective-permute-start(bf16[256,128]{1,0:T(8,128)(2,1)S(1)} %get-tuple-element.26), channel_id=1, source_target_pairs={{0,1},{1,0},{2,3},{3,2},{4,5},{5,4},{6,7},{7,6},{8,9},{9,8},{10,11... | collective-permute-start | bytes 196616 | tf_op jit(solution)/shard_map/ppermute | solution.py:478
  41.4 3.0 %collective-permute-done.23.other = bf16[256,128]{1,0:T(8,128)(2,1)S(1)} collective-permute-done((bf16[256,128]{1,0:T(8,128)(2,1)S(1)}, bf16[256,128]{1,0:T(8,128)(2,1)S(1)}, u32[]{:S(2)}, u32[]{:S(2)}) %collective-permute-start.23) | collective-permute-done | bytes 65568 | tf_op jit(solution)/shard_map/ppermute | solution.py:478
  44.4 0.5 grad_b.1
  44.9 0.1 collective-permute-start.24
  44.9 0.2 convert_add_fusion
  45.1 0.1 fusion.7
  45.2 0.8 collective-permute-start.2
  46.0 0.5 collective-permute-done.24.got
  46.6 0.1 chip_sum.1
  46.7 3.5 %collective-permute-start.28 = (bf16[16,2688]{1,0:T(8,128)(2,1)S(1)}, bf16[16,2688]{1,0:T(8,128)(2,1)S(1)}, u32[]{:S(2)}, u32[]{:S(2)}) collective-permute-start(bf16[16,2688]{1,0:T(8,128)(2,1)S(1)} %get-tuple-element.32), channel_id=1, source_target_pairs={{0,24},{2,28},{4,26},{6,30},{8,16},{10,20},{12,18},{14,22},{16,8},... | collective-permute-start | bytes 258056 | tf_op jit(solution)/shard_map/ppermute | solution.py:470
  50.2 0.9 collective-permute-start.26
  51.1 0.7 collective-permute-start.25
  51.8 0.1 fusion
  51.9 1.8 %collective-permute-done.28 = bf16[16,2688]{1,0:T(8,128)(2,1)S(1)} collective-permute-done((bf16[16,2688]{1,0:T(8,128)(2,1)S(1)}, bf16[16,2688]{1,0:T(8,128)(2,1)S(1)}, u32[]{:S(2)}, u32[]{:S(2)}) %collective-permute-start.28) | collective-permute-done | bytes 86048 | tf_op jit(solution)/shard_map/ppermute | solution.py:470
  53.7 3.5 %collective-permute-start.5 = (bf16[2,864,128]{2,1,0:T(8,128)(2,1)S(1)}, bf16[2,864,128]{2,1,0:T(8,128)(2,1)S(1)}, u32[]{:S(2)}, u32[]{:S(2)}) collective-permute-start(bf16[2,864,128]{2,1,0:T(8,128)(2,1)S(1)} %fusion), channel_id=1, source_target_pairs={{0,8},{2,10},{4,12},{6,14},{8,0},{10,2},{12,4},{14,6},{16,24},{18,... | collective-permute-start | bytes 1327112 | tf_op jit(solution)/shard_map/ppermute | solution.py:470
  57.2 0.9 collective-permute-done.27
  58.2 3.6 %collective-permute-start.29 = (f32[16,2688]{1,0:T(8,128)S(1)}, f32[16,2688]{1,0:T(8,128)S(1)}, u32[]{:S(2)}, u32[]{:S(2)}) collective-permute-start(f32[16,2688]{1,0:T(8,128)S(1)} %convert_add_fusion.2.own), channel_id=1, source_target_pairs={{0,2},{2,0},{4,6},{6,4},{8,10},{10,8},{12,14},{14,12},{16,18},{18,... | collective-permute-start | bytes 516104 | tf_op jit(solution)/shard_map/ppermute | solution.py:470
  61.8 0.1 fusion.9
  61.9 0.7 collective-permute-start.3
  62.6 5.6 %collective-permute-done.5 = bf16[2,864,128]{2,1,0:T(8,128)(2,1)S(1)} collective-permute-done((bf16[2,864,128]{2,1,0:T(8,128)(2,1)S(1)}, bf16[2,864,128]{2,1,0:T(8,128)(2,1)S(1)}, u32[]{:S(2)}, u32[]{:S(2)}) %collective-permute-start.5) | collective-permute-done | bytes 442400 | tf_op jit(solution)/shard_map/ppermute | solution.py:470
  68.2 0.2 bitcast_add_fusion
  68.4 0.1 chunk_sum.1
  68.5 2.6 %collective-permute-start.33 = (bf16[16,2560]{1,0:T(8,128)(2,1)S(1)}, bf16[16,2560]{1,0:T(8,128)(2,1)S(1)}, u32[]{:S(2)}, u32[]{:S(2)}) collective-permute-start(bf16[16,2560]{1,0:T(8,128)(2,1)S(1)} %get-tuple-element.33), channel_id=1, source_target_pairs={{0,24},{2,28},{4,26},{6,30},{8,16},{10,20},{12,18},{14,22},{16,8},... | collective-permute-start | bytes 245768 | tf_op jit(solution)/shard_map/ppermute | solution.py:470
  71.1 0.9 collective-permute-start.32
  72.0 0.9 collective-permute-start.31
  72.9 0.7 collective-permute-start.30
  73.6 4.1 %collective-permute-done.33 = bf16[16,2560]{1,0:T(8,128)(2,1)S(1)} collective-permute-done((bf16[16,2560]{1,0:T(8,128)(2,1)S(1)}, bf16[16,2560]{1,0:T(8,128)(2,1)S(1)}, u32[]{:S(2)}, u32[]{:S(2)}) %collective-permute-start.33) | collective-permute-done | bytes 81952 | tf_op jit(solution)/shard_map/ppermute | solution.py:470
  77.7 1.4 %collective-permute-start.6 = (bf16[864,128]{1,0:T(8,128)(2,1)S(1)}, bf16[864,128]{1,0:T(8,128)(2,1)S(1)}, u32[]{:S(2)}, u32[]{:S(2)}) collective-permute-start(bf16[864,128]{1,0:T(8,128)(2,1)S(1)} %fusion.10), channel_id=1, source_target_pairs={{0,4},{2,6},{4,0},{6,2},{8,12},{10,14},{12,8},{14,10},{16,20},{18,... | collective-permute-start | bytes 663560 | tf_op jit(solution)/shard_map/ppermute | solution.py:470
  79.1 1.5 %collective-permute-done.32 = bf16[16,2560]{1,0:T(8,128)(2,1)S(1)} collective-permute-done((bf16[16,2560]{1,0:T(8,128)(2,1)S(1)}, bf16[16,2560]{1,0:T(8,128)(2,1)S(1)}, u32[]{:S(2)}, u32[]{:S(2)}) %collective-permute-start.32) | collective-permute-done | bytes 81952 | tf_op jit(solution)/shard_map/ppermute | solution.py:470
  80.6 0.2 collective-permute-start.34
  80.8 3.8 %collective-permute-done.6 = bf16[864,128]{1,0:T(8,128)(2,1)S(1)} collective-permute-done((bf16[864,128]{1,0:T(8,128)(2,1)S(1)}, bf16[864,128]{1,0:T(8,128)(2,1)S(1)}, u32[]{:S(2)}, u32[]{:S(2)}) %collective-permute-start.6) | collective-permute-done | bytes 221216 | tf_op jit(solution)/shard_map/ppermute | solution.py:470
  84.6 0.1 fusion.2
  84.6 2.0 %collective-permute-start.7 = (bf16[864,128]{1,0:T(8,128)(2,1)S(1)}, bf16[864,128]{1,0:T(8,128)(2,1)S(1)}, u32[]{:S(2)}, u32[]{:S(2)}) collective-permute-start(bf16[864,128]{1,0:T(8,128)(2,1)S(1)} %fusion.2), channel_id=1, source_target_pairs={{0,16},{2,18},{4,20},{6,22},{8,24},{10,26},{12,28},{14,30},{16,0},... | collective-permute-start | bytes 663560 | tf_op jit(solution)/shard_map/ppermute | solution.py:470
  86.7 0.5 slice.86
  87.2 0.9 fill.2.refs_1_
  88.1 8.3 %collective-permute-done.7.far = bf16[864,128]{1,0:T(8,128)(2,1)S(1)} collective-permute-done((bf16[864,128]{1,0:T(8,128)(2,1)S(1)}, bf16[864,128]{1,0:T(8,128)(2,1)S(1)}, u32[]{:S(2)}, u32[]{:S(2)}) %collective-permute-start.7) | collective-permute-done | bytes 221216 | tf_op jit(solution)/shard_map/ppermute | solution.py:470
  96.4 0.9 last_sum.1
  97.2 0.9 fill.3
  (43 shorter events, 0.3 us)
Async XLA Ops:
  0.6 1.3 %copy-start.1 = (bf16[256,2560]{1,0:T(8,128)(2,1)S(1)}, bf16[256,2560]{1,0:T(8,128)(2,1)}, u32[]{:S(2)}) copy-start(bf16[256,2560]{1,0:T(8,128)(2,1)} %grad.3) | copy-start | bytes 3932164
  0.6 1.5 %copy-start.2 = (bf16[128,2560]{1,0:T(8,128)(2,1)S(1)}, bf16[128,2560]{1,0:T(8,128)(2,1)}, u32[]{:S(2)}) copy-start(bf16[128,2560]{1,0:T(8,128)(2,1)} %factor.1) | copy-start | bytes 1966084
  0.7 11.5 %copy-start = (bf16[256,13824]{1,0:T(8,128)(2,1)S(1)}, bf16[256,13824]{1,0:T(8,128)(2,1)}, u32[]{:S(2)}) copy-start(bf16[256,13824]{1,0:T(8,128)(2,1)} %acts.5) | copy-start | bytes 21233668
  2.1 3.5 %copy-start.3 = (bf16[1,864,128]{2,1,0:T(8,128)(2,1)S(1)}, bf16[1,864,128]{2,1,0:T(8,128)(2,1)}, u32[]{:S(2)}) copy-start(bf16[1,864,128]{2,1,0:T(8,128)(2,1)} %param.9) | copy-start | bytes 663556
  2.1 9.2 %copy-start.4 = (f32[256]{0:T(256)S(1)}, f32[256]{0:T(256)}, u32[]{:S(2)}) copy-start(f32[256]{0:T(256)} %param.11) | copy-start | bytes 3076
  2.1 9.2 %copy-start.5 = (s32[1,16]{1,0:T(1,128)S(1)}, s32[1,16]{1,0:T(1,128)}, u32[]{:S(2)}) copy-start(s32[1,16]{1,0:T(1,128)} %lengths.1) | copy-start | bytes 196
  2.1 9.2 %copy-start.6 = (s32[1,16]{1,0:T(1,128)S(1)}, s32[1,16]{1,0:T(1,128)}, u32[]{:S(2)}) copy-start(s32[1,16]{1,0:T(1,128)} %rewards.1) | copy-start | bytes 196
  2.6 9.5 %collective-permute-start = (f32[256,128]{1,0:T(8,128)S(1)}, f32[256,128]{1,0:T(8,128)S(1)}, u32[]{:S(2)}, u32[]{:S(2)}) collective-permute-start(f32[256,128]{1,0:T(8,128)S(1)} %back.1), channel_id=1, source_target_pairs={{0,1},{1,0},{2,3},{3,2},{4,5},{5,4},{6,7},{7,6},{8,9},{9,8},{10,11... | collective-permute-start | bytes 393224 | tf_op jit(solution)/shard_map/ppermute | solution.py:478
  5.7 12.6 %collective-permute-start.8 = (bf16[864,128]{1,0:T(8,128)(2,1)S(1)}, bf16[864,128]{1,0:T(8,128)(2,1)S(1)}, u32[]{:S(2)}, u32[]{:S(2)}) collective-permute-start(bf16[864,128]{1,0:T(8,128)(2,1)S(1)} %bitcast.41), channel_id=1, source_target_pairs={{0,16},{2,18},{4,20},{6,22},{8,24},{10,26},{12,28},{14,30},{16,0},... | collective-permute-start | bytes 663560 | tf_op jit(solution)/shard_map/ppermute | solution.py:470
  8.2 10.7 %collective-permute-start.14 = (bf16[864,128]{1,0:T(8,128)(2,1)S(1)}, bf16[864,128]{1,0:T(8,128)(2,1)S(1)}, u32[]{:S(2)}, u32[]{:S(2)}) collective-permute-start(bf16[864,128]{1,0:T(8,128)(2,1)S(1)} %bitcast.42), channel_id=1, source_target_pairs={{0,4},{2,6},{4,0},{6,2},{8,12},{10,14},{12,8},{14,10},{16,20},{18,... | collective-permute-start | bytes 663560 | tf_op jit(solution)/shard_map/ppermute | solution.py:470
  9.8 10.0 %collective-permute-start.16 = (bf16[864,128]{1,0:T(8,128)(2,1)S(1)}, bf16[864,128]{1,0:T(8,128)(2,1)S(1)}, u32[]{:S(2)}, u32[]{:S(2)}) collective-permute-start(bf16[864,128]{1,0:T(8,128)(2,1)S(1)} %bitcast.43), channel_id=1, source_target_pairs={{0,8},{2,10},{4,12},{6,14},{8,0},{10,2},{12,4},{14,6},{16,24},{18,... | collective-permute-start | bytes 663560 | tf_op jit(solution)/shard_map/ppermute | solution.py:470
  14.9 30.0 %collective-permute-start.1 = (bf16[2,2,864,128]{3,2,1,0:T(8,128)(2,1)S(1)}, bf16[2,2,864,128]{3,2,1,0:T(8,128)(2,1)S(1)}, u32[]{:S(2)}, u32[]{:S(2)}) collective-permute-start(bf16[2,2,864,128]{3,2,1,0:T(8,128)(2,1)S(1)} %get-tuple-element.21), channel_id=1, source_target_pairs={{0,2},{2,0},{4,6},{6,4},{8,10},{10,8},{12,14},{14,12},{16,18},{18,... | collective-permute-start | bytes 2654216 | tf_op jit(solution)/shard_map/ppermute | solution.py:470
  15.0 4.7 %collective-permute-start.13 = (bf16[864,128]{1,0:T(8,128)(2,1)S(1)}, bf16[864,128]{1,0:T(8,128)(2,1)S(1)}, u32[]{:S(2)}, u32[]{:S(2)}) collective-permute-start(bf16[864,128]{1,0:T(8,128)(2,1)S(1)} %bitcast.44), channel_id=1, source_target_pairs={{0,2},{2,0},{4,6},{6,4},{8,10},{10,8},{12,14},{14,12},{16,18},{18,... | collective-permute-start | bytes 663560 | tf_op jit(solution)/shard_map/ppermute | solution.py:470
  18.3 6.3 %collective-permute-start.9 = (bf16[864,128]{1,0:T(8,128)(2,1)S(1)}, bf16[864,128]{1,0:T(8,128)(2,1)S(1)}, u32[]{:S(2)}, u32[]{:S(2)}) collective-permute-start(bf16[864,128]{1,0:T(8,128)(2,1)S(1)} %collective-permute-done.8.refs_8_), channel_id=1, source_target_pairs={{0,8},{2,10},{4,12},{6,14},{8,0},{10,2},{12,4},{14,6},{16,24},{18,... | collective-permute-start | bytes 663560 | tf_op jit(solution)/shard_map/ppermute | solution.py:470
  18.9 7.2 %collective-permute-start.15 = (bf16[864,128]{1,0:T(8,128)(2,1)S(1)}, bf16[864,128]{1,0:T(8,128)(2,1)S(1)}, u32[]{:S(2)}, u32[]{:S(2)}) collective-permute-start(bf16[864,128]{1,0:T(8,128)(2,1)S(1)} %collective-permute-done.14.refs_2_), channel_id=1, source_target_pairs={{0,2},{2,0},{4,6},{6,4},{8,10},{10,8},{12,14},{14,12},{16,18},{18,... | collective-permute-start | bytes 663560 | tf_op jit(solution)/shard_map/ppermute | solution.py:470
  19.7 6.4 %collective-permute-start.17 = (bf16[864,128]{1,0:T(8,128)(2,1)S(1)}, bf16[864,128]{1,0:T(8,128)(2,1)S(1)}, u32[]{:S(2)}, u32[]{:S(2)}) collective-permute-start(bf16[864,128]{1,0:T(8,128)(2,1)S(1)} %collective-permute-done.16.refs_4_), channel_id=1, source_target_pairs={{0,2},{2,0},{4,6},{6,4},{8,10},{10,8},{12,14},{14,12},{16,18},{18,... | collective-permute-start | bytes 663560 | tf_op jit(solution)/shard_map/ppermute | solution.py:470
  19.7 8.3 %collective-permute-start.18 = (bf16[864,128]{1,0:T(8,128)(2,1)S(1)}, bf16[864,128]{1,0:T(8,128)(2,1)S(1)}, u32[]{:S(2)}, u32[]{:S(2)}) collective-permute-start(bf16[864,128]{1,0:T(8,128)(2,1)S(1)} %collective-permute-done.16.refs_4_), channel_id=1, source_target_pairs={{0,4},{2,6},{4,0},{6,2},{8,12},{10,14},{12,8},{14,10},{16,20},{18,... | collective-permute-start | bytes 663560 | tf_op jit(solution)/shard_map/ppermute | solution.py:470
  24.6 8.3 %collective-permute-start.21 = (bf16[864,128]{1,0:T(8,128)(2,1)S(1)}, bf16[864,128]{1,0:T(8,128)(2,1)S(1)}, u32[]{:S(2)}, u32[]{:S(2)}) collective-permute-start(bf16[864,128]{1,0:T(8,128)(2,1)S(1)} %collective-permute-done.8.refs_8_), channel_id=1, source_target_pairs={{0,4},{2,6},{4,0},{6,2},{8,12},{10,14},{12,8},{14,10},{16,20},{18,... | collective-permute-start | bytes 663560 | tf_op jit(solution)/shard_map/ppermute | solution.py:470
  26.1 6.8 %collective-permute-start.20 = (bf16[864,128]{1,0:T(8,128)(2,1)S(1)}, bf16[864,128]{1,0:T(8,128)(2,1)S(1)}, u32[]{:S(2)}, u32[]{:S(2)}) collective-permute-start(bf16[864,128]{1,0:T(8,128)(2,1)S(1)} %collective-permute-done.8.refs_8_), channel_id=1, source_target_pairs={{0,2},{2,0},{4,6},{6,4},{8,10},{10,8},{12,14},{14,12},{16,18},{18,... | collective-permute-start | bytes 663560 | tf_op jit(solution)/shard_map/ppermute | solution.py:470
  26.1 10.9 %collective-permute-start.11 = (bf16[864,128]{1,0:T(8,128)(2,1)S(1)}, bf16[864,128]{1,0:T(8,128)(2,1)S(1)}, u32[]{:S(2)}, u32[]{:S(2)}) collective-permute-start(bf16[864,128]{1,0:T(8,128)(2,1)S(1)} %collective-permute-done.9.refs_0_), channel_id=1, source_target_pairs={{0,4},{2,6},{4,0},{6,2},{8,12},{10,14},{12,8},{14,10},{16,20},{18,... | collective-permute-start | bytes 663560 | tf_op jit(solution)/shard_map/ppermute | solution.py:470
  28.0 9.0 %collective-permute-start.19 = (bf16[864,128]{1,0:T(8,128)(2,1)S(1)}, bf16[864,128]{1,0:T(8,128)(2,1)S(1)}, u32[]{:S(2)}, u32[]{:S(2)}) collective-permute-start(bf16[864,128]{1,0:T(8,128)(2,1)S(1)} %collective-permute-done.18.refs_6_), channel_id=1, source_target_pairs={{0,2},{2,0},{4,6},{6,4},{8,10},{10,8},{12,14},{14,12},{16,18},{18,... | collective-permute-start | bytes 663560 | tf_op jit(solution)/shard_map/ppermute | solution.py:470
  32.9 4.7 %collective-permute-start.22 = (bf16[864,128]{1,0:T(8,128)(2,1)S(1)}, bf16[864,128]{1,0:T(8,128)(2,1)S(1)}, u32[]{:S(2)}, u32[]{:S(2)}) collective-permute-start(bf16[864,128]{1,0:T(8,128)(2,1)S(1)} %collective-permute-done.21.refs_10_), channel_id=1, source_target_pairs={{0,2},{2,0},{4,6},{6,4},{8,10},{10,8},{12,14},{14,12},{16,18},{18,... | collective-permute-start | bytes 663560 | tf_op jit(solution)/shard_map/ppermute | solution.py:470
  32.9 6.4 %collective-permute-start.10 = (bf16[864,128]{1,0:T(8,128)(2,1)S(1)}, bf16[864,128]{1,0:T(8,128)(2,1)S(1)}, u32[]{:S(2)}, u32[]{:S(2)}) collective-permute-start(bf16[864,128]{1,0:T(8,128)(2,1)S(1)} %collective-permute-done.9.refs_0_), channel_id=1, source_target_pairs={{0,2},{2,0},{4,6},{6,4},{8,10},{10,8},{12,14},{14,12},{16,18},{18,... | collective-permute-start | bytes 663560 | tf_op jit(solution)/shard_map/ppermute | solution.py:470
  37.0 2.2 %collective-permute-start.12 = (bf16[864,128]{1,0:T(8,128)(2,1)S(1)}, bf16[864,128]{1,0:T(8,128)(2,1)S(1)}, u32[]{:S(2)}, u32[]{:S(2)}) collective-permute-start(bf16[864,128]{1,0:T(8,128)(2,1)S(1)} %collective-permute-done.11.refs_2_), channel_id=1, source_target_pairs={{0,2},{2,0},{4,6},{6,4},{8,10},{10,8},{12,14},{14,12},{16,18},{18,... | collective-permute-start | bytes 663560 | tf_op jit(solution)/shard_map/ppermute | solution.py:470
  37.1 14.1 %collective-permute-start.4 = (bf16[2,2,864,128]{3,2,1,0:T(8,128)(2,1)S(1)}, bf16[2,2,864,128]{3,2,1,0:T(8,128)(2,1)S(1)}, u32[]{:S(2)}, u32[]{:S(2)}) collective-permute-start(bf16[2,2,864,128]{3,2,1,0:T(8,128)(2,1)S(1)} %get-tuple-element.23), channel_id=1, source_target_pairs={{0,2},{2,0},{4,6},{6,4},{8,10},{10,8},{12,14},{14,12},{16,18},{18,... | collective-permute-start | bytes 2654216 | tf_op jit(solution)/shard_map/ppermute | solution.py:470
  40.0 4.3 %collective-permute-start.23 = (bf16[256,128]{1,0:T(8,128)(2,1)S(1)}, bf16[256,128]{1,0:T(8,128)(2,1)S(1)}, u32[]{:S(2)}, u32[]{:S(2)}) collective-permute-start(bf16[256,128]{1,0:T(8,128)(2,1)S(1)} %get-tuple-element.26), channel_id=1, source_target_pairs={{0,1},{1,0},{2,3},{3,2},{4,5},{5,4},{6,7},{7,6},{8,9},{9,8},{10,11... | collective-permute-start | bytes 196616 | tf_op jit(solution)/shard_map/ppermute | solution.py:478
  44.9 1.7 %collective-permute-start.24 = (bf16[4,16,2688]{2,1,0:T(8,128)(2,1)S(1)}, bf16[4,16,2688]{2,1,0:T(8,128)(2,1)S(1)}, u32[]{:S(2)}, u32[]{:S(2)}) collective-permute-start(bf16[4,16,2688]{2,1,0:T(8,128)(2,1)S(1)} %get-tuple-element.28), channel_id=1, source_target_pairs={{0,2},{2,0},{4,6},{6,4},{8,10},{10,8},{12,14},{14,12},{16,18},{18,... | collective-permute-start | bytes 1032200 | tf_op jit(solution)/shard_map/ppermute | solution.py:470
  45.2 16.5 %collective-permute-start.2 = (bf16[2,864,128]{2,1,0:T(8,128)(2,1)S(1)}, bf16[2,864,128]{2,1,0:T(8,128)(2,1)S(1)}, u32[]{:S(2)}, u32[]{:S(2)}) collective-permute-start(bf16[2,864,128]{2,1,0:T(8,128)(2,1)S(1)} %pad_maximum_fusion), channel_id=1, source_target_pairs={{0,4},{2,6},{4,0},{6,2},{8,12},{10,14},{12,8},{14,10},{16,20},{18,... | collective-permute-start | bytes 1327112 | tf_op jit(solution)/shard_map/ppermute | solution.py:470
  46.7 7.0 %collective-permute-start.28 = (bf16[16,2688]{1,0:T(8,128)(2,1)S(1)}, bf16[16,2688]{1,0:T(8,128)(2,1)S(1)}, u32[]{:S(2)}, u32[]{:S(2)}) collective-permute-start(bf16[16,2688]{1,0:T(8,128)(2,1)S(1)} %get-tuple-element.32), channel_id=1, source_target_pairs={{0,24},{2,28},{4,26},{6,30},{8,16},{10,20},{12,18},{14,22},{16,8},... | collective-permute-start | bytes 258056 | tf_op jit(solution)/shard_map/ppermute | solution.py:470
  50.2 8.0 %collective-permute-start.27 = (bf16[16,2688]{1,0:T(8,128)(2,1)S(1)}, bf16[16,2688]{1,0:T(8,128)(2,1)S(1)}, u32[]{:S(2)}, u32[]{:S(2)}) collective-permute-start(bf16[16,2688]{1,0:T(8,128)(2,1)S(1)} %get-tuple-element.31), channel_id=1, source_target_pairs={{0,16},{2,20},{4,18},{6,22},{8,24},{10,28},{12,26},{14,30},{16,0},... | collective-permute-start | bytes 258056 | tf_op jit(solution)/shard_map/ppermute | solution.py:470
  50.2 8.0 %collective-permute-start.26 = (bf16[16,2688]{1,0:T(8,128)(2,1)S(1)}, bf16[16,2688]{1,0:T(8,128)(2,1)S(1)}, u32[]{:S(2)}, u32[]{:S(2)}) collective-permute-start(bf16[16,2688]{1,0:T(8,128)(2,1)S(1)} %get-tuple-element.30), channel_id=1, source_target_pairs={{0,8},{2,12},{4,10},{6,14},{8,0},{10,4},{12,2},{14,6},{16,24},{18,... | collective-permute-start | bytes 258056 | tf_op jit(solution)/shard_map/ppermute | solution.py:470
  51.1 7.0 %collective-permute-start.25 = (bf16[16,2688]{1,0:T(8,128)(2,1)S(1)}, bf16[16,2688]{1,0:T(8,128)(2,1)S(1)}, u32[]{:S(2)}, u32[]{:S(2)}) collective-permute-start(bf16[16,2688]{1,0:T(8,128)(2,1)S(1)} %get-tuple-element.29), channel_id=1, source_target_pairs={{0,0},{2,4},{4,2},{6,6},{8,8},{10,12},{12,10},{14,14},{16,16},{18,... | collective-permute-start | bytes 258056 | tf_op jit(solution)/shard_map/ppermute | solution.py:470
  53.7 14.6 %collective-permute-start.5 = (bf16[2,864,128]{2,1,0:T(8,128)(2,1)S(1)}, bf16[2,864,128]{2,1,0:T(8,128)(2,1)S(1)}, u32[]{:S(2)}, u32[]{:S(2)}) collective-permute-start(bf16[2,864,128]{2,1,0:T(8,128)(2,1)S(1)} %fusion), channel_id=1, source_target_pairs={{0,8},{2,10},{4,12},{6,14},{8,0},{10,2},{12,4},{14,6},{16,24},{18,... | collective-permute-start | bytes 1327112 | tf_op jit(solution)/shard_map/ppermute | solution.py:470
  58.2 10.2 %collective-permute-start.29 = (f32[16,2688]{1,0:T(8,128)S(1)}, f32[16,2688]{1,0:T(8,128)S(1)}, u32[]{:S(2)}, u32[]{:S(2)}) collective-permute-start(f32[16,2688]{1,0:T(8,128)S(1)} %convert_add_fusion.2.own), channel_id=1, source_target_pairs={{0,2},{2,0},{4,6},{6,4},{8,10},{10,8},{12,14},{14,12},{16,18},{18,... | collective-permute-start | bytes 516104 | tf_op jit(solution)/shard_map/ppermute | solution.py:470
  61.9 26.2 %collective-permute-start.3 = (bf16[864,128]{1,0:T(8,128)(2,1)S(1)}, bf16[864,128]{1,0:T(8,128)(2,1)S(1)}, u32[]{:S(2)}, u32[]{:S(2)}) collective-permute-start(bf16[864,128]{1,0:T(8,128)(2,1)S(1)} %get-tuple-element.37), channel_id=1, source_target_pairs={{0,8},{2,10},{4,12},{6,14},{8,0},{10,2},{12,4},{14,6},{16,24},{18,... | collective-permute-start | bytes 663560 | tf_op jit(solution)/shard_map/ppermute | solution.py:470
  68.5 9.2 %collective-permute-start.33 = (bf16[16,2560]{1,0:T(8,128)(2,1)S(1)}, bf16[16,2560]{1,0:T(8,128)(2,1)S(1)}, u32[]{:S(2)}, u32[]{:S(2)}) collective-permute-start(bf16[16,2560]{1,0:T(8,128)(2,1)S(1)} %get-tuple-element.33), channel_id=1, source_target_pairs={{0,24},{2,28},{4,26},{6,30},{8,16},{10,20},{12,18},{14,22},{16,8},... | collective-permute-start | bytes 245768 | tf_op jit(solution)/shard_map/ppermute | solution.py:470
  71.1 9.5 %collective-permute-start.32 = (bf16[16,2560]{1,0:T(8,128)(2,1)S(1)}, bf16[16,2560]{1,0:T(8,128)(2,1)S(1)}, u32[]{:S(2)}, u32[]{:S(2)}) collective-permute-start(bf16[16,2560]{1,0:T(8,128)(2,1)S(1)} %get-tuple-element.33), channel_id=1, source_target_pairs={{0,16},{2,20},{4,18},{6,22},{8,24},{10,28},{12,26},{14,30},{16,0},... | collective-permute-start | bytes 245768 | tf_op jit(solution)/shard_map/ppermute | solution.py:470
  72.0 8.6 %collective-permute-start.31 = (bf16[16,2560]{1,0:T(8,128)(2,1)S(1)}, bf16[16,2560]{1,0:T(8,128)(2,1)S(1)}, u32[]{:S(2)}, u32[]{:S(2)}) collective-permute-start(bf16[16,2560]{1,0:T(8,128)(2,1)S(1)} %get-tuple-element.33), channel_id=1, source_target_pairs={{0,8},{2,12},{4,10},{6,14},{8,0},{10,4},{12,2},{14,6},{16,24},{18,... | collective-permute-start | bytes 245768 | tf_op jit(solution)/shard_map/ppermute | solution.py:470
  72.9 7.7 %collective-permute-start.30 = (bf16[16,2560]{1,0:T(8,128)(2,1)S(1)}, bf16[16,2560]{1,0:T(8,128)(2,1)S(1)}, u32[]{:S(2)}, u32[]{:S(2)}) collective-permute-start(bf16[16,2560]{1,0:T(8,128)(2,1)S(1)} %get-tuple-element.33), channel_id=1, source_target_pairs={{0,0},{2,4},{4,2},{6,6},{8,8},{10,12},{12,10},{14,14},{16,16},{18,... | collective-permute-start | bytes 245768 | tf_op jit(solution)/shard_map/ppermute | solution.py:470
  77.7 6.9 %collective-permute-start.6 = (bf16[864,128]{1,0:T(8,128)(2,1)S(1)}, bf16[864,128]{1,0:T(8,128)(2,1)S(1)}, u32[]{:S(2)}, u32[]{:S(2)}) collective-permute-start(bf16[864,128]{1,0:T(8,128)(2,1)S(1)} %fusion.10), channel_id=1, source_target_pairs={{0,4},{2,6},{4,0},{6,2},{8,12},{10,14},{12,8},{14,10},{16,20},{18,... | collective-permute-start | bytes 663560 | tf_op jit(solution)/shard_map/ppermute | solution.py:470
  80.6 16.6 %collective-permute-start.34 = (bf16[4,16,2560]{2,1,0:T(8,128)(2,1)S(1)}, bf16[4,16,2560]{2,1,0:T(8,128)(2,1)S(1)}, u32[]{:S(2)}, u32[]{:S(2)}) collective-permute-start(bf16[4,16,2560]{2,1,0:T(8,128)(2,1)S(1)} %pad_maximum_fusion.1.refs_0_), channel_id=1, source_target_pairs={{0,2},{2,0},{4,6},{6,4},{8,10},{10,8},{12,14},{14,12},{16,18},{18,... | collective-permute-start | bytes 983048 | tf_op jit(solution)/shard_map/ppermute | solution.py:470
  84.6 11.7 %collective-permute-start.7 = (bf16[864,128]{1,0:T(8,128)(2,1)S(1)}, bf16[864,128]{1,0:T(8,128)(2,1)S(1)}, u32[]{:S(2)}, u32[]{:S(2)}) collective-permute-start(bf16[864,128]{1,0:T(8,128)(2,1)S(1)} %fusion.2), channel_id=1, source_target_pairs={{0,16},{2,18},{4,20},{6,22},{8,24},{10,26},{12,28},{14,30},{16,0},... | collective-permute-start | bytes 663560 | tf_op jit(solution)/shard_map/ppermute | solution.py:470
